TPU v7x, 32 devices: a whole 2x2x4 slice. The times are simulated.
32 devices in a mesh: gx: 8 (over z, x), gy: 4 (over y, core).
Axes of the slice: x: 2, y: 2, z: 4, core: 2. Of those that a mesh axis runs over, the one named last changes fastest.
Arguments:
- volume: bfloat16 [16, 32, 32, 256], P(None, 'gx', 'gy'), may hold values from -6 to 6
- fine_kernel: bfloat16 [3, 3, 3, 16, 16], replicated, may hold values from -0.3125 to 0.3125
- coarse_kernel: bfloat16 [3, 3, 3, 32, 16], replicated, may hold values from -0.3125 to 0.3125
- fine_cotangent: bfloat16 [16, 32, 32, 256], P(None, 'gx', 'gy'), may hold values from -6 to 6
- coarse_cotangent: bfloat16 [32, 16, 16, 128], P(None, 'gx', 'gy'), may hold values from -18 to 18
Outputs:
- fine_out: bfloat16 [16, 32, 32, 256], P(None, 'gx', 'gy')
- coarse_out: bfloat16 [32, 16, 16, 128], P(None, 'gx', 'gy')
- volume_grad: bfloat16 [16, 32, 32, 256], P(None, 'gx', 'gy')
- fine_kernel_grad: float32 [3, 3, 3, 16, 16], replicated
- coarse_kernel_grad: float32 [3, 3, 3, 32, 16], replicated
All inputs are finite; a program needn't handle non-finite values.
Results may differ from a plain program's by a relative error of at most 0.0064.
Values may be sent and summed in bfloat16 or wider, within the bound.
No kernel may reach another device: no remote copies, remote signals or barrier semaphores. Data moves between devices by JAX's collectives and lax.ppermute only.
A program may use at most 64 MiB of HBM per device.

v0:
```python
import functools

import jax
import jax.numpy as jnp
from jax import lax
from jax.experimental import pallas as pl
from jax.experimental.pallas import tpu as pltpu
from jax.sharding import PartitionSpec as P

F32 = jnp.float32
BF16 = jnp.bfloat16


def mm(left, right):
    return jnp.dot(left, right, preferred_element_type=F32)


def mm_t(left, right):
    return lax.dot_general(left, right, (((1,), (1,)), ((), ())), preferred_element_type=F32)


def one_hot(shape, rule):
    rows = lax.broadcasted_iota(jnp.int32, shape, 0)
    cols = lax.broadcasted_iota(jnp.int32, shape, 1)
    return jnp.where(rule(rows, cols), 1.0, 0.0).astype(BF16)


def swap_matrix(outer, inner):
    count = outer * inner
    return one_hot((count, count), lambda r, c: c == (r % inner) * outer + r // inner)


def moved(values, width, offset):
    lanes = values.shape[1]
    place = lax.broadcasted_iota(jnp.int32, values.shape, 1) % width
    if offset == 1:
        return jnp.where(place == 0, 0.0, pltpu.roll(values, 1, 1))
    return jnp.where(place == width - 1, 0.0, pltpu.roll(values, lanes - 1, 1))


def combine(parts, width):
    rows = parts.shape[0] // 3
    return (
        parts[rows : 2 * rows]
        + moved(parts[:rows], width, 1)
        + moved(parts[2 * rows :], width, -1)
    )


def to_rows(values):
    chans, rows, width = values.shape
    return values.astype(F32).reshape(chans * rows, width).astype(BF16)


def band(taps_ref, out_ref, out_chans, in_chans, out_rows):
    wide = (out_rows + 2) * in_chans
    spread = one_hot((in_chans, wide), lambda r, c: c % in_chans == r)
    tiled = mm(taps_ref[...], spread)
    block = lax.broadcasted_iota(jnp.int32, (out_chans, wide), 1) // in_chans
    for a in range(3):
        for c in range(3):
            taps = [
                tiled[((a * 3 + b) * 3 + c) * out_chans : ((a * 3 + b) * 3 + c + 1) * out_chans]
                for b in range(3)
            ]
            for y in range(out_rows):
                value = jnp.where(
                    block == y,
                    taps[0],
                    jnp.where(block == y + 1, taps[1], jnp.where(block == y + 2, taps[2], 0.0)),
                )
                start = (c * out_rows + y) * out_chans
                out_ref[a, start : start + out_chans, :] = value.astype(BF16)


def weights_kernel(kf, kft, kc, kct, wa, wt, wc, wct, *, c1, c2, ny):
    band(kf, wa, c1, c1, ny + 2)
    band(kft, wt, c1, c1, ny)
    band(kc, wc, c2, c1, ny // 2 + 4)
    band(kct, wct, c1, c2, ny // 2 + 2)


def cot_pack_kernel(fc, cc, dn, up):
    c1, nz = fc.shape[:2]
    c2 = cc.shape[0]
    dn[:c1] = fc[:, 0]
    up[:c1] = fc[:, nz - 1]
    for ref in (dn, up):
        ref[c1:, :, : cc.shape[2]] = cc[: c2 // 2]
        ref[c1:, :, cc.shape[2] :] = cc[c2 // 2 :]


def rows_kernel(vol, lo, hi, own, dn, up):
    chans, nz, ny, nx = vol.shape
    swap = swap_matrix(ny, chans)
    depth = lo.shape[1]
    layers = [(lo, z) for z in range(depth)] + [(vol, z) for z in range(nz)]
    layers += [(hi, z) for z in range(depth)]
    edge = 2 * chans
    for place, (ref, z) in enumerate(layers):
        value = mm(swap, to_rows(ref[:, z])).astype(BF16)
        span = slice(place * nx, (place + 1) * nx)
        own[:, span] = value
        dn[:, span] = value[:edge]
        up[:, span] = value[-edge:]


def fine_kernel_fn(flags, xo, xl, xh, wa, fo_out, sl_out, pz_dn, pz_up, pz_own, *, c1, nz, ny, nx):
    swap_back = swap_matrix(c1, ny)
    pool = one_hot((nx, nx // 2), lambda r, c: r // 2 == c)
    sums = None
    half = nx // 2
    for layer in range(nz + 4):
        parts = None
        for dz in range(3):
            span = slice((layer + dz) * nx, (layer + dz + 1) * nx)
            x = jnp.concatenate([xl[:, span], xo[:, span], xh[:, span]], axis=0)
            term = mm(wa[dz], x)
            parts = term if parts is None else parts + term
        pre = combine(parts, nx)
        sig = jax.nn.sigmoid(pre)
        span = slice((layer + 1) * nx, (layer + 2) * nx)
        inner = slice(c1, c1 + c1 * ny)
        fo = (xo[:, span].astype(F32) + pre[inner] * sig[inner]).astype(BF16)
        if 1 <= layer <= nz + 2:
            sl_out[:, (layer - 1) * nx : layer * nx] = sig * (1.0 + pre * (1.0 - sig))
        if 2 <= layer < nz + 2:
            fo_out[:, layer - 2] = mm(swap_back, fo).reshape(c1, ny, nx).astype(BF16)
        pooled = mm(fo, pool)
        if layer % 2 == 0:
            sums = pooled
            continue
        sums = sums + pooled
        rows = [
            sums[2 * r * c1 : (2 * r + 1) * c1] + sums[(2 * r + 1) * c1 : (2 * r + 2) * c1]
            for r in range(ny // 2)
        ]
        value = jnp.concatenate(rows, axis=0) * 0.125
        place = layer // 2
        last = nz // 2 + 1
        if place == 0:
            value = jnp.where(flags[0] != 0, 0.0, value)
        if place == last:
            value = jnp.where(flags[1] != 0, 0.0, value)
        value = value.astype(BF16)
        if place < last:
            pz_up[:, place * half : (place + 1) * half] = value
        if place > 0:
            pz_dn[:, (place - 1) * half : place * half] = value
        if 0 < place < last:
            pz_own[:, (place - 1) * half : place * half] = value


def cot_rows_kernel(fc, cc, lo, hi, fc_out, cc_out, dn, up, *, c1, c2, ny):
    nz, nx = fc.shape[1], fc.shape[3]
    half = nx // 2
    hz, hy = nz // 2, ny // 2
    swap = swap_matrix(ny, c1)
    layers = [lo[:c1]] + [fc[:, z] for z in range(nz)] + [hi[:c1]]
    for place, value in enumerate(layers):
        span = slice(place * nx, (place + 1) * nx)
        fc_out[:, span] = mm(swap, to_rows(value)).astype(BF16)
    swap_c = swap_matrix(hz * hy, c2)
    blocks = [
        jnp.concatenate([lo[c1:, :, :half], lo[c1:, :, half:]], axis=0),
        cc[...],
        jnp.concatenate([hi[c1:, :, :half], hi[c1:, :, half:]], axis=0),
    ]
    for index, block in enumerate(blocks):
        value = mm(swap_c, to_rows(block)).astype(BF16)
        for z in range(hz):
            place = index * hz + z
            cc_out[:, place * half : (place + 1) * half] = value[z * hy * c2 : (z + 1) * hy * c2]
    wide = cc_out.shape[1]
    edge = 2 * c2
    for ref, fine_rows, coarse_rows in (
        (dn, slice(0, c1), slice(0, edge)),
        (up, slice((ny - 1) * c1, ny * c1), slice((hy - 2) * c2, hy * c2)),
    ):
        ref[:edge] = cc_out[coarse_rows]
        ref[edge : edge + c1] = fc_out[fine_rows, :wide]
        ref[edge + c1 : edge + 2 * c1] = fc_out[fine_rows, wide:]


def pooled_rows_kernel(lo, own, hi, dn, up):
    edge = dn.shape[0]
    start = 0
    for ref in (lo, own, hi):
        width = ref.shape[1]
        dn[:, start : start + width] = ref[:edge]
        up[:, start : start + width] = ref[-edge:]
        start += width


def coarse_kernel_fn(
    flags, po, pzl, pzh, pyl, pyh, cc, fc, cyl, cyh, sl, xo, xl, xh, wc, wct,
    co_out, fs_out, fg_out, g_out, p_ref, cs_ref, *, c1, c2, nz, ny, nx,
):
    half, hz, hy = nx // 2, nz // 2, ny // 2
    three = 3 * c1
    p_ref[:three] = pyl[...]
    p_ref[three + hy * c1 :] = pyh[...]
    start = 0
    for ref in (pzl, po, pzh):
        p_ref[three : three + hy * c1, start : start + ref.shape[1]] = ref[...]
        start += ref.shape[1]
    edge = 2 * c2
    swap_c = swap_matrix(c2, hz * hy)
    for pair in range((hz + 4) // 2):
        parts = None
        for dz in range(3):
            first = (2 * pair + dz) * half
            term = mm(wc[dz], p_ref[:, first : first + nx])
            parts = term if parts is None else parts + term
        pre = combine(parts, half)
        sig = jax.nn.sigmoid(pre)
        span = slice(pair * nx, (pair + 1) * nx)
        cot = jnp.concatenate([cyl[:edge, span], cc[:, span], cyh[:edge, span]], axis=0)
        cs_ref[:, span] = (cot.astype(F32) * (sig * (1.0 + pre * (1.0 - sig)))).astype(BF16)
        if pair == 1:
            inner = slice(edge, edge + hy * c2)
            out = (pre[inner] * sig[inner]).astype(BF16)
            stacked = jnp.concatenate([out[:, :half], out[:, half:]], axis=0)
            co_out[...] = mm(swap_c, stacked).astype(BF16)
    widen = one_hot((half, nx), lambda r, c: c // 2 == r)
    wide = cc.shape[1]
    for pair in range((hz + 2) // 2):
        parts = None
        for dz in range(3):
            first = (2 * pair + dz) * half
            term = mm(wct[dz], cs_ref[:, first : first + nx])
            parts = term if parts is None else parts + term
        grad = combine(parts, half) * 0.125
        high = grad.astype(BF16)
        low = (grad - high.astype(F32)).astype(BF16)
        for side in range(2):
            lanes = slice(side * half, (side + 1) * half)
            up = mm(high[:, lanes], widen) + mm(low[:, lanes], widen)
            blocks = [up[(y + 2) // 2 * c1 : (y + 2) // 2 * c1 + c1] for y in range(-1, ny + 1)]
            spread = jnp.concatenate(blocks, axis=0)
            coarse_layer = 2 * pair + side - 1
            for layer in (2 * coarse_layer, 2 * coarse_layer + 1):
                if not -1 <= layer <= nz:
                    continue
                place = layer + 1
                span = slice(place * nx, (place + 1) * nx)
                fold = place * nx // wide
                inside = slice(place * nx - fold * wide, (place + 1) * nx - fold * wide)
                edge_rows = slice(edge + fold * c1, edge + (fold + 1) * c1)
                cot = jnp.concatenate(
                    [cyl[edge_rows, inside], fc[:, span], cyh[edge_rows, inside]], axis=0
                )
                total = cot.astype(F32) + spread
                slope = total * sl[:, span]
                row = lax.broadcasted_iota(jnp.int32, slope.shape, 0) // c1
                outside = jnp.logical_and(row == 0, flags[2] != 0)
                outside = jnp.logical_or(outside, jnp.logical_and(row == ny + 1, flags[3] != 0))
                if layer == -1:
                    outside = jnp.logical_or(outside, flags[0] != 0)
                if layer == nz:
                    outside = jnp.logical_or(outside, flags[1] != 0)
                fs_out[:, span] = jnp.where(outside, 0.0, slope).astype(BF16)
                if 0 <= layer < nz:
                    fg_out[:, layer * nx : (layer + 1) * nx] = total[c1 : c1 + c1 * ny]
    nine = 9 * c1
    slopes = fs_out[c1 : c1 + c1 * ny, nx : (nz + 1) * nx].astype(F32)
    shifted = [
        moved(slopes, nx, -1).astype(BF16), slopes.astype(BF16), moved(slopes, nx, 1).astype(BF16)
    ]
    total = None
    for y in range(ny):
        left = jnp.concatenate([s[y * c1 : (y + 1) * c1] for s in shifted], axis=0)
        right = []
        for a in range(3):
            span = slice((a + 2) * nx, (a + 2 + nz) * nx)
            for b in range(3):
                at = y + b - 1
                if at < 0:
                    right.append(xl[c1:, span])
                elif at >= ny:
                    right.append(xh[:c1, span])
                else:
                    right.append(xo[at * c1 : (at + 1) * c1, span])
        term = mm_t(left, jnp.concatenate(right, axis=0))
        total = term if total is None else total + term
    g_out[:three, :nine] = total
    slopes = cs_ref[edge : edge + hy * c2, 2 * half : (2 + hz) * half].astype(F32)
    shifted = [
        moved(slopes, half, -1).astype(BF16),
        slopes.astype(BF16),
        moved(slopes, half, 1).astype(BF16),
    ]
    total = None
    for y in range(hy):
        left = jnp.concatenate([s[y * c2 : (y + 1) * c2] for s in shifted], axis=0)
        right = [
            p_ref[(y + 2) * c1 : (y + 5) * c1, (a + 2) * half : (a + 2 + hz) * half]
            for a in range(3)
        ]
        term = mm_t(left, jnp.concatenate(right, axis=0))
        total = term if total is None else total + term
    g_out[three:, :nine] = total


def volume_grad_kernel(fs, fg, wt, out, *, c1, nz, ny, nx):
    swap_back = swap_matrix(c1, ny)
    for layer in range(nz):
        parts = None
        for dz in range(3):
            term = mm(wt[dz], fs[:, (layer + dz) * nx : (layer + dz + 1) * nx])
            parts = term if parts is None else parts + term
        total = fg[:, layer * nx : (layer + 1) * nx] + combine(parts, nx)
        out[:, layer] = mm(swap_back, total.astype(BF16)).reshape(c1, ny, nx).astype(BF16)


def finish_kernel(*refs, c1, c2, scale_fine, scale_coarse):
    parts, (fine, coarse) = refs[:-2], refs[-2:]
    total = tree_sum([part[...].astype(F32) for part in parts])
    for a in range(3):
        for b in range(3):
            lanes = slice((a * 3 + b) * c1, (a * 3 + b + 1) * c1)
            for c in range(3):
                at = (a * 3 + b) * 3 + c
                fine[at] = total[c * c1 : (c + 1) * c1, lanes] * scale_fine
                first = 3 * c1 + c * c2
                coarse[at] = total[first : first + c2, lanes] * scale_coarse


def tree_sum(values):
    while len(values) > 1:
        values = [values[i] + values[i + 1] for i in range(0, len(values), 2)]
    return values[0]


def shapes(*pairs):
    return [jax.ShapeDtypeStruct(shape, kind) for shape, kind in pairs]


def call(body, outs, args, flops=0, flags=False, scratch=(), name=None):
    specs = [pl.BlockSpec(memory_space=pltpu.VMEM) for _ in args]
    if flags:
        specs[0] = pl.BlockSpec(memory_space=pltpu.SMEM)
    nbytes = sum(a.size * a.dtype.itemsize for a in args)
    return pl.pallas_call(
        body,
        out_shape=outs,
        in_specs=specs,
        out_specs=[pl.BlockSpec(memory_space=pltpu.VMEM) for _ in outs],
        scratch_shapes=list(scratch),
        cost_estimate=pl.CostEstimate(flops=flops, bytes_accessed=nbytes, transcendentals=0),
        name=name,
    )(*args)


def shift_axis(value, axis, step):
    count = lax.axis_size(axis)
    pairs = [(i, i + step) for i in range(count) if 0 <= i + step < count]
    return lax.ppermute(value, axis, pairs)


def swap_bits(value, bits):
    ny = lax.axis_size("gy")
    count = lax.axis_size("gx") * ny
    flip = sum((bit if axis == "gy" else bit * ny) for axis, bit in bits)
    return lax.ppermute(value, ("gx", "gy"), [(i, i ^ flip) for i in range(count)])


def local(volume, fine_kernel, coarse_kernel, fine_cotangent, coarse_cotangent):
    c1, nz, ny, nx = volume.shape
    c2 = coarse_cotangent.shape[0]
    hz, hy, half = nz // 2, ny // 2, nx // 2
    gx, gy = lax.axis_size("gx"), lax.axis_size("gy")
    cells = nz * gx * ny * gy * nx
    at_x, at_y = lax.axis_index("gx"), lax.axis_index("gy")
    flags = jnp.stack([at_x == 0, at_x == gx - 1, at_y == 0, at_y == gy - 1]).astype(jnp.int32)
    sizes = dict(c1=c1, nz=nz, ny=ny, nx=nx)

    depth = 3
    vol_lo = shift_axis(volume[:, nz - depth :], "gx", 1)
    vol_hi = shift_axis(volume[:, :depth], "gx", -1)

    taps_f = fine_kernel.reshape(27 * c1, c1)
    taps_c = coarse_kernel.reshape(27 * c2, c1)
    flip_f = fine_kernel[::-1, ::-1, ::-1].swapaxes(3, 4).reshape(27 * c1, c1)
    flip_c = coarse_kernel[::-1, ::-1, ::-1].swapaxes(3, 4).reshape(27 * c1, c2)
    wa, wt, wc, wct = call(
        functools.partial(weights_kernel, c1=c1, c2=c2, ny=ny),
        shapes(
            ((3, 3 * (ny + 2) * c1, (ny + 4) * c1), BF16),
            ((3, 3 * ny * c1, (ny + 2) * c1), BF16),
            ((3, 3 * (hy + 4) * c2, (hy + 6) * c1), BF16),
            ((3, 3 * (hy + 2) * c1, (hy + 4) * c2), BF16),
        ),
        [taps_f, flip_f, taps_c, flip_c],
        flops=10**9,
        name="weights",
    )
    cot_c = coarse_cotangent.reshape(c2, hz * hy, half)
    cot_dn, cot_up = call(
        cot_pack_kernel,
        shapes(((2 * c1, ny, nx), BF16), ((2 * c1, ny, nx), BF16)),
        [fine_cotangent, cot_c],
        flops=10**8,
        name="cot_pack",
    )

    layers = nz + 2 * depth
    own, row_dn, row_up = call(
        rows_kernel,
        shapes(
            ((ny * c1, layers * nx), BF16),
            ((2 * c1, layers * nx), BF16),
            ((2 * c1, layers * nx), BF16),
        ),
        [volume, vol_lo, vol_hi],
        flops=10**9,
        name="rows",
    )
    cot_lo = shift_axis(cot_up, "gx", 1)
    cot_hi = shift_axis(cot_dn, "gx", -1)
    row_lo = shift_axis(row_up, "gy", 1)
    row_hi = shift_axis(row_dn, "gy", -1)

    fine_out, slopes, pz_dn, pz_up, pz_own = call(
        functools.partial(fine_kernel_fn, **sizes),
        shapes(
            ((c1, nz, ny, nx), BF16),
            (((ny + 2) * c1, (nz + 2) * nx), F32),
            ((hy * c1, (hz + 1) * half), BF16),
            ((hy * c1, (hz + 1) * half), BF16),
            ((hy * c1, hz * half), BF16),
        ),
        [flags, own, row_lo, row_hi, wa],
        flops=3 * 10**9,
        flags=True,
        name="fine",
    )
    pz_lo = shift_axis(pz_up, "gx", 1)
    pz_hi = shift_axis(pz_dn, "gx", -1)
    fcot, ccot, cy_dn, cy_up = call(
        functools.partial(cot_rows_kernel, c1=c1, c2=c2, ny=ny),
        shapes(
            ((ny * c1, (nz + 2) * nx), BF16),
            ((hy * c2, 3 * hz * half), BF16),
            ((2 * c2 + 2 * c1, 3 * hz * half), BF16),
            ((2 * c2 + 2 * c1, 3 * hz * half), BF16),
        ),
        [fine_cotangent, cot_c, cot_lo, cot_hi],
        flops=10**9,
        name="cot_rows",
    )
    cy_lo = shift_axis(cy_up, "gy", 1)
    cy_hi = shift_axis(cy_dn, "gy", -1)
    wide = (hz + 2 * (hz + 1)) * half
    py_dn, py_up = call(
        pooled_rows_kernel,
        shapes(((3 * c1, wide), BF16), ((3 * c1, wide), BF16)),
        [pz_lo, pz_own, pz_hi],
        flops=10**8,
        name="pooled_rows",
    )
    py_lo = shift_axis(py_up, "gy", 1)
    py_hi = shift_axis(py_dn, "gy", -1)

    coarse_out, fslope, fgrad, terms = call(
        functools.partial(coarse_kernel_fn, c2=c2, **sizes),
        shapes(
            ((c2 * hz * hy, half), BF16),
            (((ny + 2) * c1, (nz + 2) * nx), BF16),
            ((ny * c1, nz * nx), F32),
            ((3 * c1 + 3 * c2, 9 * c1), F32),
        ),
        [flags, pz_own, pz_lo, pz_hi, py_lo, py_hi, ccot, fcot, cy_lo, cy_hi, slopes]
        + [own, row_lo, row_hi, wc, wct],
        flops=4 * 10**9,
        flags=True,
        scratch=[
            pltpu.VMEM(((hy + 6) * c1, wide), BF16),
            pltpu.VMEM(((hy + 4) * c2, 3 * hz * half), BF16),
        ],
        name="coarse",
    )

    bits = [("gy", 1 << n) for n in range(gy.bit_length() - 1)]
    bits += [("gx", 1 << n) for n in range(gx.bit_length() - 1)]
    first = len(bits) % 2
    rounds = [bits[:1]] * first
    rounds += [bits[n : n + 2] for n in range(first, len(bits), 2)]
    value = terms
    for index, group in enumerate(rounds):
        if index:
            value = value.astype(BF16)
        parts = [value] + [swap_bits(value, [bit]) for bit in group]
        if len(group) == 2:
            parts.append(swap_bits(value, group))
        if index + 1 < len(rounds):
            value = tree_sum([part.astype(F32) for part in parts])
    (volume_grad,) = call(
        functools.partial(volume_grad_kernel, **sizes),
        shapes(((c1, nz, ny, nx), BF16)),
        [fslope, fgrad, wt],
        flops=2 * 10**9,
        name="volume_grad",
    )
    fine_grad, coarse_grad = call(
        functools.partial(
            finish_kernel,
            c1=c1,
            c2=c2,
            scale_fine=cells ** (-0.5),
            scale_coarse=(cells // 8) ** (-0.5),
        ),
        shapes(((27, c1, c1), F32), ((27, c2, c1), F32)),
        parts,
        flops=10**7,
        name="finish",
    )
    return (
        fine_out,
        coarse_out.reshape(c2, hz, hy, half),
        volume_grad,
        fine_grad.reshape(fine_kernel.shape),
        coarse_grad.reshape(coarse_kernel.shape),
    )


def solution(mesh):
    split = P(None, "gx", "gy", None)
    return jax.shard_map(
        local,
        mesh=mesh,
        in_specs=(split, P(), P(), split, split),
        out_specs=(split, split, split, P(), P()),
        check_vma=False,
    )
```

profile of v0, /device:TPU:0, one launch (start us, length us, event | category | flops | bytes accessed | tf_op | source)
XLA Modules:
  0.0 99.5 jit_solution(12928114184745944780)
XLA Ops:
  0.7 1.1 %fusion = (bf16[16,3,8,256]{3,2,1,0:T(8,128)(2,1)S(1)}, bf16[16,3,8,256]{3,2,1,0:T(8,128)(2,1)S(1)}) fusion(bf16[16,4,8,256]{3,2,1,0:T(8,128)(2,1)} %vol.1), kind=kLoop, calls=%fused_computation.4 | loop fusion | bytes 786432 | tf_op jit(solution)/shard_map/slice | solution.py:380
  1.8 1.3 %collective-permute-start.1 = (bf16[16,3,8,256]{3,2,1,0:T(8,128)(2,1)S(1)}, bf16[16,3,8,256]{3,2,1,0:T(8,128)(2,1)S(1)}, u32[]{:S(2)}, u32[]{:S(2)}) collective-permute-start(bf16[16,3,8,256]{3,2,1,0:T(8,128)(2,1)S(1)} %get-tuple-element.62), channel_id=1, source_target_pairs={{4,0},{8,4},{12,8},{16,12},{20,16},{24,20},{28,24},{5,1},{9,5},{13... | collective-permute-start | bytes 589832 | tf_op jit(solution)/shard_map/ppermute | solution.py:358
  3.0 5.5 %collective-permute-start = (bf16[16,3,8,256]{3,2,1,0:T(8,128)(2,1)S(1)}, bf16[16,3,8,256]{3,2,1,0:T(8,128)(2,1)S(1)}, u32[]{:S(2)}, u32[]{:S(2)}) collective-permute-start(bf16[16,3,8,256]{3,2,1,0:T(8,128)(2,1)S(1)} %get-tuple-element.63), channel_id=1, source_target_pairs={{0,4},{4,8},{8,12},{12,16},{16,20},{20,24},{24,28},{1,5},{5,9},{9,... | collective-permute-start | bytes 589832 | tf_op jit(solution)/shard_map/ppermute | solution.py:358
  8.6 1.7 %cot_pack.1 = (bf16[32,8,256]{2,1,0:T(8,128)(2,1)}, bf16[32,8,256]{2,1,0:T(8,128)(2,1)}) custom-call(bf16[16,4,8,256]{3,2,1,0:T(8,128)(2,1)} %fc.3, bf16[32,8,128]{2,1,0:T(8,128)(2,1)} %bitcast.22), custom_call_target="tpu_custom_call" | custom-call | flops 100000000 | bytes 327680 | tf_op jit(solution)/shard_map/cot_pack/pallas_call | solution.py:344
  10.3 4.8 %collective-permute-start.8 = (bf16[32,8,256]{2,1,0:T(8,128)(2,1)}, bf16[32,8,256]{2,1,0:T(8,128)(2,1)S(1)}, u32[]{:S(2)}, u32[]{:S(2)}) collective-permute-start(bf16[32,8,256]{2,1,0:T(8,128)(2,1)} %get-tuple-element.41), channel_id=1, source_target_pairs={{0,4},{4,8},{8,12},{12,16},{16,20},{20,24},{24,28},{1,5},{5,9},{9,... | collective-permute-start | bytes 393224 | tf_op jit(solution)/shard_map/ppermute | solution.py:358
  15.1 1.3 %collective-permute-start.9 = (bf16[32,8,256]{2,1,0:T(8,128)(2,1)}, bf16[32,8,256]{2,1,0:T(8,128)(2,1)S(1)}, u32[]{:S(2)}, u32[]{:S(2)}) collective-permute-start(bf16[32,8,256]{2,1,0:T(8,128)(2,1)} %get-tuple-element.42), channel_id=1, source_target_pairs={{4,0},{8,4},{12,8},{16,12},{20,16},{24,20},{28,24},{5,1},{9,5},{13... | collective-permute-start | bytes 393224 | tf_op jit(solution)/shard_map/ppermute | solution.py:358
  20.0 2.3 %rows.1 = (bf16[128,2560]{1,0:T(8,128)(2,1)}, bf16[32,2560]{1,0:T(8,128)(2,1)}, bf16[32,2560]{1,0:T(8,128)(2,1)}) custom-call(bf16[16,4,8,256]{3,2,1,0:T(8,128)(2,1)} %vol.1, bf16[16,3,8,256]{3,2,1,0:T(8,128)(2,1)} %copy-done.7, bf16[16,3,8,256]{3,2,1,0:T(8,128)(2,1)} %copy-done.6), custom_call_target="tpu_custom_call" | custom-call | flops 1000000000 | bytes 655360 | tf_op jit(solution)/shard_map/rows/pallas_call | solution.py:344
  22.3 1.3 %collective-permute-start.2 = (bf16[32,2560]{1,0:T(8,128)(2,1)}, bf16[32,2560]{1,0:T(8,128)(2,1)S(1)}, u32[]{:S(2)}, u32[]{:S(2)}) collective-permute-start(bf16[32,2560]{1,0:T(8,128)(2,1)} %get-tuple-element.32), channel_id=1, source_target_pairs={{0,1},{1,2},{2,3},{4,5},{5,6},{6,7},{8,9},{9,10},{10,11},{12,13},{... | collective-permute-start | bytes 491528 | tf_op jit(solution)/shard_map/ppermute | solution.py:358
  23.6 1.3 %collective-permute-start.3 = (bf16[32,2560]{1,0:T(8,128)(2,1)}, bf16[32,2560]{1,0:T(8,128)(2,1)S(1)}, u32[]{:S(2)}, u32[]{:S(2)}) collective-permute-start(bf16[32,2560]{1,0:T(8,128)(2,1)} %get-tuple-element.33), channel_id=1, source_target_pairs={{1,0},{2,1},{3,2},{5,4},{6,5},{7,6},{9,8},{10,9},{11,10},{13,12},{... | collective-permute-start | bytes 491528 | tf_op jit(solution)/shard_map/ppermute | solution.py:358
  24.9 3.0 %weights.1 = (bf16[3,480,192]{2,1,0:T(8,128)(2,1)}, bf16[3,384,160]{2,1,0:T(8,128)(2,1)}, bf16[3,768,160]{2,1,0:T(8,128)(2,1)}, bf16[3,288,256]{2,1,0:T(8,128)(2,1)}) custom-call(bf16[432,16]{1,0:T(8,128)(2,1)} %bitcast.18, bf16[432,16]{1,0:T(8,128)(2,1)} %bitcast.20, bf16[864,16]{1,0:T(8,128)(2,1)} %bitcast.17, bf16[432,32]{1,0:T(8,128)(2,1)} %bitcast.19), custom_call_target="tpu_custom_call" | custom-call | flops 1000000000 | bytes 82944 | tf_op jit(solution)/shard_map/weights/pallas_call | solution.py:344
  29.5 6.3 %fine.1 = (bf16[16,4,8,256]{3,2,1,0:T(8,128)(2,1)}, f32[160,1536]{1,0:T(8,128)}, bf16[64,384]{1,0:T(8,128)(2,1)}, bf16[64,384]{1,0:T(8,128)(2,1)}, bf16[64,256]{1,0:T(8,128)(2,1)}) custom-call(s32[4]{0:T(128)} %add_convert_fusion.2.flags, bf16[128,2560]{1,0:T(8,128)(2,1)} %get-tuple-element.31.xo, bf16[32,2560]{1,0:T(8,128)(2,1)} %copy-done.8, ...), custom_call_target="tpu_custom_call" | custom-call | flops 3000000000 | bytes 1536016 | tf_op jit(solution)/shard_map/fine/pallas_call | solution.py:344
  35.8 4.5 %collective-permute-start.4 = (bf16[64,384]{1,0:T(8,128)(2,1)}, bf16[64,384]{1,0:T(8,128)(2,1)S(1)}, u32[]{:S(2)}, u32[]{:S(2)}) collective-permute-start(bf16[64,384]{1,0:T(8,128)(2,1)} %get-tuple-element.37), channel_id=1, source_target_pairs={{0,4},{4,8},{8,12},{12,16},{16,20},{20,24},{24,28},{1,5},{5,9},{9,... | collective-permute-start | bytes 147464 | tf_op jit(solution)/shard_map/ppermute | solution.py:358
  40.3 1.3 %collective-permute-start.5 = (bf16[64,384]{1,0:T(8,128)(2,1)}, bf16[64,384]{1,0:T(8,128)(2,1)S(1)}, u32[]{:S(2)}, u32[]{:S(2)}) collective-permute-start(bf16[64,384]{1,0:T(8,128)(2,1)} %get-tuple-element.38), channel_id=1, source_target_pairs={{4,0},{8,4},{12,8},{16,12},{20,16},{24,20},{28,24},{5,1},{9,5},{13... | collective-permute-start | bytes 147464 | tf_op jit(solution)/shard_map/ppermute | solution.py:358
  42.9 2.3 %cot_rows.1 = (bf16[128,1536]{1,0:T(8,128)(2,1)}, bf16[128,768]{1,0:T(8,128)(2,1)}, bf16[96,768]{1,0:T(8,128)(2,1)}, bf16[96,768]{1,0:T(8,128)(2,1)}) custom-call(bf16[16,4,8,256]{3,2,1,0:T(8,128)(2,1)} %fc.3, bf16[32,8,128]{2,1,0:T(8,128)(2,1)} %bitcast.23, bf16[32,8,256]{2,1,0:T(8,128)(2,1)} %copy-done.12, bf16[32,8,256]{2,1,0:T(8,128)(2,1)} %copy-done.13), custom_call_target="tpu_custom_call" | custom-call | flops 1000000000 | bytes 589824 | tf_op jit(solution)/shard_map/cot_rows/pallas_call | solution.py:344
  45.2 5.5 %collective-permute-start.10 = (bf16[96,768]{1,0:T(8,128)(2,1)}, bf16[96,768]{1,0:T(8,128)(2,1)S(1)}, u32[]{:S(2)}, u32[]{:S(2)}) collective-permute-start(bf16[96,768]{1,0:T(8,128)(2,1)} %get-tuple-element.45), channel_id=1, source_target_pairs={{0,1},{1,2},{2,3},{4,5},{5,6},{6,7},{8,9},{9,10},{10,11},{12,13},{... | collective-permute-start | bytes 442376 | tf_op jit(solution)/shard_map/ppermute | solution.py:358
  50.7 1.3 %collective-permute-start.11 = (bf16[96,768]{1,0:T(8,128)(2,1)}, bf16[96,768]{1,0:T(8,128)(2,1)S(1)}, u32[]{:S(2)}, u32[]{:S(2)}) collective-permute-start(bf16[96,768]{1,0:T(8,128)(2,1)} %get-tuple-element.46), channel_id=1, source_target_pairs={{1,0},{2,1},{3,2},{5,4},{6,5},{7,6},{9,8},{10,9},{11,10},{13,12},{... | collective-permute-start | bytes 442376 | tf_op jit(solution)/shard_map/ppermute | solution.py:358
  52.6 1.5 %pooled_rows.1 = (bf16[48,1024]{1,0:T(8,128)(2,1)}, bf16[48,1024]{1,0:T(8,128)(2,1)}) custom-call(bf16[64,384]{1,0:T(8,128)(2,1)} %copy-done.16, bf16[64,256]{1,0:T(8,128)(2,1)} %get-tuple-element.36.own.po, bf16[64,384]{1,0:T(8,128)(2,1)} %copy-done.17), custom_call_target="tpu_custom_call" | custom-call | flops 100000000 | bytes 131072 | tf_op jit(solution)/shard_map/pooled_rows/pallas_call | solution.py:344
  54.2 3.3 %collective-permute-start.6 = (bf16[48,1024]{1,0:T(8,128)(2,1)}, bf16[48,1024]{1,0:T(8,128)(2,1)S(1)}, u32[]{:S(2)}, u32[]{:S(2)}) collective-permute-start(bf16[48,1024]{1,0:T(8,128)(2,1)} %get-tuple-element.39), channel_id=1, source_target_pairs={{0,1},{1,2},{2,3},{4,5},{5,6},{6,7},{8,9},{9,10},{10,11},{12,13},{... | collective-permute-start | bytes 294920 | tf_op jit(solution)/shard_map/ppermute | solution.py:358
  57.5 1.3 %collective-permute-start.7 = (bf16[48,1024]{1,0:T(8,128)(2,1)}, bf16[48,1024]{1,0:T(8,128)(2,1)S(1)}, u32[]{:S(2)}, u32[]{:S(2)}) collective-permute-start(bf16[48,1024]{1,0:T(8,128)(2,1)} %get-tuple-element.40), channel_id=1, source_target_pairs={{1,0},{2,1},{3,2},{5,4},{6,5},{7,6},{9,8},{10,9},{11,10},{13,12},{... | collective-permute-start | bytes 294920 | tf_op jit(solution)/shard_map/ppermute | solution.py:358
  58.9 3.3 %collective-permute-done.7.pyh = bf16[48,1024]{1,0:T(8,128)(2,1)S(1)} collective-permute-done((bf16[48,1024]{1,0:T(8,128)(2,1)}, bf16[48,1024]{1,0:T(8,128)(2,1)S(1)}, u32[]{:S(2)}, u32[]{:S(2)}) %collective-permute-start.7) | collective-permute-done | bytes 98336 | tf_op jit(solution)/shard_map/ppermute | solution.py:358
  62.8 7.1 %coarse.1 = (bf16[256,128]{1,0:T(8,128)(2,1)}, bf16[160,1536]{1,0:T(8,128)(2,1)}, f32[128,1024]{1,0:T(8,128)}, f32[144,144]{1,0:T(8,128)}) custom-call(s32[4]{0:T(128)} %add_convert_fusion.2.flags, bf16[64,256]{1,0:T(8,128)(2,1)} %get-tuple-element.36.own.po, bf16[64,384]{1,0:T(8,128)(2,1)} %copy-done.16, bf16[64,384]{1,0:T(8,128)(2,1)} %copy-done.17, ...), custom_call_target="tpu_custom_call" | custom-call | flops 4000000000 | bytes 4358160 | tf_op jit(solution)/shard_map/coarse/pallas_call | solution.py:344
  69.8 3.2 %collective-permute-start.12 = (f32[144,144]{1,0:T(8,128)}, f32[144,144]{1,0:T(8,128)S(1)}, u32[]{:S(2)}, u32[]{:S(2)}) collective-permute-start(f32[144,144]{1,0:T(8,128)} %get-tuple-element.54), channel_id=1, source_target_pairs={{0,1},{1,0},{2,3},{3,2},{4,5},{5,4},{6,7},{7,6},{8,9},{9,8},{10,11... | collective-permute-start | bytes 248840 | tf_op jit(solution)/shard_map/ppermute | solution.py:365
  73.1 1.2 %collective-permute-done.12 = f32[144,144]{1,0:T(8,128)S(1)} collective-permute-done((f32[144,144]{1,0:T(8,128)}, f32[144,144]{1,0:T(8,128)S(1)}, u32[]{:S(2)}, u32[]{:S(2)}) %collective-permute-start.12) | collective-permute-done | bytes 82976 | tf_op jit(solution)/shard_map/ppermute | solution.py:365
  75.2 2.4 %collective-permute-start.15 = (bf16[144,144]{1,0:T(8,128)(2,1)S(1)}, bf16[144,144]{1,0:T(8,128)(2,1)S(1)}, u32[]{:S(2)}, u32[]{:S(2)}) collective-permute-start(bf16[144,144]{1,0:T(8,128)(2,1)S(1)} %add_convert_fusion.1), channel_id=1, source_target_pairs={{0,6},{1,7},{2,4},{3,5},{4,2},{5,3},{6,0},{7,1},{8,14},{9,15},{10,... | collective-permute-start | bytes 124424 | tf_op jit(solution)/shard_map/ppermute | solution.py:365
  78.0 1.4 %collective-permute-start.13 = (bf16[144,144]{1,0:T(8,128)(2,1)S(1)}, bf16[144,144]{1,0:T(8,128)(2,1)S(1)}, u32[]{:S(2)}, u32[]{:S(2)}) collective-permute-start(bf16[144,144]{1,0:T(8,128)(2,1)S(1)} %add_convert_fusion.1), channel_id=1, source_target_pairs={{0,2},{1,3},{2,0},{3,1},{4,6},{5,7},{6,4},{7,5},{8,10},{9,11},{10,... | collective-permute-start | bytes 124424 | tf_op jit(solution)/shard_map/ppermute | solution.py:365
  79.4 1.3 %collective-permute-done.15 = bf16[144,144]{1,0:T(8,128)(2,1)S(1)} collective-permute-done((bf16[144,144]{1,0:T(8,128)(2,1)S(1)}, bf16[144,144]{1,0:T(8,128)(2,1)S(1)}, u32[]{:S(2)}, u32[]{:S(2)}) %collective-permute-start.15) | collective-permute-done | bytes 41504 | tf_op jit(solution)/shard_map/ppermute | solution.py:365
  80.7 1.6 %collective-permute-done.14 = bf16[144,144]{1,0:T(8,128)(2,1)S(1)} collective-permute-done((bf16[144,144]{1,0:T(8,128)(2,1)S(1)}, bf16[144,144]{1,0:T(8,128)(2,1)S(1)}, u32[]{:S(2)}, u32[]{:S(2)}) %collective-permute-start.14) | collective-permute-done | bytes 41504 | tf_op jit(solution)/shard_map/ppermute | solution.py:365
  82.4 5.7 %collective-permute-start.18 = (bf16[144,144]{1,0:T(8,128)(2,1)S(1)}, bf16[144,144]{1,0:T(8,128)(2,1)S(1)}, u32[]{:S(2)}, u32[]{:S(2)}) collective-permute-start(bf16[144,144]{1,0:T(8,128)(2,1)S(1)} %add_convert_fusion.refs_0_), channel_id=1, source_target_pairs={{0,24},{1,25},{2,26},{3,27},{4,28},{5,29},{6,30},{7,31},{8,16},{9,... | collective-permute-start | bytes 124424 | tf_op jit(solution)/shard_map/ppermute | solution.py:365
  88.7 4.1 %volume_grad.1 = bf16[16,4,8,256]{3,2,1,0:T(8,128)(2,1)} custom-call(bf16[160,1536]{1,0:T(8,128)(2,1)} %get-tuple-element.51.fs, f32[128,1024]{1,0:T(8,128)} %get-tuple-element.52.fg, bf16[3,384,160]{2,1,0:T(8,128)(2,1)} %get-tuple-element.53.wt), custom_call_target="tpu_custom_call" | custom-call | flops 2000000000 | bytes 1384448 | tf_op jit(solution)/shard_map/volume_grad/pallas_call | solution.py:344
  92.9 1.5 %collective-permute-done.17.refs_2_ = bf16[144,144]{1,0:T(8,128)(2,1)S(1)} collective-permute-done((bf16[144,144]{1,0:T(8,128)(2,1)S(1)}, bf16[144,144]{1,0:T(8,128)(2,1)S(1)}, u32[]{:S(2)}, u32[]{:S(2)}) %collective-permute-start.17) | collective-permute-done | bytes 41504 | tf_op jit(solution)/shard_map/ppermute | solution.py:365
  95.6 2.0 %finish.1 = (f32[27,16,16]{2,1,0:T(8,128)}, f32[27,32,16]{2,1,0:T(8,128)}) custom-call(bf16[144,144]{1,0:T(8,128)(2,1)} %copy-done.1, bf16[144,144]{1,0:T(8,128)(2,1)} %copy-done.5, bf16[144,144]{1,0:T(8,128)(2,1)} %copy-done.4, bf16[144,144]{1,0:T(8,128)(2,1)} %copy-done.3), custom_call_target="tpu_custom_call" | custom-call | flops 10000000 | bytes 165888 | tf_op jit(solution)/shard_map/finish/pallas_call | solution.py:344
  97.7 1.9 %copy.12 = f32[3,3,3,32,16]{3,4,2,1,0:T(8,128)} copy(f32[3,3,3,32,16]{4,3,2,1,0:T(8,128)} %bitcast.16) | data formatting | bytes 110592
  (60 shorter events, 11.0 us)
Async XLA Ops:
  0.6 15.7 %copy-start = (bf16[3,3,3,32,16]{3,4,2,1,0:T(8,128)(2,1)S(1)}, bf16[3,3,3,32,16]{3,4,2,1,0:T(8,128)(2,1)}, u32[]{:S(2)}) copy-start(bf16[3,3,3,32,16]{3,4,2,1,0:T(8,128)(2,1)} %param.7) | copy-start | bytes 82948
  0.6 17.2 %copy-start.2 = (bf16[3,3,3,16,16]{4,3,2,1,0:T(8,128)(2,1)S(1)}, bf16[3,3,3,16,16]{4,3,2,1,0:T(8,128)(2,1)}, u32[]{:S(2)}) copy-start(bf16[3,3,3,16,16]{4,3,2,1,0:T(8,128)(2,1)} %param.6) | copy-start | bytes 41476
  1.8 16.9 %collective-permute-start.1 = (bf16[16,3,8,256]{3,2,1,0:T(8,128)(2,1)S(1)}, bf16[16,3,8,256]{3,2,1,0:T(8,128)(2,1)S(1)}, u32[]{:S(2)}, u32[]{:S(2)}) collective-permute-start(bf16[16,3,8,256]{3,2,1,0:T(8,128)(2,1)S(1)} %get-tuple-element.62), channel_id=1, source_target_pairs={{4,0},{8,4},{12,8},{16,12},{20,16},{24,20},{28,24},{5,1},{9,5},{13... | collective-permute-start | bytes 589832 | tf_op jit(solution)/shard_map/ppermute | solution.py:358
  3.0 15.6 %collective-permute-start = (bf16[16,3,8,256]{3,2,1,0:T(8,128)(2,1)S(1)}, bf16[16,3,8,256]{3,2,1,0:T(8,128)(2,1)S(1)}, u32[]{:S(2)}, u32[]{:S(2)}) collective-permute-start(bf16[16,3,8,256]{3,2,1,0:T(8,128)(2,1)S(1)} %get-tuple-element.63), channel_id=1, source_target_pairs={{0,4},{4,8},{8,12},{12,16},{16,20},{20,24},{24,28},{1,5},{5,9},{9,... | collective-permute-start | bytes 589832 | tf_op jit(solution)/shard_map/ppermute | solution.py:358
  10.3 31.4 %collective-permute-start.8 = (bf16[32,8,256]{2,1,0:T(8,128)(2,1)}, bf16[32,8,256]{2,1,0:T(8,128)(2,1)S(1)}, u32[]{:S(2)}, u32[]{:S(2)}) collective-permute-start(bf16[32,8,256]{2,1,0:T(8,128)(2,1)} %get-tuple-element.41), channel_id=1, source_target_pairs={{0,4},{4,8},{8,12},{12,16},{16,20},{20,24},{24,28},{1,5},{5,9},{9,... | collective-permute-start | bytes 393224 | tf_op jit(solution)/shard_map/ppermute | solution.py:358
  15.1 26.6 %collective-permute-start.9 = (bf16[32,8,256]{2,1,0:T(8,128)(2,1)}, bf16[32,8,256]{2,1,0:T(8,128)(2,1)S(1)}, u32[]{:S(2)}, u32[]{:S(2)}) collective-permute-start(bf16[32,8,256]{2,1,0:T(8,128)(2,1)} %get-tuple-element.42), channel_id=1, source_target_pairs={{4,0},{8,4},{12,8},{16,12},{20,16},{24,20},{28,24},{5,1},{9,5},{13... | collective-permute-start | bytes 393224 | tf_op jit(solution)/shard_map/ppermute | solution.py:358
  18.6 0.7 copy-start.6
  19.3 0.7 copy-start.7
  22.3 6.2 %collective-permute-start.2 = (bf16[32,2560]{1,0:T(8,128)(2,1)}, bf16[32,2560]{1,0:T(8,128)(2,1)S(1)}, u32[]{:S(2)}, u32[]{:S(2)}) collective-permute-start(bf16[32,2560]{1,0:T(8,128)(2,1)} %get-tuple-element.32), channel_id=1, source_target_pairs={{0,1},{1,2},{2,3},{4,5},{5,6},{6,7},{8,9},{9,10},{10,11},{12,13},{... | collective-permute-start | bytes 491528 | tf_op jit(solution)/shard_map/ppermute | solution.py:358
  23.6 5.2 %collective-permute-start.3 = (bf16[32,2560]{1,0:T(8,128)(2,1)}, bf16[32,2560]{1,0:T(8,128)(2,1)S(1)}, u32[]{:S(2)}, u32[]{:S(2)}) collective-permute-start(bf16[32,2560]{1,0:T(8,128)(2,1)} %get-tuple-element.33), channel_id=1, source_target_pairs={{1,0},{2,1},{3,2},{5,4},{6,5},{7,6},{9,8},{10,9},{11,10},{13,12},{... | collective-permute-start | bytes 491528 | tf_op jit(solution)/shard_map/ppermute | solution.py:358
  28.5 0.7 copy-start.8
  28.8 0.7 copy-start.9
  35.8 16.2 %collective-permute-start.4 = (bf16[64,384]{1,0:T(8,128)(2,1)}, bf16[64,384]{1,0:T(8,128)(2,1)S(1)}, u32[]{:S(2)}, u32[]{:S(2)}) collective-permute-start(bf16[64,384]{1,0:T(8,128)(2,1)} %get-tuple-element.37), channel_id=1, source_target_pairs={{0,4},{4,8},{8,12},{12,16},{16,20},{20,24},{24,28},{1,5},{5,9},{9,... | collective-permute-start | bytes 147464 | tf_op jit(solution)/shard_map/ppermute | solution.py:358
  40.3 11.7 %collective-permute-start.5 = (bf16[64,384]{1,0:T(8,128)(2,1)}, bf16[64,384]{1,0:T(8,128)(2,1)S(1)}, u32[]{:S(2)}, u32[]{:S(2)}) collective-permute-start(bf16[64,384]{1,0:T(8,128)(2,1)} %get-tuple-element.38), channel_id=1, source_target_pairs={{4,0},{8,4},{12,8},{16,12},{20,16},{24,20},{28,24},{5,1},{9,5},{13... | collective-permute-start | bytes 147464 | tf_op jit(solution)/shard_map/ppermute | solution.py:358
  41.6 0.6 copy-start.12
  42.3 0.6 copy-start.13
  45.2 13.6 %collective-permute-start.10 = (bf16[96,768]{1,0:T(8,128)(2,1)}, bf16[96,768]{1,0:T(8,128)(2,1)S(1)}, u32[]{:S(2)}, u32[]{:S(2)}) collective-permute-start(bf16[96,768]{1,0:T(8,128)(2,1)} %get-tuple-element.45), channel_id=1, source_target_pairs={{0,1},{1,2},{2,3},{4,5},{5,6},{6,7},{8,9},{9,10},{10,11},{12,13},{... | collective-permute-start | bytes 442376 | tf_op jit(solution)/shard_map/ppermute | solution.py:358
  50.7 8.1 %collective-permute-start.11 = (bf16[96,768]{1,0:T(8,128)(2,1)}, bf16[96,768]{1,0:T(8,128)(2,1)S(1)}, u32[]{:S(2)}, u32[]{:S(2)}) collective-permute-start(bf16[96,768]{1,0:T(8,128)(2,1)} %get-tuple-element.46), channel_id=1, source_target_pairs={{1,0},{2,1},{3,2},{5,4},{6,5},{7,6},{9,8},{10,9},{11,10},{13,12},{... | collective-permute-start | bytes 442376 | tf_op jit(solution)/shard_map/ppermute | solution.py:358
  54.2 4.7 %collective-permute-start.6 = (bf16[48,1024]{1,0:T(8,128)(2,1)}, bf16[48,1024]{1,0:T(8,128)(2,1)S(1)}, u32[]{:S(2)}, u32[]{:S(2)}) collective-permute-start(bf16[48,1024]{1,0:T(8,128)(2,1)} %get-tuple-element.39), channel_id=1, source_target_pairs={{0,1},{1,2},{2,3},{4,5},{5,6},{6,7},{8,9},{9,10},{10,11},{12,13},{... | collective-permute-start | bytes 294920 | tf_op jit(solution)/shard_map/ppermute | solution.py:358
  57.5 4.6 %collective-permute-start.7 = (bf16[48,1024]{1,0:T(8,128)(2,1)}, bf16[48,1024]{1,0:T(8,128)(2,1)S(1)}, u32[]{:S(2)}, u32[]{:S(2)}) collective-permute-start(bf16[48,1024]{1,0:T(8,128)(2,1)} %get-tuple-element.40), channel_id=1, source_target_pairs={{1,0},{2,1},{3,2},{5,4},{6,5},{7,6},{9,8},{10,9},{11,10},{13,12},{... | collective-permute-start | bytes 294920 | tf_op jit(solution)/shard_map/ppermute | solution.py:358
  58.8 3.3 %copy-start.10 = (bf16[96,768]{1,0:T(8,128)(2,1)}, bf16[96,768]{1,0:T(8,128)(2,1)S(1)}, u32[]{:S(2)}) copy-start(bf16[96,768]{1,0:T(8,128)(2,1)S(1)} %collective-permute-done.10.cyl) | copy-start | bytes 442372
  58.8 3.3 %copy-start.11 = (bf16[96,768]{1,0:T(8,128)(2,1)}, bf16[96,768]{1,0:T(8,128)(2,1)S(1)}, u32[]{:S(2)}) copy-start(bf16[96,768]{1,0:T(8,128)(2,1)S(1)} %collective-permute-done.11.cyh) | copy-start | bytes 442372
  58.9 3.3 %copy-start.14 = (bf16[48,1024]{1,0:T(8,128)(2,1)}, bf16[48,1024]{1,0:T(8,128)(2,1)S(1)}, u32[]{:S(2)}) copy-start(bf16[48,1024]{1,0:T(8,128)(2,1)S(1)} %collective-permute-done.6.pyl) | copy-start | bytes 294916
  69.8 4.5 %collective-permute-start.12 = (f32[144,144]{1,0:T(8,128)}, f32[144,144]{1,0:T(8,128)S(1)}, u32[]{:S(2)}, u32[]{:S(2)}) collective-permute-start(f32[144,144]{1,0:T(8,128)} %get-tuple-element.54), channel_id=1, source_target_pairs={{0,1},{1,0},{2,3},{3,2},{4,5},{5,4},{6,7},{7,6},{8,9},{9,8},{10,11... | collective-permute-start | bytes 248840 | tf_op jit(solution)/shard_map/ppermute | solution.py:365
  75.2 5.5 %collective-permute-start.15 = (bf16[144,144]{1,0:T(8,128)(2,1)S(1)}, bf16[144,144]{1,0:T(8,128)(2,1)S(1)}, u32[]{:S(2)}, u32[]{:S(2)}) collective-permute-start(bf16[144,144]{1,0:T(8,128)(2,1)S(1)} %add_convert_fusion.1), channel_id=1, source_target_pairs={{0,6},{1,7},{2,4},{3,5},{4,2},{5,3},{6,0},{7,1},{8,14},{9,15},{10,... | collective-permute-start | bytes 124424 | tf_op jit(solution)/shard_map/ppermute | solution.py:365
  77.7 4.7 %collective-permute-start.14 = (bf16[144,144]{1,0:T(8,128)(2,1)S(1)}, bf16[144,144]{1,0:T(8,128)(2,1)S(1)}, u32[]{:S(2)}, u32[]{:S(2)}) collective-permute-start(bf16[144,144]{1,0:T(8,128)(2,1)S(1)} %add_convert_fusion.1), channel_id=1, source_target_pairs={{0,4},{1,5},{2,6},{3,7},{4,0},{5,1},{6,2},{7,3},{8,12},{9,13},{10,... | collective-permute-start | bytes 124424 | tf_op jit(solution)/shard_map/ppermute | solution.py:365
  78.0 4.4 %collective-permute-start.13 = (bf16[144,144]{1,0:T(8,128)(2,1)S(1)}, bf16[144,144]{1,0:T(8,128)(2,1)S(1)}, u32[]{:S(2)}, u32[]{:S(2)}) collective-permute-start(bf16[144,144]{1,0:T(8,128)(2,1)S(1)} %add_convert_fusion.1), channel_id=1, source_target_pairs={{0,2},{1,3},{2,0},{3,1},{4,6},{5,7},{6,4},{7,5},{8,10},{9,11},{10,... | collective-permute-start | bytes 124424 | tf_op jit(solution)/shard_map/ppermute | solution.py:365
  82.4 10.4 %copy-start.1 = (bf16[144,144]{1,0:T(8,128)(2,1)}, bf16[144,144]{1,0:T(8,128)(2,1)S(1)}, u32[]{:S(2)}) copy-start(bf16[144,144]{1,0:T(8,128)(2,1)S(1)} %add_convert_fusion.refs_0_) | copy-start | bytes 124420
  82.4 10.4 %collective-permute-start.18 = (bf16[144,144]{1,0:T(8,128)(2,1)S(1)}, bf16[144,144]{1,0:T(8,128)(2,1)S(1)}, u32[]{:S(2)}, u32[]{:S(2)}) collective-permute-start(bf16[144,144]{1,0:T(8,128)(2,1)S(1)} %add_convert_fusion.refs_0_), channel_id=1, source_target_pairs={{0,24},{1,25},{2,26},{3,27},{4,28},{5,29},{6,30},{7,31},{8,16},{9,... | collective-permute-start | bytes 124424 | tf_op jit(solution)/shard_map/ppermute | solution.py:365
  88.1 6.3 %collective-permute-start.17 = (bf16[144,144]{1,0:T(8,128)(2,1)S(1)}, bf16[144,144]{1,0:T(8,128)(2,1)S(1)}, u32[]{:S(2)}, u32[]{:S(2)}) collective-permute-start(bf16[144,144]{1,0:T(8,128)(2,1)S(1)} %add_convert_fusion.refs_0_), channel_id=1, source_target_pairs={{0,16},{1,17},{2,18},{3,19},{4,20},{5,21},{6,22},{7,23},{8,24},{9,... | collective-permute-start | bytes 124424 | tf_op jit(solution)/shard_map/ppermute | solution.py:365
  88.1 6.3 %collective-permute-start.16 = (bf16[144,144]{1,0:T(8,128)(2,1)S(1)}, bf16[144,144]{1,0:T(8,128)(2,1)S(1)}, u32[]{:S(2)}, u32[]{:S(2)}) collective-permute-start(bf16[144,144]{1,0:T(8,128)(2,1)S(1)} %add_convert_fusion.refs_0_), channel_id=1, source_target_pairs={{0,8},{1,9},{2,10},{3,11},{4,12},{5,13},{6,14},{7,15},{8,0},{9,1},... | collective-permute-start | bytes 124424 | tf_op jit(solution)/shard_map/ppermute | solution.py:365
  92.8 1.5 %copy-start.3 = (bf16[144,144]{1,0:T(8,128)(2,1)}, bf16[144,144]{1,0:T(8,128)(2,1)S(1)}, u32[]{:S(2)}) copy-start(bf16[144,144]{1,0:T(8,128)(2,1)S(1)} %collective-permute-done.18.refs_3_) | copy-start | bytes 124420
  (5 other events, 3.1 us)
where the time goes:
time: 100 us; the launch traced here: 99.5 us
  starting transfers between devices  46.4 us (46%)
  Pallas kernels  30.3 us (30%)
  local copies, waits for them, and re-layouts  11 us (11%)
  waiting for transfers between devices  9.3 us (9%)
  other arithmetic  1.63 us (2%)
    ppermute x12, starting transfers between devices, shift_axis(): return lax.ppermute(value, axis, pairs)  32.7 us
    pallas_call x9, Pallas kernels, call(): pl.pallas_call(body, out_shape=outs, in_specs=specs, out_specs=[pl.BlockS...  30.3 us
    ppermute x7, starting transfers between devices, swap_bits(): lax.ppermute(value, ('gx', 'gy'), [(i, i ^ flip) for i in range(count)])  13.7 us
    unnamed x38, local copies, waits for them, and re-layouts  8.5 us
    ppermute x7, waiting for transfers between devices, swap_bits(): lax.ppermute(value, ('gx', 'gy'), [(i, i ^ flip) for i in range(count)])  5.7 us
    ppermute x12, waiting for transfers between devices, shift_axis(): return lax.ppermute(value, axis, pairs)  3.6 us
  transfers between devices with their start and end apart: 19, of which 7 were waited for; matrix products, arithmetic and copies ran while one was open for 3% of the time, Pallas kernels for 21%

commit v1 on v0

v1 whole, which is shorter than its diff:
```python
import functools

import jax
import jax.numpy as jnp
from jax import lax
from jax.experimental import pallas as pl
from jax.experimental.pallas import tpu as pltpu
from jax.sharding import PartitionSpec as P

F32 = jnp.float32
BF16 = jnp.bfloat16


def mm(left, right):
    return jnp.dot(left, right, preferred_element_type=F32)


def mm_t(left, right):
    return lax.dot_general(left, right, (((1,), (1,)), ((), ())), preferred_element_type=F32)


def one_hot(shape, rule):
    rows = lax.broadcasted_iota(jnp.int32, shape, 0)
    cols = lax.broadcasted_iota(jnp.int32, shape, 1)
    return jnp.where(rule(rows, cols), 1.0, 0.0).astype(BF16)


def swap_matrix(outer, inner):
    count = outer * inner
    return one_hot((count, count), lambda r, c: c == (r % inner) * outer + r // inner)


def moved(values, width, offset):
    lanes = values.shape[1]
    place = lax.broadcasted_iota(jnp.int32, values.shape, 1) % width
    if offset == 1:
        return jnp.where(place == 0, 0.0, pltpu.roll(values, 1, 1))
    return jnp.where(place == width - 1, 0.0, pltpu.roll(values, lanes - 1, 1))


def combine(parts, width):
    rows = parts.shape[0] // 3
    return (
        parts[rows : 2 * rows]
        + moved(parts[:rows], width, 1)
        + moved(parts[2 * rows :], width, -1)
    )


def to_rows(values):
    chans, rows, width = values.shape
    return values.astype(F32).reshape(chans * rows, width).astype(BF16)


def band(taps_ref, out_ref, out_rows, turned, flipped):
    m, n = taps_ref.shape[1:][::-1] if turned else taps_ref.shape[1:]
    wide = (out_rows + 2) * n
    spread = one_hot((n, wide), lambda r, c: c % n == r)
    block = lax.broadcasted_iota(jnp.int32, (m, wide), 1) // n
    if turned:
        tiled = [
            lax.dot_general(
                taps_ref[at], spread, (((0,), (0,)), ((), ())), preferred_element_type=F32
            )
            for at in range(27)
        ]
    else:
        every = mm(taps_ref[...].reshape(27 * m, n), spread)
        tiled = [every[at * m : (at + 1) * m] for at in range(27)]
    if flipped:
        tiled = tiled[::-1]
    for a in range(3):
        for c in range(3):
            taps = [tiled[(a * 3 + b) * 3 + c] for b in range(3)]
            for y in range(out_rows):
                value = jnp.where(
                    block == y,
                    taps[0],
                    jnp.where(block == y + 1, taps[1], jnp.where(block == y + 2, taps[2], 0.0)),
                )
                start = (c * out_rows + y) * m
                out_ref[a, start : start + m, :] = value.astype(BF16)


def weights_kernel(kf, kc, wa, wt, wc, wct, *, ny):
    band(kf, wa, ny + 2, False, False)
    band(kf, wt, ny, True, True)
    band(kc, wc, ny // 2 + 4, True, False)
    band(kc, wct, ny // 2 + 2, False, True)


def ends():
    out = []
    for axis in ("gx", "gy"):
        at = lax.axis_index(axis)
        out.append((at % 2 == 0, at == 0, at == lax.axis_size(axis) - 1))
    return out


def volume_rows_kernel(vol, own, even, odd):
    c1, nz, ny, nx = vol.shape
    swap = swap_matrix(ny, c1)
    for z in range(nz):
        own[:, z * nx : (z + 1) * nx] = mm(swap, to_rows(vol[:, z])).astype(BF16)
    low, high = own[:, : even.shape[1]], own[:, own.shape[1] - even.shape[1] :]
    first = ends()[0][0]
    even[...] = jnp.where(first, high, low)
    odd[...] = jnp.where(first, low, high)


def cot_rows_kernel(fc, cc, fine, coarse, even, odd):
    c1, nz, ny, nx = fc.shape
    c2, cells, half = cc.shape
    hy = ny // 2
    swap = swap_matrix(ny, c1)
    for z in range(nz):
        fine[:, z * nx : (z + 1) * nx] = mm(swap, to_rows(fc[:, z])).astype(BF16)
    rows = mm(swap_matrix(cells, c2), to_rows(cc[...])).astype(BF16)
    for z in range(cells // hy):
        coarse[:, z * half : (z + 1) * half] = rows[z * hy * c2 : (z + 1) * hy * c2]
    first = ends()[0][0]
    low, high = fine[:, :nx], fine[:, (nz - 1) * nx :]
    even[:, :nx] = jnp.where(first, high, low)
    odd[:, :nx] = jnp.where(first, low, high)
    even[:, nx:] = coarse[...]
    odd[:, nx:] = coarse[...]


def stack_layers(out, own, even, odd, lanes):
    first = ends()[0][0]
    width = lanes.stop - lanes.start
    low, high = even[:, lanes], odd[:, lanes]
    out[:, :width] = jnp.where(first, high, low)
    out[:, width : width + own.shape[1]] = own[...]
    out[:, width + own.shape[1] :] = jnp.where(first, low, high)


def volume_layers_kernel(own, z_even, z_odd, out, even, odd):
    stack_layers(out, own, z_even, z_odd, slice(0, z_even.shape[1]))
    edge = even.shape[0]
    first = ends()[1][0]
    low, high = out[:edge], out[out.shape[0] - edge :]
    even[...] = jnp.where(first, high, low)
    odd[...] = jnp.where(first, low, high)


def coarse_layers_kernel(po, pz_even, pz_odd, fo, co, cz_even, cz_odd, p_out, f_out, c_out, even, odd):
    nx = cz_even.shape[1] - co.shape[1]
    stack_layers(p_out, po, pz_even, pz_odd, slice(0, pz_even.shape[1]))
    stack_layers(f_out, fo, cz_even, cz_odd, slice(0, nx))
    stack_layers(c_out, co, cz_even, cz_odd, slice(nx, cz_even.shape[1]))
    three = even.shape[0]
    c1 = three // 3
    pooled, wide = p_out.shape[1], c_out.shape[1]
    first = ends()[1][0]

    def put(rows, lanes, low, high):
        even[rows, lanes] = jnp.where(first, high, low)
        odd[rows, lanes] = jnp.where(first, low, high)

    def tail(ref, count):
        return slice(ref.shape[0] - count, ref.shape[0])

    put(slice(0, three), slice(0, pooled), p_out[:three], p_out[tail(p_out, three)])
    near = slice(pooled, pooled + wide)
    far = slice(pooled + wide, pooled + 2 * wide)
    low, high = c_out[: 4 * c1], c_out[tail(c_out, 4 * c1)]
    put(slice(0, three), near, low[:three], high[:three])
    put(slice(0, c1), far, low[three:], high[three:])
    low, high = f_out[:c1], f_out[tail(f_out, c1)]
    put(slice(c1, 2 * c1), far, low[:, :wide], high[:, :wide])
    put(slice(2 * c1, three), far, low[:, wide:], high[:, wide:])


def weight_rows(w_ref, dz, first, count):
    rows = w_ref.shape[1] // 3
    return jnp.concatenate(
        [w_ref[dz, c * rows + first : c * rows + first + count] for c in range(3)], axis=0
    )


def fine_kernel_fn(xo, y_even, y_odd, wa, x_ref, pre_out, fo_out, pz_even, pz_odd, pz_own, *, c1, nz, ny, nx):
    (first_x, start_x, stop_x), (first_y, _, _) = ends()
    low, high = y_even[...], y_odd[...]
    x_ref[: 2 * c1] = jnp.where(first_y, high, low)
    x_ref[2 * c1 : 2 * c1 + c1 * ny] = xo[...]
    x_ref[2 * c1 + c1 * ny :] = jnp.where(first_y, low, high)
    pool = one_hot((nx, nx // 2), lambda r, c: r // 2 == c)
    cells = []
    sums = None
    weights = [weight_rows(wa, dz, c1, c1 * ny) for dz in range(3)]
    for layer in range(nz + 4):
        parts = None
        for dz in range(3):
            term = mm(weights[dz], x_ref[:, (layer + dz) * nx : (layer + dz + 1) * nx])
            parts = term if parts is None else parts + term
        pre = combine(parts, nx)
        sig = jax.nn.sigmoid(pre)
        span = slice((layer + 1) * nx, (layer + 2) * nx)
        fo = (xo[:, span].astype(F32) + pre * sig).astype(BF16)
        if 1 <= layer <= nz + 2:
            pre_out[:, (layer - 1) * nx : layer * nx] = pre
        if 2 <= layer < nz + 2:
            fo_out[:, (layer - 2) * nx : (layer - 1) * nx] = fo
        pooled = mm(fo, pool)
        if layer % 2 == 0:
            sums = pooled
            continue
        sums = sums + pooled
        rows = [
            sums[2 * r * c1 : (2 * r + 1) * c1] + sums[(2 * r + 1) * c1 : (2 * r + 2) * c1]
            for r in range(ny // 2)
        ]
        value = jnp.concatenate(rows, axis=0) * 0.125
        place = layer // 2
        last = nz // 2 + 1
        if place == 0:
            value = jnp.where(start_x, 0.0, value)
        if place == last:
            value = jnp.where(stop_x, 0.0, value)
        cells.append(value.astype(BF16))
    pz_own[...] = jnp.concatenate(cells[1:-1], axis=1)
    low, high = jnp.concatenate(cells[1:], axis=1), jnp.concatenate(cells[:-1], axis=1)
    pz_even[...] = jnp.where(first_x, high, low)
    pz_odd[...] = jnp.where(first_x, low, high)


def slope_kernel_fn(x_ref, wa, pre_ref, fo, fo_out, sl_out, *, c1, nz, ny, nx):
    swap_back = swap_matrix(c1, ny)
    low = [weight_rows(wa, dz, 0, c1) for dz in range(3)]
    high = [weight_rows(wa, dz, c1 + c1 * ny, c1) for dz in range(3)]
    for layer in range(nz + 2):
        edges = []
        for weights in (low, high):
            parts = None
            for dz in range(3):
                term = mm(weights[dz], x_ref[:, (layer + 1 + dz) * nx : (layer + 2 + dz) * nx])
                parts = term if parts is None else parts + term
            edges.append(combine(parts, nx))
        span = slice(layer * nx, (layer + 1) * nx)
        pre = jnp.concatenate([edges[0], pre_ref[:, span], edges[1]], axis=0)
        sig = jax.nn.sigmoid(pre)
        sl_out[:, span] = sig * (1.0 + pre * (1.0 - sig))
    for layer in range(nz):
        rows = mm(swap_back, fo[:, layer * nx : (layer + 1) * nx])
        fo_out[:, layer] = rows.reshape(c1, ny, nx).astype(BF16)


def coarse_kernel_fn(
    po, fc, cc, y_even, y_odd, sl, x_ref, wc, wct,
    co_out, fs_out, fg_out, g_out, p_ref, cs_ref, edge_ref, *, c1, c2, nz, ny, nx,
):
    half, hz, hy = nx // 2, nz // 2, ny // 2
    three = 3 * c1
    (_, start_x, stop_x), (first_y, start_y, stop_y) = ends()
    low, high = y_even[...], y_odd[...]
    edge_ref[0] = jnp.where(first_y, high, low)
    edge_ref[1] = jnp.where(first_y, low, high)
    pooled, wide = po.shape[1], cc.shape[1]
    p_ref[:three] = edge_ref[0, :, :pooled]
    p_ref[three : three + hy * c1] = po[...]
    p_ref[three + hy * c1 :] = edge_ref[1, :, :pooled]
    edge = 2 * c2
    swap_c = swap_matrix(c2, hz * hy)
    for pair in range((hz + 4) // 2):
        parts = None
        for dz in range(3):
            first = (2 * pair + dz) * half
            term = mm(wc[dz], p_ref[:, first : first + nx])
            parts = term if parts is None else parts + term
        pre = combine(parts, half)
        sig = jax.nn.sigmoid(pre)
        span = slice(pair * nx, (pair + 1) * nx)
        near = slice(pooled + pair * nx, pooled + (pair + 1) * nx)
        far = slice(pooled + wide + pair * nx, pooled + wide + (pair + 1) * nx)
        cot = jnp.concatenate(
            [
                edge_ref[0, :, near],
                edge_ref[0, :c1, far],
                cc[:, span],
                edge_ref[1, :, near],
                edge_ref[1, :c1, far],
            ],
            axis=0,
        )
        cs_ref[:, span] = (cot.astype(F32) * (sig * (1.0 + pre * (1.0 - sig)))).astype(BF16)
        if pair == 1:
            inner = slice(edge, edge + hy * c2)
            out = (pre[inner] * sig[inner]).astype(BF16)
            stacked = jnp.concatenate([out[:, :half], out[:, half:]], axis=0)
            co_out[...] = mm(swap_c, stacked).astype(BF16)
    widen = one_hot((half, nx), lambda r, c: c // 2 == r)
    base = pooled + wide
    for pair in range((hz + 2) // 2):
        parts = None
        for dz in range(3):
            first = (2 * pair + dz) * half
            term = mm(wct[dz], cs_ref[:, first : first + nx])
            parts = term if parts is None else parts + term
        grad = combine(parts, half) * 0.125
        high = grad.astype(BF16)
        low = (grad - high.astype(F32)).astype(BF16)
        for side in range(2):
            lanes = slice(side * half, (side + 1) * half)
            up = mm(high[:, lanes], widen) + mm(low[:, lanes], widen)
            blocks = [up[(y + 2) // 2 * c1 : (y + 2) // 2 * c1 + c1] for y in range(-1, ny + 1)]
            spread = jnp.concatenate(blocks, axis=0)
            coarse_layer = 2 * pair + side - 1
            for layer in (2 * coarse_layer, 2 * coarse_layer + 1):
                if not -1 <= layer <= nz:
                    continue
                place = layer + 1
                span = slice(place * nx, (place + 1) * nx)
                fold = place * nx // wide
                first = base + place * nx - fold * wide
                inside = slice(first, first + nx)
                rows = slice((fold + 1) * c1, (fold + 2) * c1)
                cot = jnp.concatenate(
                    [edge_ref[0, rows, inside], fc[:, span], edge_ref[1, rows, inside]], axis=0
                )
                total = cot.astype(F32) + spread
                slope = total * sl[:, span]
                row = lax.broadcasted_iota(jnp.int32, slope.shape, 0) // c1
                outside = jnp.logical_and(row == 0, start_y)
                outside = jnp.logical_or(outside, jnp.logical_and(row == ny + 1, stop_y))
                if layer == -1:
                    outside = jnp.logical_or(outside, start_x)
                if layer == nz:
                    outside = jnp.logical_or(outside, stop_x)
                fs_out[:, span] = jnp.where(outside, 0.0, slope).astype(BF16)
                if 0 <= layer < nz:
                    fg_out[:, layer * nx : (layer + 1) * nx] = total[c1 : c1 + c1 * ny]
    slopes = fs_out[c1 : c1 + c1 * ny, nx : (nz + 1) * nx].astype(F32)
    shifted = [
        moved(slopes, nx, -1).astype(BF16), slopes.astype(BF16), moved(slopes, nx, 1).astype(BF16)
    ]
    fine = None
    for y in range(ny):
        left = jnp.concatenate([s[y * c1 : (y + 1) * c1] for s in shifted], axis=0)
        right = [
            x_ref[(y + 1) * c1 : (y + 4) * c1, (a + 2) * nx : (a + 2 + nz) * nx] for a in range(3)
        ]
        term = mm_t(left, jnp.concatenate(right, axis=0))
        fine = term if fine is None else fine + term
    slopes = cs_ref[edge : edge + hy * c2, 2 * half : (2 + hz) * half].astype(F32)
    shifted = [
        moved(slopes, half, -1).astype(BF16),
        slopes.astype(BF16),
        moved(slopes, half, 1).astype(BF16),
    ]
    coarse = None
    for y in range(hy):
        left = jnp.concatenate([s[y * c2 : (y + 1) * c2] for s in shifted], axis=0)
        right = [
            p_ref[(y + 2) * c1 : (y + 5) * c1, (a + 2) * half : (a + 2 + hz) * half]
            for a in range(3)
        ]
        term = mm_t(left, jnp.concatenate(right, axis=0))
        coarse = term if coarse is None else coarse + term
    g_out[:three, :] = fine[:, : 8 * c1]
    g_out[three : 9 * c1, :] = coarse[:, : 8 * c1]
    last = [fine[:, 8 * c1 :], coarse[:, 8 * c1 :]]
    last = jnp.concatenate(last, axis=0)
    groups = [last[r * c1 : (r + 1) * c1] for r in range(9)]
    g_out[9 * c1 : 10 * c1, :] = jnp.concatenate(groups[:8], axis=1)
    g_out[10 * c1 :, :] = jnp.concatenate([groups[8]] * 8, axis=1)


def volume_grad_kernel(fs, fg, wt, out, *, c1, nz, ny, nx):
    swap_back = swap_matrix(c1, ny)
    for layer in range(nz):
        parts = None
        for dz in range(3):
            term = mm(wt[dz], fs[:, (layer + dz) * nx : (layer + dz + 1) * nx])
            parts = term if parts is None else parts + term
        total = fg[:, layer * nx : (layer + 1) * nx] + combine(parts, nx)
        out[:, layer] = mm(swap_back, total.astype(BF16)).reshape(c1, ny, nx).astype(BF16)


def finish_kernel(*refs, c1, c2, scale_fine, scale_coarse):
    parts, (fine, coarse) = refs[:-2], refs[-2:]
    total = tree_sum([part[...].astype(F32) for part in parts])
    tail = total[9 * c1 :]
    groups = [tail[:c1, r * c1 : (r + 1) * c1] for r in range(8)] + [tail[c1:, :c1]]
    last = jnp.concatenate(groups, axis=0)
    for c in range(3):
        own = slice(c * c1, (c + 1) * c1)
        for ab in range(8):
            fine[ab * 3 + c] = total[own, ab * c1 : (ab + 1) * c1] * scale_fine
        fine[24 + c] = last[own] * scale_fine
    for part, taps in ((total[3 * c1 : 9 * c1], 8), (last[3 * c1 :], 1)):
        turned = part.T * scale_coarse
        for ab in range(taps):
            for c in range(3):
                at = (8 if taps == 1 else ab) * 3 + c
                coarse[at] = turned[ab * c1 : (ab + 1) * c1, c * c2 : (c + 1) * c2]


def tree_sum(values):
    while len(values) > 1:
        values = [values[i] + values[i + 1] for i in range(0, len(values), 2)]
    return values[0]


def shapes(*pairs):
    return [pltpu.VMEM(shape, kind) for shape, kind in pairs]


def result(shape, kind):
    return jax.ShapeDtypeStruct(shape, kind)


def call(body, outs, args, flops=0, scratch=(), name=None):
    specs = [pl.BlockSpec(memory_space=pltpu.VMEM) for _ in args]
    nbytes = sum(a.size * a.dtype.itemsize for a in args)
    placed = [pltpu.with_memory_space_constraint(arg, pltpu.VMEM) for arg in args]
    return pl.pallas_call(
        body,
        out_shape=outs,
        in_specs=specs,
        out_specs=[pl.BlockSpec(memory_space=pltpu.VMEM) for _ in outs],
        scratch_shapes=list(scratch),
        compiler_params=pltpu.CompilerParams(vmem_limit_bytes=24 * 2**20),
        cost_estimate=pl.CostEstimate(flops=flops, bytes_accessed=nbytes, transcendentals=0),
        name=name,
    )(*placed)


def swap_pairs(even, odd, axis):
    count = lax.axis_size(axis)
    out = []
    for value, first in ((even, 0), (odd, 1)):
        pairs = [(i, i + 1) for i in range(first, count - 1, 2)]
        pairs += [(target, source) for source, target in pairs]
        out.append(lax.ppermute(value, axis, pairs))
    return out


def swap_bits(value, bits):
    ny = lax.axis_size("gy")
    count = lax.axis_size("gx") * ny
    flip = sum((bit if axis == "gy" else bit * ny) for axis, bit in bits)
    return lax.ppermute(value, ("gx", "gy"), [(i, i ^ flip) for i in range(count)])


def local(volume, fine_kernel, coarse_kernel, fine_cotangent, coarse_cotangent):
    c1, nz, ny, nx = volume.shape
    c2 = coarse_cotangent.shape[0]
    hz, hy, half = nz // 2, ny // 2, nx // 2
    gx, gy = lax.axis_size("gx"), lax.axis_size("gy")
    cells = nz * gx * ny * gy * nx
    sizes = dict(c1=c1, nz=nz, ny=ny, nx=nx)
    depth = 3
    rows, half_rows = ny * c1, hy * c1

    own, z_even, z_odd = call(
        volume_rows_kernel,
        shapes(((rows, nz * nx), BF16), ((rows, depth * nx), BF16), ((rows, depth * nx), BF16)),
        [volume],
        flops=10**8,
        name="volume_rows",
    )
    z_even, z_odd = swap_pairs(z_even, z_odd, "gx")
    wa, wt, wc, wct = call(
        functools.partial(weights_kernel, ny=ny),
        shapes(
            ((3, 3 * (ny + 2) * c1, (ny + 4) * c1), BF16),
            ((3, 3 * ny * c1, (ny + 2) * c1), BF16),
            ((3, 3 * (hy + 4) * c2, (hy + 6) * c1), BF16),
            ((3, 3 * (hy + 2) * c1, (hy + 4) * c2), BF16),
        ),
        [
            fine_kernel.reshape(27, c1, c1),
            coarse_kernel.swapaxes(3, 4).reshape(27, c1, c2),
        ],
        flops=10**9,
        name="weights",
    )
    fine_cot, coarse_cot, cz_even, cz_odd = call(
        cot_rows_kernel,
        shapes(
            ((rows, nz * nx), BF16),
            ((hy * c2, hz * half), BF16),
            ((rows, nx + hz * half), BF16),
            ((rows, nx + hz * half), BF16),
        ),
        [fine_cotangent, coarse_cotangent.reshape(c2, hz * hy, half)],
        flops=10**8,
        name="cot_rows",
    )

    layers = (nz + 2 * depth) * nx
    own, y_even, y_odd = call(
        volume_layers_kernel,
        shapes(((rows, layers), BF16), ((2 * c1, layers), BF16), ((2 * c1, layers), BF16)),
        [own, z_even, z_odd],
        flops=10**8,
        name="volume_layers",
    )
    y_even, y_odd = swap_pairs(y_even, y_odd, "gy")
    cz_even, cz_odd = swap_pairs(cz_even, cz_odd, "gx")

    volume_rows, pre, fine_rows, pz_even, pz_odd, pz_own = call(
        functools.partial(fine_kernel_fn, **sizes),
        shapes(
            ((rows + 4 * c1, layers), BF16),
            ((rows, (nz + 2) * nx), F32),
            ((rows, nz * nx), BF16),
            ((half_rows, (hz + 1) * half), BF16),
            ((half_rows, (hz + 1) * half), BF16),
            ((half_rows, hz * half), BF16),
        ),
        [own, y_even, y_odd, wa],
        flops=3 * 10**9,
        name="fine",
    )
    pz_even, pz_odd = swap_pairs(pz_even, pz_odd, "gx")
    fine_out, slopes = call(
        functools.partial(slope_kernel_fn, **sizes),
        [result((c1, nz, ny, nx), BF16)] + shapes(((rows + 2 * c1, (nz + 2) * nx), F32)),
        [volume_rows, wa, pre, fine_rows],
        flops=2 * 10**9,
        name="slopes",
    )
    pooled_lanes = (3 * hz + 2) * half
    cot_lanes = 3 * hz * half
    sent = (3 * c1, pooled_lanes + 2 * cot_lanes)
    pooled, fine_cot, coarse_cot, y_even, y_odd = call(
        coarse_layers_kernel,
        shapes(
            ((half_rows, pooled_lanes), BF16),
            ((rows, (nz + 2) * nx), BF16),
            ((hy * c2, cot_lanes), BF16),
            (sent, BF16),
            (sent, BF16),
        ),
        [pz_own, pz_even, pz_odd, fine_cot, coarse_cot, cz_even, cz_odd],
        flops=10**8,
        name="coarse_layers",
    )
    y_even, y_odd = swap_pairs(y_even, y_odd, "gy")

    coarse_out, fslope, fgrad, terms = call(
        functools.partial(coarse_kernel_fn, c2=c2, **sizes),
        shapes(
            ((c2 * hz * hy, half), BF16),
            ((rows + 2 * c1, (nz + 2) * nx), BF16),
            ((rows, nz * nx), F32),
            ((11 * c1, 8 * c1), F32),
        ),
        [pooled, fine_cot, coarse_cot, y_even, y_odd, slopes, volume_rows, wc, wct],
        flops=4 * 10**9,
        scratch=[
            pltpu.VMEM(((hy + 6) * c1, pooled_lanes), BF16),
            pltpu.VMEM(((hy + 4) * c2, cot_lanes), BF16),
            pltpu.VMEM((2,) + sent, BF16),
        ],
        name="coarse",
    )

    bits = [("gy", 1 << n) for n in range(gy.bit_length() - 1)]
    bits += [("gx", 1 << n) for n in range(gx.bit_length() - 1)]
    first = len(bits) % 2
    rounds = [bits[:1]] * first
    rounds += [bits[n : n + 2] for n in range(first, len(bits), 2)]
    value = terms
    for index, group in enumerate(rounds):
        if index:
            value = value.astype(BF16)
        parts = [value] + [swap_bits(value, [bit]) for bit in group]
        if len(group) == 2:
            parts.append(swap_bits(value, group))
        if index + 1 < len(rounds):
            value = tree_sum([part.astype(F32) for part in parts])
    (volume_grad,) = call(
        functools.partial(volume_grad_kernel, **sizes),
        [result((c1, nz, ny, nx), BF16)],
        [fslope, fgrad, wt],
        flops=2 * 10**9,
        name="volume_grad",
    )
    fine_grad, coarse_grad = call(
        functools.partial(
            finish_kernel,
            c1=c1,
            c2=c2,
            scale_fine=cells ** (-0.5),
            scale_coarse=(cells // 8) ** (-0.5),
        ),
        [result((27, c1, c1), F32), result((27, c1, c2), F32)],
        parts,
        flops=10**7,
        name="finish",
    )
    return (
        fine_out,
        coarse_out.reshape(c2, hz, hy, half),
        volume_grad,
        fine_grad.reshape(fine_kernel.shape),
        coarse_grad.reshape(3, 3, 3, c1, c2).swapaxes(3, 4),
    )


def solution(mesh):
    split = P(None, "gx", "gy", None)
    return jax.shard_map(
        local,
        mesh=mesh,
        in_specs=(split, P(), P(), split, split),
        out_specs=(split, split, split, P(), P()),
        check_vma=False,
    )
```

time: 100 us -> 64.8 us (0.65)
  Pallas kernels: 30.3 us -> 13.3 us
  starting transfers between devices: 46.4 us -> 33.4 us
  local copies, waits for them, and re-layouts: 11 us -> 3.36 us
  waiting for transfers between devices: 9.3 us -> 13.6 us
  other arithmetic: 1.63 us -> 0.04 us
    ppermute x12 -> x10, starting transfers between devices: 32.7 us -> 14.8 us  [swap_pairs(): out.append(lax.ppermute(value, axis, pairs))]
    pallas_call x9 -> x10, Pallas kernels: 30.3 us -> 13.3 us  [call(): pl.pallas_call(body, out_shape=outs, in_specs=specs, out_specs=[pl.BlockS...]
    ppermute x12 -> x10, waiting for transfers between devices: 3.6 us -> 9.11 us  [swap_pairs(): out.append(lax.ppermute(value, axis, pairs))]
    unnamed x38 -> x11, local copies, waits for them, and re-layouts: 8.5 us -> 3.36 us
    ppermute x7, starting transfers between devices: 13.7 us -> 18.6 us  [swap_bits(): lax.ppermute(value, ('gx', 'gy'), [(i, i ^ flip) for i in range(count)])]
    ppermute x7, waiting for transfers between devices: 5.7 us -> 4.44 us  [swap_bits(): lax.ppermute(value, ('gx', 'gy'), [(i, i ^ flip) for i in range(count)])]
    slice x1 -> x0, local copies, waits for them, and re-layouts: 1.09 us -> none  [local(): vol_hi = shift_axis(volume[:, :depth], 'gx', -1)]
  transfers between devices with their start and end apart: 19 -> 17, of which waited for: 7 -> 6; matrix products, arithmetic and copies ran while one was open for 3% -> 1% of each run, Pallas kernels for 21% -> 12%
where the time goes in v1:
time: 64.8 us; the launch traced here: 64.5 us
  starting transfers between devices  33.4 us (52%)
  waiting for transfers between devices  13.6 us (21%)
  Pallas kernels  13.3 us (21%)
  local copies, waits for them, and re-layouts  3.36 us (5%)
  between operations  0.82 us (1%)
    ppermute x7, starting transfers between devices, swap_bits(): lax.ppermute(value, ('gx', 'gy'), [(i, i ^ flip) for i in range(count)])  18.6 us
    ppermute x10, starting transfers between devices, swap_pairs(): out.append(lax.ppermute(value, axis, pairs))  14.8 us
    pallas_call x10, Pallas kernels, call(): pl.pallas_call(body, out_shape=outs, in_specs=specs, out_specs=[pl.BlockS...  13.3 us
    ppermute x10, waiting for transfers between devices, swap_pairs(): out.append(lax.ppermute(value, axis, pairs))  9.11 us
    ppermute x7, waiting for transfers between devices, swap_bits(): lax.ppermute(value, ('gx', 'gy'), [(i, i ^ flip) for i in range(count)])  4.44 us
    unnamed x11, local copies, waits for them, and re-layouts  3.36 us
  transfers between devices with their start and end apart: 17, of which 6 were waited for; matrix products, arithmetic and copies ran while one was open for 1% of the time, Pallas kernels for 12%

profile of v1, /device:TPU:0, one launch (start us, length us, event | category | flops | bytes accessed | tf_op | source)
XLA Modules:
  0.0 64.5 jit_solution(6875169036907501248)
XLA Ops:
  0.6 0.9 %copy-done = bf16[16,4,8,256]{3,2,1,0:T(8,128)(2,1)S(1)} copy-done((bf16[16,4,8,256]{3,2,1,0:T(8,128)(2,1)S(1)}, bf16[16,4,8,256]{3,2,1,0:T(8,128)(2,1)}, u32[]{:S(2)}) %copy-start) | copy-done | bytes 262168
  1.6 0.2 volume_rows.1
  1.8 3.0 %collective-permute-start = (bf16[128,768]{1,0:T(8,128)(2,1)S(1)}, bf16[128,768]{1,0:T(8,128)(2,1)S(1)}, u32[]{:S(2)}, u32[]{:S(2)}) collective-permute-start(bf16[128,768]{1,0:T(8,128)(2,1)S(1)} %get-tuple-element.39), channel_id=1, source_target_pairs={{0,4},{8,12},{16,20},{24,28},{4,0},{12,8},{20,16},{28,24},{1,5},{9... | collective-permute-start | bytes 589832 | tf_op jit(solution)/shard_map/ppermute | solution.py:435
  4.8 0.7 %collective-permute-start.1 = (bf16[128,768]{1,0:T(8,128)(2,1)S(1)}, bf16[128,768]{1,0:T(8,128)(2,1)S(1)}, u32[]{:S(2)}, u32[]{:S(2)}) collective-permute-start(bf16[128,768]{1,0:T(8,128)(2,1)S(1)} %get-tuple-element.40), channel_id=1, source_target_pairs={{4,8},{12,16},{20,24},{8,4},{16,12},{24,20},{5,9},{13,17},{21,25},... | collective-permute-start | bytes 589832 | tf_op jit(solution)/shard_map/ppermute | solution.py:435
  5.5 7.7 %collective-permute-done.z_even = bf16[128,768]{1,0:T(8,128)(2,1)S(1)} collective-permute-done((bf16[128,768]{1,0:T(8,128)(2,1)S(1)}, bf16[128,768]{1,0:T(8,128)(2,1)S(1)}, u32[]{:S(2)}, u32[]{:S(2)}) %collective-permute-start) | collective-permute-done | bytes 196640 | tf_op jit(solution)/shard_map/ppermute | solution.py:435
  13.4 0.7 %collective-permute-start.3 = (bf16[32,2560]{1,0:T(8,128)(2,1)S(1)}, bf16[32,2560]{1,0:T(8,128)(2,1)S(1)}, u32[]{:S(2)}, u32[]{:S(2)}) collective-permute-start(bf16[32,2560]{1,0:T(8,128)(2,1)S(1)} %get-tuple-element.43), channel_id=1, source_target_pairs={{1,2},{2,1},{5,6},{6,5},{9,10},{10,9},{13,14},{14,13},{17,18},{18,... | collective-permute-start | bytes 491528 | tf_op jit(solution)/shard_map/ppermute | solution.py:435
  14.1 0.9 %copy-done.1 = bf16[16,4,8,256]{3,2,1,0:T(8,128)(2,1)S(1)} copy-done((bf16[16,4,8,256]{3,2,1,0:T(8,128)(2,1)S(1)}, bf16[16,4,8,256]{3,2,1,0:T(8,128)(2,1)}, u32[]{:S(2)}) %copy-start.1) | copy-done | bytes 262168
  15.0 0.8 %copy-done.4 = bf16[32,2,4,128]{3,2,1,0:T(4,128)(2,1)S(1)} copy-done((bf16[32,2,4,128]{3,2,1,0:T(4,128)(2,1)S(1)}, bf16[32,2,4,128]{3,2,1,0:T(4,128)(2,1)}, u32[]{:S(2)}) %copy-start.4) | copy-done | bytes 65560
  15.9 0.3 cot_rows.1
  16.1 2.5 %collective-permute-start.6 = (bf16[128,512]{1,0:T(8,128)(2,1)S(1)}, bf16[128,512]{1,0:T(8,128)(2,1)S(1)}, u32[]{:S(2)}, u32[]{:S(2)}) collective-permute-start(bf16[128,512]{1,0:T(8,128)(2,1)S(1)} %get-tuple-element.54), channel_id=1, source_target_pairs={{0,4},{8,12},{16,20},{24,28},{4,0},{12,8},{20,16},{28,24},{1,5},{9... | collective-permute-start | bytes 393224 | tf_op jit(solution)/shard_map/ppermute | solution.py:435
  18.7 0.7 %collective-permute-start.7 = (bf16[128,512]{1,0:T(8,128)(2,1)S(1)}, bf16[128,512]{1,0:T(8,128)(2,1)S(1)}, u32[]{:S(2)}, u32[]{:S(2)}) collective-permute-start(bf16[128,512]{1,0:T(8,128)(2,1)S(1)} %get-tuple-element.55), channel_id=1, source_target_pairs={{4,8},{12,16},{20,24},{8,4},{16,12},{24,20},{5,9},{13,17},{21,25},... | collective-permute-start | bytes 393224 | tf_op jit(solution)/shard_map/ppermute | solution.py:435
  19.4 0.8 %weights.1 = (bf16[3,480,192]{2,1,0:T(8,128)(2,1)S(1)}, bf16[3,384,160]{2,1,0:T(8,128)(2,1)S(1)}, bf16[3,768,160]{2,1,0:T(8,128)(2,1)S(1)}, bf16[3,288,256]{2,1,0:T(8,128)(2,1)S(1)}) custom-call(bf16[27,16,16]{2,1,0:T(8,128)(2,1)S(1)} %bitcast.11, bf16[27,16,32]{2,1,0:T(8,128)(2,1)S(1)} %bitcast.12), custom_call_target="tpu_custom_call" | custom-call | flops 1000000000 | bytes 41472 | tf_op jit(solution)/shard_map/weights/pallas_call | solution.py:417
  20.2 2.4 %fine.1 = (bf16[192,2560]{1,0:T(8,128)(2,1)S(1)}, f32[128,1536]{1,0:T(8,128)S(1)}, bf16[128,1024]{1,0:T(8,128)(2,1)S(1)}, bf16[64,384]{1,0:T(8,128)(2,1)S(1)}, b...) custom-call(bf16[128,2560]{1,0:T(8,128)(2,1)S(1)} %get-tuple-element.41.xo, ...), custom_call_target="tpu_custom_call" | custom-call | flops 3000000000 | bytes 1536000 | tf_op jit(solution)/shard_map/fine/pallas_call | solution.py:417
  22.6 4.3 %collective-permute-start.4 = (bf16[64,384]{1,0:T(8,128)(2,1)S(1)}, bf16[64,384]{1,0:T(8,128)(2,1)S(1)}, u32[]{:S(2)}, u32[]{:S(2)}) collective-permute-start(bf16[64,384]{1,0:T(8,128)(2,1)S(1)} %get-tuple-element.50), channel_id=1, source_target_pairs={{0,4},{8,12},{16,20},{24,28},{4,0},{12,8},{20,16},{28,24},{1,5},{9... | collective-permute-start | bytes 147464 | tf_op jit(solution)/shard_map/ppermute | solution.py:435
  27.0 0.7 %collective-permute-start.5 = (bf16[64,384]{1,0:T(8,128)(2,1)S(1)}, bf16[64,384]{1,0:T(8,128)(2,1)S(1)}, u32[]{:S(2)}, u32[]{:S(2)}) collective-permute-start(bf16[64,384]{1,0:T(8,128)(2,1)S(1)} %get-tuple-element.51), channel_id=1, source_target_pairs={{4,8},{12,16},{20,24},{8,4},{16,12},{24,20},{5,9},{13,17},{21,25},... | collective-permute-start | bytes 147464 | tf_op jit(solution)/shard_map/ppermute | solution.py:435
  27.6 1.4 %collective-permute-done.4.pz_even = bf16[64,384]{1,0:T(8,128)(2,1)S(1)} collective-permute-done((bf16[64,384]{1,0:T(8,128)(2,1)S(1)}, bf16[64,384]{1,0:T(8,128)(2,1)S(1)}, u32[]{:S(2)}, u32[]{:S(2)}) %collective-permute-start.4) | collective-permute-done | bytes 49184 | tf_op jit(solution)/shard_map/ppermute | solution.py:435
  29.1 1.5 %collective-permute-start.8 = (bf16[48,2560]{1,0:T(8,128)(2,1)S(1)}, bf16[48,2560]{1,0:T(8,128)(2,1)S(1)}, u32[]{:S(2)}, u32[]{:S(2)}) collective-permute-start(bf16[48,2560]{1,0:T(8,128)(2,1)S(1)} %get-tuple-element.59), channel_id=1, source_target_pairs={{0,1},{2,3},{1,0},{3,2},{4,5},{6,7},{5,4},{7,6},{8,9},{10,11},{9,8... | collective-permute-start | bytes 737288 | tf_op jit(solution)/shard_map/ppermute | solution.py:435
  30.6 0.7 %collective-permute-start.9 = (bf16[48,2560]{1,0:T(8,128)(2,1)S(1)}, bf16[48,2560]{1,0:T(8,128)(2,1)S(1)}, u32[]{:S(2)}, u32[]{:S(2)}) collective-permute-start(bf16[48,2560]{1,0:T(8,128)(2,1)S(1)} %get-tuple-element.60), channel_id=1, source_target_pairs={{1,2},{2,1},{5,6},{6,5},{9,10},{10,9},{13,14},{14,13},{17,18},{18,... | collective-permute-start | bytes 737288 | tf_op jit(solution)/shard_map/ppermute | solution.py:435
  31.3 1.6 %slopes.1 = (bf16[16,4,8,256]{3,2,1,0:T(8,128)(2,1)}, f32[160,1536]{1,0:T(8,128)S(1)}) custom-call(bf16[192,2560]{1,0:T(8,128)(2,1)S(1)} %get-tuple-element.45.x_ref, bf16[3,480,192]{2,1,0:T(8,128)(2,1)S(1)} %get-tuple-element.44.wa, f32[128,1536]{1,0:T(8,128)S(1)} %get-tuple-element.46.pre_ref, bf16[128,1024]{1,0:T(8,128)(2,1)S(1)} %get-tuple-element.47.fo), custom_call_target="tpu_custom_call" | custom-call | flops 2000000000 | bytes 2584576 | tf_op jit(solution)/shard_map/slopes/pallas_call | solution.py:417
  32.9 4.1 %coarse.1 = (bf16[256,128]{1,0:T(8,128)(2,1)S(1)}, bf16[160,1536]{1,0:T(8,128)(2,1)S(1)}, f32[128,1024]{1,0:T(8,128)S(1)}, f32[176,128]{1,0:T(8,128)S(1)}) custom-call(bf16[64,1024]{1,0:T(8,128)(2,1)S(1)} %get-tuple-element.56.po, bf16[128,1536]{1,0:T(8,128)(2,1)S(1)} %get-tuple-element.57.fc, bf16[128,768]{1,0:T(8,128)(2,1)S(1)} %get-tuple-element.58.cc, ...), custom_call_target="tpu_custom_call" | custom-call | flops 4000000000 | bytes 4358144 | tf_op jit(solution)/shard_map/coarse/pallas_call | solution.py:417
  37.0 5.7 %collective-permute-start.10 = (f32[176,128]{1,0:T(8,128)S(1)}, f32[176,128]{1,0:T(8,128)S(1)}, u32[]{:S(2)}, u32[]{:S(2)}) collective-permute-start(f32[176,128]{1,0:T(8,128)S(1)} %get-tuple-element.68), channel_id=1, source_target_pairs={{0,1},{1,0},{2,3},{3,2},{4,5},{5,4},{6,7},{7,6},{8,9},{9,8},{10,11... | collective-permute-start | bytes 270344 | tf_op jit(solution)/shard_map/ppermute | solution.py:443
  42.7 0.9 %collective-permute-done.10 = f32[176,128]{1,0:T(8,128)S(1)} collective-permute-done((f32[176,128]{1,0:T(8,128)S(1)}, f32[176,128]{1,0:T(8,128)S(1)}, u32[]{:S(2)}, u32[]{:S(2)}) %collective-permute-start.10) | collective-permute-done | bytes 90144 | tf_op jit(solution)/shard_map/ppermute | solution.py:443
  43.7 6.3 %collective-permute-start.13 = (bf16[176,128]{1,0:T(8,128)(2,1)S(1)}, bf16[176,128]{1,0:T(8,128)(2,1)S(1)}, u32[]{:S(2)}, u32[]{:S(2)}) collective-permute-start(bf16[176,128]{1,0:T(8,128)(2,1)S(1)} %add_convert_fusion.1), channel_id=1, source_target_pairs={{0,6},{1,7},{2,4},{3,5},{4,2},{5,3},{6,0},{7,1},{8,14},{9,15},{10,... | collective-permute-start | bytes 135176 | tf_op jit(solution)/shard_map/ppermute | solution.py:443
  50.0 0.6 collective-permute-start.11
  50.6 1.4 %collective-permute-done.13 = bf16[176,128]{1,0:T(8,128)(2,1)S(1)} collective-permute-done((bf16[176,128]{1,0:T(8,128)(2,1)S(1)}, bf16[176,128]{1,0:T(8,128)(2,1)S(1)}, u32[]{:S(2)}, u32[]{:S(2)}) %collective-permute-start.13) | collective-permute-done | bytes 45088 | tf_op jit(solution)/shard_map/ppermute | solution.py:443
  52.0 2.0 %collective-permute-done.12 = bf16[176,128]{1,0:T(8,128)(2,1)S(1)} collective-permute-done((bf16[176,128]{1,0:T(8,128)(2,1)S(1)}, bf16[176,128]{1,0:T(8,128)(2,1)S(1)}, u32[]{:S(2)}, u32[]{:S(2)}) %collective-permute-start.12) | collective-permute-done | bytes 45088 | tf_op jit(solution)/shard_map/ppermute | solution.py:443
  54.1 3.5 %collective-permute-start.14 = (bf16[176,128]{1,0:T(8,128)(2,1)S(1)}, bf16[176,128]{1,0:T(8,128)(2,1)S(1)}, u32[]{:S(2)}, u32[]{:S(2)}) collective-permute-start(bf16[176,128]{1,0:T(8,128)(2,1)S(1)} %add_convert_fusion.refs_0_), channel_id=1, source_target_pairs={{0,8},{1,9},{2,10},{3,11},{4,12},{5,13},{6,14},{7,15},{8,0},{9,1},... | collective-permute-start | bytes 135176 | tf_op jit(solution)/shard_map/ppermute | solution.py:443
  57.6 2.4 %collective-permute-start.16 = (bf16[176,128]{1,0:T(8,128)(2,1)S(1)}, bf16[176,128]{1,0:T(8,128)(2,1)S(1)}, u32[]{:S(2)}, u32[]{:S(2)}) collective-permute-start(bf16[176,128]{1,0:T(8,128)(2,1)S(1)} %add_convert_fusion.refs_0_), channel_id=1, source_target_pairs={{0,24},{1,25},{2,26},{3,27},{4,28},{5,29},{6,30},{7,31},{8,16},{9,... | collective-permute-start | bytes 135176 | tf_op jit(solution)/shard_map/ppermute | solution.py:443
  60.0 2.7 %volume_grad.1 = bf16[16,4,8,256]{3,2,1,0:T(8,128)(2,1)} custom-call(bf16[160,1536]{1,0:T(8,128)(2,1)S(1)} %get-tuple-element.65.fs, f32[128,1024]{1,0:T(8,128)S(1)} %get-tuple-element.66.fg, bf16[3,384,160]{2,1,0:T(8,128)(2,1)S(1)} %get-tuple-element.67.wt), custom_call_target="tpu_custom_call" | custom-call | flops 2000000000 | bytes 1384448 | tf_op jit(solution)/shard_map/volume_grad/pallas_call | solution.py:417
  62.8 0.6 copy.10
  63.4 0.1 collective-permute-done.16.refs_3_
  63.5 1.0 %finish.1 = (f32[27,16,16]{2,1,0:T(8,128)}, f32[27,16,32]{2,1,0:T(8,128)}) custom-call(bf16[176,128]{1,0:T(8,128)(2,1)S(1)} %add_convert_fusion.refs_0_, bf16[176,128]{1,0:T(8,128)(2,1)S(1)} %collective-permute-done.14.refs_1_, bf16[176,128]{1,0:T(8,128)(2,1)S(1)} %collective-permute-done.15.refs_2_, bf16[176,128]{1,0:T(8,128)(2,1)S(1)} %collective-permute-done.16.refs_3_), custom_call_target="tpu_custom_call" | custom-call | flops 10000000 | bytes 180224 | tf_op jit(solution)/shard_map/finish/pallas_call | solution.py:417
  (25 shorter events, 0.4 us)
Async XLA Ops:
  0.6 1.0 %copy-start = (bf16[16,4,8,256]{3,2,1,0:T(8,128)(2,1)S(1)}, bf16[16,4,8,256]{3,2,1,0:T(8,128)(2,1)}, u32[]{:S(2)}) copy-start(bf16[16,4,8,256]{3,2,1,0:T(8,128)(2,1)} %vol.1) | copy-start | bytes 786436
  1.6 17.8 %copy-start.2 = (bf16[3,3,3,16,16]{4,3,2,1,0:T(8,128)(2,1)S(1)}, bf16[3,3,3,16,16]{4,3,2,1,0:T(8,128)(2,1)}, u32[]{:S(2)}) copy-start(bf16[3,3,3,16,16]{4,3,2,1,0:T(8,128)(2,1)} %param.6) | copy-start | bytes 41476
  1.6 17.8 %copy-start.3 = (bf16[3,3,3,32,16]{3,4,2,1,0:T(8,128)(2,1)S(1)}, bf16[3,3,3,32,16]{3,4,2,1,0:T(8,128)(2,1)}, u32[]{:S(2)}) copy-start(bf16[3,3,3,32,16]{3,4,2,1,0:T(8,128)(2,1)} %param.7) | copy-start | bytes 82948
  1.8 11.4 %collective-permute-start = (bf16[128,768]{1,0:T(8,128)(2,1)S(1)}, bf16[128,768]{1,0:T(8,128)(2,1)S(1)}, u32[]{:S(2)}, u32[]{:S(2)}) collective-permute-start(bf16[128,768]{1,0:T(8,128)(2,1)S(1)} %get-tuple-element.39), channel_id=1, source_target_pairs={{0,4},{8,12},{16,20},{24,28},{4,0},{12,8},{20,16},{28,24},{1,5},{9... | collective-permute-start | bytes 589832 | tf_op jit(solution)/shard_map/ppermute | solution.py:435
  4.8 8.4 %collective-permute-start.1 = (bf16[128,768]{1,0:T(8,128)(2,1)S(1)}, bf16[128,768]{1,0:T(8,128)(2,1)S(1)}, u32[]{:S(2)}, u32[]{:S(2)}) collective-permute-start(bf16[128,768]{1,0:T(8,128)(2,1)S(1)} %get-tuple-element.40), channel_id=1, source_target_pairs={{4,8},{12,16},{20,24},{8,4},{16,12},{24,20},{5,9},{13,17},{21,25},... | collective-permute-start | bytes 589832 | tf_op jit(solution)/shard_map/ppermute | solution.py:435
  13.3 6.9 %collective-permute-start.2 = (bf16[32,2560]{1,0:T(8,128)(2,1)S(1)}, bf16[32,2560]{1,0:T(8,128)(2,1)S(1)}, u32[]{:S(2)}, u32[]{:S(2)}) collective-permute-start(bf16[32,2560]{1,0:T(8,128)(2,1)S(1)} %get-tuple-element.42), channel_id=1, source_target_pairs={{0,1},{2,3},{1,0},{3,2},{4,5},{6,7},{5,4},{7,6},{8,9},{10,11},{9,8... | collective-permute-start | bytes 491528 | tf_op jit(solution)/shard_map/ppermute | solution.py:435
  13.4 6.8 %collective-permute-start.3 = (bf16[32,2560]{1,0:T(8,128)(2,1)S(1)}, bf16[32,2560]{1,0:T(8,128)(2,1)S(1)}, u32[]{:S(2)}, u32[]{:S(2)}) collective-permute-start(bf16[32,2560]{1,0:T(8,128)(2,1)S(1)} %get-tuple-element.43), channel_id=1, source_target_pairs={{1,2},{2,1},{5,6},{6,5},{9,10},{10,9},{13,14},{14,13},{17,18},{18,... | collective-permute-start | bytes 491528 | tf_op jit(solution)/shard_map/ppermute | solution.py:435
  14.1 1.0 %copy-start.1 = (bf16[16,4,8,256]{3,2,1,0:T(8,128)(2,1)S(1)}, bf16[16,4,8,256]{3,2,1,0:T(8,128)(2,1)}, u32[]{:S(2)}) copy-start(bf16[16,4,8,256]{3,2,1,0:T(8,128)(2,1)} %fc.1) | copy-start | bytes 786436
  15.0 0.8 %copy-start.4 = (bf16[32,2,4,128]{3,2,1,0:T(4,128)(2,1)S(1)}, bf16[32,2,4,128]{3,2,1,0:T(4,128)(2,1)}, u32[]{:S(2)}) copy-start(bf16[32,2,4,128]{3,2,1,0:T(4,128)(2,1)} %param.9) | copy-start | bytes 196612
  16.1 11.5 %collective-permute-start.6 = (bf16[128,512]{1,0:T(8,128)(2,1)S(1)}, bf16[128,512]{1,0:T(8,128)(2,1)S(1)}, u32[]{:S(2)}, u32[]{:S(2)}) collective-permute-start(bf16[128,512]{1,0:T(8,128)(2,1)S(1)} %get-tuple-element.54), channel_id=1, source_target_pairs={{0,4},{8,12},{16,20},{24,28},{4,0},{12,8},{20,16},{28,24},{1,5},{9... | collective-permute-start | bytes 393224 | tf_op jit(solution)/shard_map/ppermute | solution.py:435
  18.7 8.9 %collective-permute-start.7 = (bf16[128,512]{1,0:T(8,128)(2,1)S(1)}, bf16[128,512]{1,0:T(8,128)(2,1)S(1)}, u32[]{:S(2)}, u32[]{:S(2)}) collective-permute-start(bf16[128,512]{1,0:T(8,128)(2,1)S(1)} %get-tuple-element.55), channel_id=1, source_target_pairs={{4,8},{12,16},{20,24},{8,4},{16,12},{24,20},{5,9},{13,17},{21,25},... | collective-permute-start | bytes 393224 | tf_op jit(solution)/shard_map/ppermute | solution.py:435
  22.6 6.4 %collective-permute-start.4 = (bf16[64,384]{1,0:T(8,128)(2,1)S(1)}, bf16[64,384]{1,0:T(8,128)(2,1)S(1)}, u32[]{:S(2)}, u32[]{:S(2)}) collective-permute-start(bf16[64,384]{1,0:T(8,128)(2,1)S(1)} %get-tuple-element.50), channel_id=1, source_target_pairs={{0,4},{8,12},{16,20},{24,28},{4,0},{12,8},{20,16},{28,24},{1,5},{9... | collective-permute-start | bytes 147464 | tf_op jit(solution)/shard_map/ppermute | solution.py:435
  27.0 2.1 %collective-permute-start.5 = (bf16[64,384]{1,0:T(8,128)(2,1)S(1)}, bf16[64,384]{1,0:T(8,128)(2,1)S(1)}, u32[]{:S(2)}, u32[]{:S(2)}) collective-permute-start(bf16[64,384]{1,0:T(8,128)(2,1)S(1)} %get-tuple-element.51), channel_id=1, source_target_pairs={{4,8},{12,16},{20,24},{8,4},{16,12},{24,20},{5,9},{13,17},{21,25},... | collective-permute-start | bytes 147464 | tf_op jit(solution)/shard_map/ppermute | solution.py:435
  29.1 3.8 %collective-permute-start.8 = (bf16[48,2560]{1,0:T(8,128)(2,1)S(1)}, bf16[48,2560]{1,0:T(8,128)(2,1)S(1)}, u32[]{:S(2)}, u32[]{:S(2)}) collective-permute-start(bf16[48,2560]{1,0:T(8,128)(2,1)S(1)} %get-tuple-element.59), channel_id=1, source_target_pairs={{0,1},{2,3},{1,0},{3,2},{4,5},{6,7},{5,4},{7,6},{8,9},{10,11},{9,8... | collective-permute-start | bytes 737288 | tf_op jit(solution)/shard_map/ppermute | solution.py:435
  30.6 2.3 %collective-permute-start.9 = (bf16[48,2560]{1,0:T(8,128)(2,1)S(1)}, bf16[48,2560]{1,0:T(8,128)(2,1)S(1)}, u32[]{:S(2)}, u32[]{:S(2)}) collective-permute-start(bf16[48,2560]{1,0:T(8,128)(2,1)S(1)} %get-tuple-element.60), channel_id=1, source_target_pairs={{1,2},{2,1},{5,6},{6,5},{9,10},{10,9},{13,14},{14,13},{17,18},{18,... | collective-permute-start | bytes 737288 | tf_op jit(solution)/shard_map/ppermute | solution.py:435
  37.0 6.6 %collective-permute-start.10 = (f32[176,128]{1,0:T(8,128)S(1)}, f32[176,128]{1,0:T(8,128)S(1)}, u32[]{:S(2)}, u32[]{:S(2)}) collective-permute-start(f32[176,128]{1,0:T(8,128)S(1)} %get-tuple-element.68), channel_id=1, source_target_pairs={{0,1},{1,0},{2,3},{3,2},{4,5},{5,4},{6,7},{7,6},{8,9},{9,8},{10,11... | collective-permute-start | bytes 270344 | tf_op jit(solution)/shard_map/ppermute | solution.py:443
  43.7 8.3 %collective-permute-start.13 = (bf16[176,128]{1,0:T(8,128)(2,1)S(1)}, bf16[176,128]{1,0:T(8,128)(2,1)S(1)}, u32[]{:S(2)}, u32[]{:S(2)}) collective-permute-start(bf16[176,128]{1,0:T(8,128)(2,1)S(1)} %add_convert_fusion.1), channel_id=1, source_target_pairs={{0,6},{1,7},{2,4},{3,5},{4,2},{5,3},{6,0},{7,1},{8,14},{9,15},{10,... | collective-permute-start | bytes 135176 | tf_op jit(solution)/shard_map/ppermute | solution.py:443
  50.0 4.0 %collective-permute-start.12 = (bf16[176,128]{1,0:T(8,128)(2,1)S(1)}, bf16[176,128]{1,0:T(8,128)(2,1)S(1)}, u32[]{:S(2)}, u32[]{:S(2)}) collective-permute-start(bf16[176,128]{1,0:T(8,128)(2,1)S(1)} %add_convert_fusion.1), channel_id=1, source_target_pairs={{0,4},{1,5},{2,6},{3,7},{4,0},{5,1},{6,2},{7,3},{8,12},{9,13},{10,... | collective-permute-start | bytes 135176 | tf_op jit(solution)/shard_map/ppermute | solution.py:443
  50.0 4.0 %collective-permute-start.11 = (bf16[176,128]{1,0:T(8,128)(2,1)S(1)}, bf16[176,128]{1,0:T(8,128)(2,1)S(1)}, u32[]{:S(2)}, u32[]{:S(2)}) collective-permute-start(bf16[176,128]{1,0:T(8,128)(2,1)S(1)} %add_convert_fusion.1), channel_id=1, source_target_pairs={{0,2},{1,3},{2,0},{3,1},{4,6},{5,7},{6,4},{7,5},{8,10},{9,11},{10,... | collective-permute-start | bytes 135176 | tf_op jit(solution)/shard_map/ppermute | solution.py:443
  54.1 9.3 %collective-permute-start.14 = (bf16[176,128]{1,0:T(8,128)(2,1)S(1)}, bf16[176,128]{1,0:T(8,128)(2,1)S(1)}, u32[]{:S(2)}, u32[]{:S(2)}) collective-permute-start(bf16[176,128]{1,0:T(8,128)(2,1)S(1)} %add_convert_fusion.refs_0_), channel_id=1, source_target_pairs={{0,8},{1,9},{2,10},{3,11},{4,12},{5,13},{6,14},{7,15},{8,0},{9,1},... | collective-permute-start | bytes 135176 | tf_op jit(solution)/shard_map/ppermute | solution.py:443
  57.6 5.8 %collective-permute-start.15 = (bf16[176,128]{1,0:T(8,128)(2,1)S(1)}, bf16[176,128]{1,0:T(8,128)(2,1)S(1)}, u32[]{:S(2)}, u32[]{:S(2)}) collective-permute-start(bf16[176,128]{1,0:T(8,128)(2,1)S(1)} %add_convert_fusion.refs_0_), channel_id=1, source_target_pairs={{0,16},{1,17},{2,18},{3,19},{4,20},{5,21},{6,22},{7,23},{8,24},{9,... | collective-permute-start | bytes 135176 | tf_op jit(solution)/shard_map/ppermute | solution.py:443
  57.6 5.9 %collective-permute-start.16 = (bf16[176,128]{1,0:T(8,128)(2,1)S(1)}, bf16[176,128]{1,0:T(8,128)(2,1)S(1)}, u32[]{:S(2)}, u32[]{:S(2)}) collective-permute-start(bf16[176,128]{1,0:T(8,128)(2,1)S(1)} %add_convert_fusion.refs_0_), channel_id=1, source_target_pairs={{0,24},{1,25},{2,26},{3,27},{4,28},{5,29},{6,30},{7,31},{8,16},{9,... | collective-permute-start | bytes 135176 | tf_op jit(solution)/shard_map/ppermute | solution.py:443

commit v2 on v1

v2 whole, which is shorter than its diff:
```python
import functools

import jax
import jax.numpy as jnp
from jax import lax
from jax.experimental import pallas as pl
from jax.experimental.pallas import tpu as pltpu
from jax.sharding import PartitionSpec as P


F32 = jnp.float32
BF16 = jnp.bfloat16


def mm(left, right):
    return jnp.dot(left, right, preferred_element_type=F32)


def mm_t(left, right):
    return lax.dot_general(left, right, (((1,), (1,)), ((), ())), preferred_element_type=F32)


def one_hot(shape, rule):
    rows = lax.broadcasted_iota(jnp.int32, shape, 0)
    cols = lax.broadcasted_iota(jnp.int32, shape, 1)
    return jnp.where(rule(rows, cols), 1.0, 0.0).astype(BF16)


def swap_matrix(outer, inner):
    count = outer * inner
    return one_hot((count, count), lambda r, c: c == (r % inner) * outer + r // inner)


def moved(values, width, offset):
    lanes = values.shape[1]
    place = lax.broadcasted_iota(jnp.int32, values.shape, 1) % width
    if offset == 1:
        return jnp.where(place == 0, 0.0, pltpu.roll(values, 1, 1))
    return jnp.where(place == width - 1, 0.0, pltpu.roll(values, lanes - 1, 1))


def combine(parts, width):
    rows = parts.shape[0] // 3
    return (
        parts[rows : 2 * rows]
        + moved(parts[:rows], width, 1)
        + moved(parts[2 * rows :], width, -1)
    )


def to_rows(values):
    chans, rows, width = values.shape
    return values.astype(F32).reshape(chans * rows, width).astype(BF16)


def band(taps_ref, out_ref, out_rows, turned, flipped):
    m, n = taps_ref.shape[1:][::-1] if turned else taps_ref.shape[1:]
    wide = (out_rows + 2) * n
    spread = one_hot((n, wide), lambda r, c: c % n == r)
    block = lax.broadcasted_iota(jnp.int32, (m, wide), 1) // n
    if turned:
        tiled = [
            lax.dot_general(
                taps_ref[at], spread, (((0,), (0,)), ((), ())), preferred_element_type=F32
            )
            for at in range(27)
        ]
    else:
        every = mm(taps_ref[...].reshape(27 * m, n), spread)
        tiled = [every[at * m : (at + 1) * m] for at in range(27)]
    if flipped:
        tiled = tiled[::-1]
    for a in range(3):
        for c in range(3):
            taps = [tiled[(a * 3 + b) * 3 + c] for b in range(3)]
            for y in range(out_rows):
                value = jnp.where(
                    block == y,
                    taps[0],
                    jnp.where(block == y + 1, taps[1], jnp.where(block == y + 2, taps[2], 0.0)),
                )
                start = (c * out_rows + y) * m
                out_ref[start : start + m, a * wide : (a + 1) * wide] = value.astype(BF16)


def weights_kernel(kf, kc, wa, wt, wc, wct, *, ny):
    band(kf, wa, ny, False, False)
    band(kf, wt, ny, True, True)
    band(kc, wc, ny // 2 + 2, True, False)
    band(kc, wct, ny // 2, False, True)


def ends():
    return [lax.axis_index(axis) % 2 == 0 for axis in ("gx", "gy")]


def volume_rows_kernel(vol, own, even, odd):
    c1, nz, ny, nx = vol.shape
    swap = swap_matrix(ny, c1)
    for z in range(nz):
        own[:, z * nx : (z + 1) * nx] = mm(swap, to_rows(vol[:, z])).astype(BF16)
    low, high = own[:, : even.shape[1]], own[:, own.shape[1] - even.shape[1] :]
    first = ends()[0]
    even[...] = jnp.where(first, high, low)
    odd[...] = jnp.where(first, low, high)


def cot_rows_kernel(fc, cc, fine, coarse):
    c1, nz, ny, nx = fc.shape
    c2, cells, half = cc.shape
    hy = ny // 2
    swap = swap_matrix(ny, c1)
    for z in range(nz):
        fine[:, z * nx : (z + 1) * nx] = mm(swap, to_rows(fc[:, z])).astype(BF16)
    rows = mm(swap_matrix(cells, c2), to_rows(cc[...])).astype(BF16)
    for z in range(cells // hy):
        coarse[:, z * half : (z + 1) * half] = rows[z * hy * c2 : (z + 1) * hy * c2]


def stack_layers(out, own, even, odd):
    first = ends()[0]
    width = even.shape[1]
    low, high = even[...], odd[...]
    out[:, :width] = jnp.where(first, high, low)
    out[:, width : width + own.shape[1]] = own[...]
    out[:, width + own.shape[1] :] = jnp.where(first, low, high)


def stack_rows(out, own, even, odd):
    first = ends()[1]
    edge = even.shape[0]
    low, high = even[...], odd[...]
    out[:edge] = jnp.where(first, high, low)
    out[edge : edge + own.shape[0]] = own[...]
    out[edge + own.shape[0] :] = jnp.where(first, low, high)


def layers_kernel(own, z_even, z_odd, out, even, odd):
    stack_layers(out, own, z_even, z_odd)
    edge = even.shape[0]
    first = ends()[1]
    low, high = out[:edge], out[out.shape[0] - edge :]
    even[...] = jnp.where(first, high, low)
    odd[...] = jnp.where(first, low, high)


def coarse_layers_kernel(po, co, z_even, z_odd, p_out, c_out, even, odd):
    lanes, rows = po.shape[1], po.shape[0]
    half = (z_even.shape[1] - lanes) // 2
    stack_layers(p_out, po, z_even.at[:, :lanes], z_odd.at[:, :lanes])
    first = ends()[0]
    width = co.shape[1]
    for part in range(2):
        span = slice(lanes + part * half, lanes + (part + 1) * half)
        low, high = z_even[:, span], z_odd[:, span]
        into = slice(part * rows, (part + 1) * rows)
        c_out[into, :half] = jnp.where(first, high, low)
        c_out[into, half + width :] = jnp.where(first, low, high)
    c_out[:, half : half + width] = co[...]
    edge = even.shape[0]
    pooled = p_out.shape[1]
    first = ends()[1]
    for ref, span in ((p_out, slice(0, pooled)), (c_out, slice(pooled, even.shape[1]))):
        low, high = ref[:edge], ref[ref.shape[0] - edge :]
        even[:, span] = jnp.where(first, high, low)
        odd[:, span] = jnp.where(first, low, high)


def three_layers(ref, rows, first, step, width):
    return jnp.concatenate(
        [ref[rows, first + dz * step : first + dz * step + width] for dz in range(3)], axis=0
    )


def fine_kernel_fn(xo, y_even, y_odd, wa, co, x_ref, pre_out, fo_out, po, z_even, z_odd, *, nz, nx):
    c1 = y_even.shape[0]
    half = nx // 2
    stack_rows(x_ref, xo, y_even, y_odd)
    pool = one_hot((nx, half), lambda r, c: r // 2 == c)
    rows = xo.shape[0]
    for layer in range(nz):
        parts = mm(wa[...], three_layers(x_ref, slice(None), layer * nx, nx, nx))
        pre = combine(parts, nx)
        pre_out[:, layer * nx : (layer + 1) * nx] = pre
        value = xo[:, (layer + 1) * nx : (layer + 2) * nx].astype(F32)
        fo = (value + pre * jax.nn.sigmoid(pre)).astype(BF16)
        fo_out[:, layer * nx : (layer + 1) * nx] = fo
        pooled = mm(fo, pool)
        if layer % 2 == 0:
            sums = pooled
            continue
        sums = sums + pooled
        cells = [
            sums[2 * r * c1 : (2 * r + 1) * c1] + sums[(2 * r + 1) * c1 : (2 * r + 2) * c1]
            for r in range(rows // c1 // 2)
        ]
        place = layer // 2
        value = jnp.concatenate(cells, axis=0) * 0.125
        po[:, place * half : (place + 1) * half] = value.astype(BF16)
    lanes = po.shape[1]
    low, high = co[:, :half], co[:, co.shape[1] - half :]
    first = ends()[0]
    for ref, value in (
        (z_even, jnp.where(first, high, low)),
        (z_odd, jnp.where(first, low, high)),
    ):
        ref[:, :lanes] = po[...]
        ref[:, lanes : lanes + half] = value[: rows // 2]
        ref[:, lanes + half :] = value[rows // 2 :]


def slope_kernel_fn(pre_ref, fo, fo_out, sl_out, *, c1, nz, ny, nx):
    swap_back = swap_matrix(c1, ny)
    for layer in range(nz):
        span = slice(layer * nx, (layer + 1) * nx)
        pre = pre_ref[:, span]
        sig = jax.nn.sigmoid(pre)
        sl_out[:, span] = sig * (1.0 + pre * (1.0 - sig))
        rows = mm(swap_back, fo[:, span])
        fo_out[:, layer] = rows.reshape(c1, ny, nx).astype(BF16)


def coarse_kernel_fn(
    po, cc, y_even, y_odd, fc, sl, wc, wct,
    p_ref, cs_ref, co_out, fs_out, fg_out, z_even, z_odd, c_ref, *, c1, c2, nz, ny, nx,
):
    half, hz, hy = nx // 2, nz // 2, ny // 2
    pooled = po.shape[1]
    stack_rows(p_ref, po, y_even.at[:, :pooled], y_odd.at[:, :pooled])
    stack_rows(c_ref, cc, y_even.at[:, pooled:], y_odd.at[:, pooled:])
    inner = slice(c2, c2 + hy * c2)
    own = []
    for pair in range((hz + 2) // 2):
        pre = combine(mm(wc[...], three_layers(p_ref, slice(None), pair * nx, half, nx)), half)
        sig = jax.nn.sigmoid(pre)
        span = slice(pair * nx, (pair + 1) * nx)
        cot = c_ref[:, span].astype(F32)
        cs_ref[:, span] = (cot * (sig * (1.0 + pre * (1.0 - sig)))).astype(BF16)
        out = (pre[inner] * sig[inner]).astype(BF16)
        own += [out[:, :half], out[:, half:]]
    stacked = jnp.concatenate(own[1:-1], axis=0)
    co_out[...] = mm(swap_matrix(c2, hz * hy), stacked).astype(BF16)
    widen = one_hot((half, nx), lambda r, c: c // 2 == r)
    for pair in range(hz // 2):
        parts = mm(wct[...], three_layers(cs_ref, slice(None), pair * nx, half, nx))
        grad = combine(parts, half) * 0.125
        high = grad.astype(BF16)
        low = (grad - high.astype(F32)).astype(BF16)
        for side in range(2):
            lanes = slice(side * half, (side + 1) * half)
            up = mm(high[:, lanes], widen) + mm(low[:, lanes], widen)
            blocks = [up[y // 2 * c1 : y // 2 * c1 + c1] for y in range(ny)]
            spread = jnp.concatenate(blocks, axis=0)
            for layer in (4 * pair + 2 * side, 4 * pair + 2 * side + 1):
                span = slice(layer * nx, (layer + 1) * nx)
                total = fc[:, span].astype(F32) + spread
                fg_out[:, span] = total
                fs_out[:, span] = (total * sl[:, span]).astype(BF16)
    low, high = fs_out[:, :nx], fs_out[:, (nz - 1) * nx :]
    first = ends()[0]
    z_even[...] = jnp.where(first, high, low)
    z_odd[...] = jnp.where(first, low, high)


def terms_of(slopes, cells, chans, count, width, rows, lanes):
    slopes = slopes.astype(F32)
    shifted = [moved(slopes, width, -1), slopes, moved(slopes, width, 1)]
    shifted = [value.astype(BF16) for value in shifted]
    total = None
    for y in range(slopes.shape[0] // chans):
        left = jnp.concatenate([s[y * chans : (y + 1) * chans] for s in shifted], axis=0)
        first = y * count + rows
        right = [
            cells[first : first + 3 * count, lanes + a * width : lanes + a * width + slopes.shape[1]]
            for a in range(3)
        ]
        term = mm_t(left, jnp.concatenate(right, axis=0))
        total = term if total is None else total + term
    return total


def terms_kernel(x_ref, fs, p_ref, cs, g_out, *, c1, c2, nx):
    half = nx // 2
    fine = terms_of(fs[...], x_ref, c1, c1, nx, 0, 0)
    inner = cs[c2 : cs.shape[0] - c2, half : cs.shape[1] - half]
    coarse = terms_of(inner, p_ref, c2, c1, half, c1, half)
    three = 3 * c1
    g_out[:three, :] = fine[:, : 8 * c1]
    g_out[three : 9 * c1, :] = coarse[:, : 8 * c1]
    last = jnp.concatenate([fine[:, 8 * c1 :], coarse[:, 8 * c1 :]], axis=0)
    groups = [last[r * c1 : (r + 1) * c1] for r in range(9)]
    g_out[9 * c1 : 10 * c1, :] = jnp.concatenate(groups[:8], axis=1)
    g_out[10 * c1 :, :] = jnp.concatenate([groups[8]] * 8, axis=1)


def volume_grad_kernel(fs, y_even, y_odd, fg, wt, co, out, co_out, rows_ref, *, c1, nz, ny, nx):
    swap_back = swap_matrix(c1, ny)
    stack_rows(rows_ref, fs, y_even, y_odd)
    for layer in range(nz):
        parts = mm(wt[...], three_layers(rows_ref, slice(None), layer * nx, nx, nx))
        total = fg[:, layer * nx : (layer + 1) * nx] + combine(parts, nx)
        out[:, layer] = mm(swap_back, total.astype(BF16)).reshape(c1, ny, nx).astype(BF16)
    co_out[...] = co[...]


def finish_kernel(*refs, c1, c2, scale_fine, scale_coarse):
    parts, (fine, coarse) = refs[:-2], refs[-2:]
    total = tree_sum([part[...].astype(F32) for part in parts])
    tail = total[9 * c1 :]
    groups = [tail[:c1, r * c1 : (r + 1) * c1] for r in range(8)] + [tail[c1:, :c1]]
    last = jnp.concatenate(groups, axis=0)
    for c in range(3):
        own = slice(c * c1, (c + 1) * c1)
        for ab in range(8):
            fine[ab * 3 + c] = total[own, ab * c1 : (ab + 1) * c1] * scale_fine
        fine[24 + c] = last[own] * scale_fine
    for part, taps in ((total[3 * c1 : 9 * c1], 8), (last[3 * c1 :], 1)):
        turned = part.T * scale_coarse
        for ab in range(taps):
            for c in range(3):
                at = (8 if taps == 1 else ab) * 3 + c
                coarse[at] = turned[ab * c1 : (ab + 1) * c1, c * c2 : (c + 1) * c2]


def tree_sum(values):
    while len(values) > 1:
        values = [values[i] + values[i + 1] for i in range(0, len(values), 2)]
    return values[0]


def shapes(*pairs):
    return [pltpu.VMEM(shape, kind) for shape, kind in pairs]


def result(shape, kind):
    return jax.ShapeDtypeStruct(shape, kind)


def call(body, outs, args, flops=0, scratch=()):
    specs = [pl.BlockSpec(memory_space=pltpu.VMEM) for _ in args]
    nbytes = sum(a.size * a.dtype.itemsize for a in args)
    placed = [pltpu.with_memory_space_constraint(arg, pltpu.VMEM) for arg in args]
    return pl.pallas_call(
        body,
        out_shape=outs,
        in_specs=specs,
        out_specs=[pl.BlockSpec(memory_space=pltpu.VMEM) for _ in outs],
        scratch_shapes=list(scratch),
        compiler_params=pltpu.CompilerParams(vmem_limit_bytes=24 * 2**20),
        cost_estimate=pl.CostEstimate(flops=flops, bytes_accessed=nbytes, transcendentals=0),
    )(*placed)


def swap_pairs(even, odd, axis):
    count = lax.axis_size(axis)
    out = []
    for value, first in ((even, 0), (odd, 1)):
        pairs = [(i, i + 1) for i in range(first, count - 1, 2)]
        pairs += [(target, source) for source, target in pairs]
        out.append(lax.ppermute(value, axis, pairs))
    return out


def swap_bits(value, bits):
    ny = lax.axis_size("gy")
    count = lax.axis_size("gx") * ny
    flip = sum((bit if axis == "gy" else bit * ny) for axis, bit in bits)
    return lax.ppermute(value, ("gx", "gy"), [(i, i ^ flip) for i in range(count)])


def program(volume, fine_kernel, coarse_kernel, fine_cotangent, coarse_cotangent):
    c1, nz, ny, nx = volume.shape
    c2 = coarse_cotangent.shape[0]
    hz, hy, half = nz // 2, ny // 2, nx // 2
    gx, gy = lax.axis_size("gx"), lax.axis_size("gy")
    cells = nz * gx * ny * gy * nx
    sizes = dict(c1=c1, nz=nz, ny=ny, nx=nx)
    rows, half_rows = ny * c1, hy * c1

    own, z_even, z_odd = call(
        volume_rows_kernel,
        shapes(((rows, nz * nx), BF16), ((rows, nx), BF16), ((rows, nx), BF16)),
        [volume],
        flops=10**8,
    )
    z_even, z_odd = swap_pairs(z_even, z_odd, "gx")
    wa, wt, wc, wct = call(
        functools.partial(weights_kernel, ny=ny),
        shapes(
            ((3 * ny * c1, 3 * (ny + 2) * c1), BF16),
            ((3 * ny * c1, 3 * (ny + 2) * c1), BF16),
            ((3 * (hy + 2) * c2, 3 * (hy + 4) * c1), BF16),
            ((3 * hy * c1, 3 * (hy + 2) * c2), BF16),
        ),
        [
            fine_kernel.reshape(27, c1, c1),
            coarse_kernel.swapaxes(3, 4).reshape(27, c1, c2),
        ],
        flops=10**9,
    )
    fine_cot, coarse_cot = call(
        cot_rows_kernel,
        shapes(((rows, nz * nx), BF16), ((hy * c2, hz * half), BF16)),
        [fine_cotangent, coarse_cotangent.reshape(c2, hz * hy, half)],
        flops=10**8,
    )

    layers = (nz + 2) * nx
    stacked = shapes(((rows, layers), BF16), ((c1, layers), BF16), ((c1, layers), BF16))
    own, y_even, y_odd = call(layers_kernel, stacked, [own, z_even, z_odd], flops=10**8)
    y_even, y_odd = swap_pairs(y_even, y_odd, "gy")

    sent = (half_rows, hz * half + 2 * half)
    volume_rows, pre, fine_rows, pooled, z_even, z_odd = call(
        functools.partial(fine_kernel_fn, nz=nz, nx=nx),
        shapes(
            ((rows + 2 * c1, layers), BF16),
            ((rows, nz * nx), F32),
            ((rows, nz * nx), BF16),
            ((half_rows, hz * half), BF16),
            (sent, BF16),
            (sent, BF16),
        ),
        [own, y_even, y_odd, wa, coarse_cot],
        flops=3 * 10**9,
    )
    z_even, z_odd = swap_pairs(z_even, z_odd, "gx")
    fine_out, slopes = call(
        functools.partial(slope_kernel_fn, **sizes),
        [result((c1, nz, ny, nx), BF16)] + shapes(((rows, nz * nx), F32)),
        [pre, fine_rows],
        flops=2 * 10**9,
    )
    pooled_lanes = 3 * hz * half
    cot_lanes = (hz + 2) * half
    sent = (2 * c1, pooled_lanes + cot_lanes)
    pooled, coarse_cot, y_even, y_odd = call(
        coarse_layers_kernel,
        shapes(
            ((half_rows, pooled_lanes), BF16),
            ((hy * c2, cot_lanes), BF16),
            (sent, BF16),
            (sent, BF16),
        ),
        [pooled, coarse_cot, z_even, z_odd],
        flops=10**8,
    )
    y_even, y_odd = swap_pairs(y_even, y_odd, "gy")

    pooled, coarse_slope, coarse_out, fslope, fgrad, z_even, z_odd = call(
        functools.partial(coarse_kernel_fn, c2=c2, **sizes),
        shapes(
            (((hy + 4) * c1, pooled_lanes), BF16),
            (((hy + 2) * c2, cot_lanes), BF16),
            ((c2 * hz * hy, half), BF16),
            ((rows, nz * nx), BF16),
            ((rows, nz * nx), F32),
            ((rows, nx), BF16),
            ((rows, nx), BF16),
        ),
        [pooled, coarse_cot, y_even, y_odd, fine_cot, slopes, wc, wct],
        flops=4 * 10**9,
        scratch=[pltpu.VMEM(((hy + 2) * c2, cot_lanes), BF16)],
    )
    z_even, z_odd = swap_pairs(z_even, z_odd, "gx")
    (terms,) = call(
        functools.partial(terms_kernel, c1=c1, c2=c2, nx=nx),
        shapes(((11 * c1, 8 * c1), F32)),
        [volume_rows, fslope, pooled, coarse_slope],
        flops=2 * 10**9,
    )
    fslope, y_even, y_odd = call(layers_kernel, stacked, [fslope, z_even, z_odd], flops=10**8)
    y_even, y_odd = swap_pairs(y_even, y_odd, "gy")

    bits = [("gy", 1 << n) for n in range(gy.bit_length() - 1)]
    bits += [("gx", 1 << n) for n in range(gx.bit_length() - 1)]
    first = len(bits) % 2
    rounds = [bits[:1]] * first
    rounds += [bits[n : n + 2] for n in range(first, len(bits), 2)]
    value = terms
    for index, group in enumerate(rounds):
        if index:
            value = value.astype(BF16)
        parts = [value]
        for some in [[bit] for bit in group] + [group] * (len(group) == 2):
            parts.append(swap_bits(value, some))
        if index + 1 < len(rounds):
            value = tree_sum([part.astype(F32) for part in parts])
    volume_grad, coarse_out = call(
        functools.partial(volume_grad_kernel, **sizes),
        [result((c1, nz, ny, nx), BF16), result((c2 * hz * hy, half), BF16)],
        [fslope, y_even, y_odd, fgrad, wt, coarse_out],
        flops=2 * 10**9,
        scratch=[pltpu.VMEM((rows + 2 * c1, layers), BF16)],
    )
    fine_grad, coarse_grad = call(
        functools.partial(
            finish_kernel,
            c1=c1,
            c2=c2,
            scale_fine=cells ** (-0.5),
            scale_coarse=(cells // 8) ** (-0.5),
        ),
        [result((27, c1, c1), F32), result((27, c1, c2), F32)],
        parts,
        flops=10**7,
    )
    return (
        fine_out,
        coarse_out.reshape(c2, hz, hy, half),
        volume_grad,
        fine_grad.reshape(fine_kernel.shape),
        coarse_grad.reshape(3, 3, 3, c1, c2).swapaxes(3, 4),
    )


def solution(mesh):
    split = P(None, "gx", "gy", None)
    return jax.shard_map(
        program,
        mesh=mesh,
        in_specs=(split, P(), P(), split, split),
        out_specs=(split, split, split, P(), P()),
        check_vma=False,
    )
```

time: 64.8 us -> 55.8 us (0.86)
  waiting for transfers between devices: 13.6 us -> 7.38 us
  Pallas kernels: 13.3 us -> 9.26 us
  starting transfers between devices: 33.4 us -> 36.8 us
  local copies, waits for them, and re-layouts: 3.36 us -> 1.19 us
    ppermute x10 -> x12, waiting for transfers between devices: 9.11 us -> 3.2 us  [swap_pairs(): out.append(lax.ppermute(value, axis, pairs))]
    ppermute x10 -> x12, starting transfers between devices: 14.8 us -> 20 us  [swap_pairs(): out.append(lax.ppermute(value, axis, pairs))]
    pallas_call x10 -> x12, Pallas kernels: 13.3 us -> 9.26 us  [call(): pl.pallas_call(body, out_shape=outs, in_specs=specs, out_specs=[pl.BlockS...]
    unnamed x11 -> x10, local copies, waits for them, and re-layouts: 3.36 us -> 1.19 us
    ppermute x7, starting transfers between devices: 18.6 us -> 16.8 us  [swap_bits(): lax.ppermute(value, ('gx', 'gy'), [(i, i ^ flip) for i in range(count)])]
  transfers between devices with their start and end apart: 17 -> 19, of which waited for: 6 -> 5; matrix products, arithmetic and copies ran while one was open for 1% -> 0% of each run, Pallas kernels for 12% -> 8%
where the time goes in v2:
time: 55.8 us; the launch traced here: 55.5 us
  starting transfers between devices  36.8 us (66%)
  Pallas kernels  9.26 us (17%)
  waiting for transfers between devices  7.38 us (13%)
  local copies, waits for them, and re-layouts  1.19 us (2%)
  between operations  0.81 us (1%)
    ppermute x12, starting transfers between devices, swap_pairs(): out.append(lax.ppermute(value, axis, pairs))  20 us
    ppermute x7, starting transfers between devices, swap_bits(): lax.ppermute(value, ('gx', 'gy'), [(i, i ^ flip) for i in range(count)])  16.8 us
    pallas_call x12, Pallas kernels, call(): pl.pallas_call(body, out_shape=outs, in_specs=specs, out_specs=[pl.BlockS...  9.26 us
    ppermute x7, waiting for transfers between devices, swap_bits(): lax.ppermute(value, ('gx', 'gy'), [(i, i ^ flip) for i in range(count)])  4.18 us
    ppermute x12, waiting for transfers between devices, swap_pairs(): out.append(lax.ppermute(value, axis, pairs))  3.2 us
    unnamed x10, local copies, waits for them, and re-layouts  1.19 us
  transfers between devices with their start and end apart: 19, of which 5 were waited for; matrix products, arithmetic and copies ran while one was open for 0% of the time, Pallas kernels for 8%

profile of v2, /device:TPU:0, one launch (start us, length us, event | category | flops | bytes accessed | tf_op | source)
XLA Modules:
  0.0 55.5 jit_solution(4975461016847703213)
XLA Ops:
  0.6 0.9 %copy-done = bf16[16,4,8,256]{3,2,1,0:T(8,128)(2,1)S(1)} copy-done((bf16[16,4,8,256]{3,2,1,0:T(8,128)(2,1)S(1)}, bf16[16,4,8,256]{3,2,1,0:T(8,128)(2,1)}, u32[]{:S(2)}) %copy-start) | copy-done | bytes 262168
  1.6 0.2 shard_map.92
  1.8 3.0 %collective-permute-start = (bf16[128,256]{1,0:T(8,128)(2,1)S(1)}, bf16[128,256]{1,0:T(8,128)(2,1)S(1)}, u32[]{:S(2)}, u32[]{:S(2)}) collective-permute-start(bf16[128,256]{1,0:T(8,128)(2,1)S(1)} %get-tuple-element.44), channel_id=1, source_target_pairs={{0,4},{8,12},{16,20},{24,28},{4,0},{12,8},{20,16},{28,24},{1,5},{9... | collective-permute-start | bytes 196616 | tf_op jit(solution)/shard_map/ppermute | solution.py:360
  4.8 0.7 %collective-permute-start.1 = (bf16[128,256]{1,0:T(8,128)(2,1)S(1)}, bf16[128,256]{1,0:T(8,128)(2,1)S(1)}, u32[]{:S(2)}, u32[]{:S(2)}) collective-permute-start(bf16[128,256]{1,0:T(8,128)(2,1)S(1)} %get-tuple-element.45), channel_id=1, source_target_pairs={{4,8},{12,16},{20,24},{8,4},{16,12},{24,20},{5,9},{13,17},{21,25},... | collective-permute-start | bytes 196616 | tf_op jit(solution)/shard_map/ppermute | solution.py:360
  5.5 1.6 %collective-permute-done.z_even = bf16[128,256]{1,0:T(8,128)(2,1)S(1)} collective-permute-done((bf16[128,256]{1,0:T(8,128)(2,1)S(1)}, bf16[128,256]{1,0:T(8,128)(2,1)S(1)}, u32[]{:S(2)}, u32[]{:S(2)}) %collective-permute-start) | collective-permute-done | bytes 65568 | tf_op jit(solution)/shard_map/ppermute | solution.py:360
  7.2 0.7 %collective-permute-start.3 = (bf16[16,1536]{1,0:T(8,128)(2,1)S(1)}, bf16[16,1536]{1,0:T(8,128)(2,1)S(1)}, u32[]{:S(2)}, u32[]{:S(2)}) collective-permute-start(bf16[16,1536]{1,0:T(8,128)(2,1)S(1)} %get-tuple-element.48), channel_id=1, source_target_pairs={{1,2},{2,1},{5,6},{6,5},{9,10},{10,9},{13,14},{14,13},{17,18},{18,... | collective-permute-start | bytes 147464 | tf_op jit(solution)/shard_map/ppermute | solution.py:360
  7.9 0.1 copy-done.2
  8.0 0.9 %shard_map.94 = (bf16[384,480]{1,0:T(8,128)(2,1)S(1)}, bf16[384,480]{1,0:T(8,128)(2,1)S(1)}, bf16[576,384]{1,0:T(8,128)(2,1)S(1)}, bf16[192,576]{1,0:T(8,128)(2,1)S(1)}) custom-call(bf16[27,16,16]{2,1,0:T(8,128)(2,1)S(1)} %bitcast.10, bf16[27,16,32]{2,1,0:T(8,128)(2,1)S(1)} %bitcast.11), custom_call_target="tpu_custom_call" | custom-call | flops 1000000000 | bytes 41472 | tf_op jit(solution)/shard_map/pallas_call | solution.py:343
  8.9 0.1 copy-done.1
  9.0 0.3 shard_map.95
  9.3 1.1 %shard_map.96 = (bf16[160,1536]{1,0:T(8,128)(2,1)S(1)}, f32[128,1024]{1,0:T(8,128)S(1)}, bf16[128,1024]{1,0:T(8,128)(2,1)S(1)}, bf16[64,256]{1,0:T(8,128)(2,1)S(...) custom-call(bf16[128,1536]{1,0:T(8,128)(2,1)S(1)} %get-tuple-element.46.xo, ...), custom_call_target="tpu_custom_call" | custom-call | flops 3000000000 | bytes 925696 | tf_op jit(solution)/shard_map/pallas_call | solution.py:343
  10.4 5.0 %collective-permute-start.4 = (bf16[64,512]{1,0:T(8,128)(2,1)S(1)}, bf16[64,512]{1,0:T(8,128)(2,1)S(1)}, u32[]{:S(2)}, u32[]{:S(2)}) collective-permute-start(bf16[64,512]{1,0:T(8,128)(2,1)S(1)} %get-tuple-element.55), channel_id=1, source_target_pairs={{0,4},{8,12},{16,20},{24,28},{4,0},{12,8},{20,16},{28,24},{1,5},{9... | collective-permute-start | bytes 196616 | tf_op jit(solution)/shard_map/ppermute | solution.py:360
  15.3 0.7 %collective-permute-start.5 = (bf16[64,512]{1,0:T(8,128)(2,1)S(1)}, bf16[64,512]{1,0:T(8,128)(2,1)S(1)}, u32[]{:S(2)}, u32[]{:S(2)}) collective-permute-start(bf16[64,512]{1,0:T(8,128)(2,1)S(1)} %get-tuple-element.56), channel_id=1, source_target_pairs={{4,8},{12,16},{20,24},{8,4},{16,12},{24,20},{5,9},{13,17},{21,25},... | collective-permute-start | bytes 196616 | tf_op jit(solution)/shard_map/ppermute | solution.py:360
  16.0 1.6 %collective-permute-done.4.z_even = bf16[64,512]{1,0:T(8,128)(2,1)S(1)} collective-permute-done((bf16[64,512]{1,0:T(8,128)(2,1)S(1)}, bf16[64,512]{1,0:T(8,128)(2,1)S(1)}, u32[]{:S(2)}, u32[]{:S(2)}) %collective-permute-start.4) | collective-permute-done | bytes 65568 | tf_op jit(solution)/shard_map/ppermute | solution.py:360
  17.6 3.0 %collective-permute-start.6 = (bf16[32,1280]{1,0:T(8,128)(2,1)S(1)}, bf16[32,1280]{1,0:T(8,128)(2,1)S(1)}, u32[]{:S(2)}, u32[]{:S(2)}) collective-permute-start(bf16[32,1280]{1,0:T(8,128)(2,1)S(1)} %get-tuple-element.59), channel_id=1, source_target_pairs={{0,1},{2,3},{1,0},{3,2},{4,5},{6,7},{5,4},{7,6},{8,9},{10,11},{9,8... | collective-permute-start | bytes 245768 | tf_op jit(solution)/shard_map/ppermute | solution.py:360
  20.7 0.7 %collective-permute-start.7 = (bf16[32,1280]{1,0:T(8,128)(2,1)S(1)}, bf16[32,1280]{1,0:T(8,128)(2,1)S(1)}, u32[]{:S(2)}, u32[]{:S(2)}) collective-permute-start(bf16[32,1280]{1,0:T(8,128)(2,1)S(1)} %get-tuple-element.60), channel_id=1, source_target_pairs={{1,2},{2,1},{5,6},{6,5},{9,10},{10,9},{13,14},{14,13},{17,18},{18,... | collective-permute-start | bytes 245768 | tf_op jit(solution)/shard_map/ppermute | solution.py:360
  21.3 1.1 %shard_map.97 = (bf16[16,4,8,256]{3,2,1,0:T(8,128)(2,1)}, f32[128,1024]{1,0:T(8,128)S(1)}) custom-call(f32[128,1024]{1,0:T(8,128)S(1)} %get-tuple-element.51.pre_ref, bf16[128,1024]{1,0:T(8,128)(2,1)S(1)} %get-tuple-element.52.fo), custom_call_target="tpu_custom_call" | custom-call | flops 2000000000 | bytes 786432 | tf_op jit(solution)/shard_map/pallas_call | solution.py:343
  22.4 1.2 %shard_map.99 = (bf16[128,768]{1,0:T(8,128)(2,1)S(1)}, bf16[192,512]{1,0:T(8,128)(2,1)S(1)}, bf16[256,128]{1,0:T(8,128)(2,1)S(1)}, bf16[128,1024]{1,0:T(8,128)(2...) custom-call(bf16[64,768]{1,0:T(8,128)(2,1)S(1)} %get-tuple-element.57.po, ...), custom_call_target="tpu_custom_call" | custom-call | flops 4000000000 | bytes 1843200 | tf_op jit(solution)/shard_map/pallas_call | solution.py:343
  23.6 1.1 %shard_map.102 = f32[176,128]{1,0:T(8,128)S(1)} custom-call(bf16[160,1536]{1,0:T(8,128)(2,1)S(1)} %get-tuple-element.76.x_ref, bf16[128,1024]{1,0:T(8,128)(2,1)S(1)} %get-tuple-element.65.own.fs, bf16[128,768]{1,0:T(8,128)(2,1)S(1)} %get-tuple-element.77.p_ref, bf16[192,512]{1,0:T(8,128)(2,1)S(1)} %get-tuple-element.78.cs), custom_call_target="tpu_custom_call" | custom-call | flops 2000000000 | bytes 1146880 | tf_op jit(solution)/shard_map/pallas_call | solution.py:343
  24.7 4.8 %collective-permute-start.12 = (f32[176,128]{1,0:T(8,128)S(1)}, f32[176,128]{1,0:T(8,128)S(1)}, u32[]{:S(2)}, u32[]{:S(2)}) collective-permute-start(f32[176,128]{1,0:T(8,128)S(1)} %shard_map.102), channel_id=1, source_target_pairs={{0,1},{1,0},{2,3},{3,2},{4,5},{5,4},{6,7},{7,6},{8,9},{9,8},{10,11... | collective-permute-start | bytes 270344 | tf_op jit(solution)/shard_map/ppermute | solution.py:368
  29.5 4.9 %collective-permute-start.8 = (bf16[128,256]{1,0:T(8,128)(2,1)S(1)}, bf16[128,256]{1,0:T(8,128)(2,1)S(1)}, u32[]{:S(2)}, u32[]{:S(2)}) collective-permute-start(bf16[128,256]{1,0:T(8,128)(2,1)S(1)} %get-tuple-element.66), channel_id=1, source_target_pairs={{0,4},{8,12},{16,20},{24,28},{4,0},{12,8},{20,16},{28,24},{1,5},{9... | collective-permute-start | bytes 196616 | tf_op jit(solution)/shard_map/ppermute | solution.py:360
  34.5 0.7 %collective-permute-start.9 = (bf16[128,256]{1,0:T(8,128)(2,1)S(1)}, bf16[128,256]{1,0:T(8,128)(2,1)S(1)}, u32[]{:S(2)}, u32[]{:S(2)}) collective-permute-start(bf16[128,256]{1,0:T(8,128)(2,1)S(1)} %get-tuple-element.67), channel_id=1, source_target_pairs={{4,8},{12,16},{20,24},{8,4},{16,12},{24,20},{5,9},{13,17},{21,25},... | collective-permute-start | bytes 196616 | tf_op jit(solution)/shard_map/ppermute | solution.py:360
  35.2 6.9 %collective-permute-start.15 = (bf16[176,128]{1,0:T(8,128)(2,1)S(1)}, bf16[176,128]{1,0:T(8,128)(2,1)S(1)}, u32[]{:S(2)}, u32[]{:S(2)}) collective-permute-start(bf16[176,128]{1,0:T(8,128)(2,1)S(1)} %add_convert_fusion.1), channel_id=1, source_target_pairs={{0,6},{1,7},{2,4},{3,5},{4,2},{5,3},{6,0},{7,1},{8,14},{9,15},{10,... | collective-permute-start | bytes 135176 | tf_op jit(solution)/shard_map/ppermute | solution.py:368
  42.0 0.6 %collective-permute-start.13 = (bf16[176,128]{1,0:T(8,128)(2,1)S(1)}, bf16[176,128]{1,0:T(8,128)(2,1)S(1)}, u32[]{:S(2)}, u32[]{:S(2)}) collective-permute-start(bf16[176,128]{1,0:T(8,128)(2,1)S(1)} %add_convert_fusion.1), channel_id=1, source_target_pairs={{0,2},{1,3},{2,0},{3,1},{4,6},{5,7},{6,4},{7,5},{8,10},{9,11},{10,... | collective-permute-start | bytes 135176 | tf_op jit(solution)/shard_map/ppermute | solution.py:368
  42.8 0.7 %collective-permute-start.11 = (bf16[16,1536]{1,0:T(8,128)(2,1)S(1)}, bf16[16,1536]{1,0:T(8,128)(2,1)S(1)}, u32[]{:S(2)}, u32[]{:S(2)}) collective-permute-start(bf16[16,1536]{1,0:T(8,128)(2,1)S(1)} %get-tuple-element.70), channel_id=1, source_target_pairs={{1,2},{2,1},{5,6},{6,5},{9,10},{10,9},{13,14},{14,13},{17,18},{18,... | collective-permute-start | bytes 147464 | tf_op jit(solution)/shard_map/ppermute | solution.py:360
  43.5 1.0 %collective-permute-done.15 = bf16[176,128]{1,0:T(8,128)(2,1)S(1)} collective-permute-done((bf16[176,128]{1,0:T(8,128)(2,1)S(1)}, bf16[176,128]{1,0:T(8,128)(2,1)S(1)}, u32[]{:S(2)}, u32[]{:S(2)}) %collective-permute-start.15) | collective-permute-done | bytes 45088 | tf_op jit(solution)/shard_map/ppermute | solution.py:368
  44.5 1.6 %collective-permute-done.14 = bf16[176,128]{1,0:T(8,128)(2,1)S(1)} collective-permute-done((bf16[176,128]{1,0:T(8,128)(2,1)S(1)}, bf16[176,128]{1,0:T(8,128)(2,1)S(1)}, u32[]{:S(2)}, u32[]{:S(2)}) %collective-permute-start.14) | collective-permute-done | bytes 45088 | tf_op jit(solution)/shard_map/ppermute | solution.py:368
  46.1 3.1 %collective-permute-start.18 = (bf16[176,128]{1,0:T(8,128)(2,1)S(1)}, bf16[176,128]{1,0:T(8,128)(2,1)S(1)}, u32[]{:S(2)}, u32[]{:S(2)}) collective-permute-start(bf16[176,128]{1,0:T(8,128)(2,1)S(1)} %add_convert_fusion.refs_0_), channel_id=1, source_target_pairs={{0,24},{1,25},{2,26},{3,27},{4,28},{5,29},{6,30},{7,31},{8,16},{9,... | collective-permute-start | bytes 135176 | tf_op jit(solution)/shard_map/ppermute | solution.py:368
  49.2 1.4 %collective-permute-start.16 = (bf16[176,128]{1,0:T(8,128)(2,1)S(1)}, bf16[176,128]{1,0:T(8,128)(2,1)S(1)}, u32[]{:S(2)}, u32[]{:S(2)}) collective-permute-start(bf16[176,128]{1,0:T(8,128)(2,1)S(1)} %add_convert_fusion.refs_0_), channel_id=1, source_target_pairs={{0,8},{1,9},{2,10},{3,11},{4,12},{5,13},{6,14},{7,15},{8,0},{9,1},... | collective-permute-start | bytes 135176 | tf_op jit(solution)/shard_map/ppermute | solution.py:368
  50.6 2.3 %shard_map.101 = (bf16[16,4,8,256]{3,2,1,0:T(8,128)(2,1)}, bf16[256,128]{1,0:T(8,128)(2,1)}) custom-call(bf16[128,1536]{1,0:T(8,128)(2,1)S(1)} %get-tuple-element.68.fs, bf16[16,1536]{1,0:T(8,128)(2,1)S(1)} %collective-permute-done.10.y_even, bf16[16,1536]{1,0:T(8,128)(2,1)S(1)} %collective-permute-done.11.y_odd, f32[128,1024]{1,0:T(8,128)S(1)} %get-tuple-element.71.fg, ...), custom_call_target="tpu_custom_call" | custom-call | flops 2000000000 | bytes 1449984 | tf_op jit(solution)/shard_map/pallas_call | solution.py:343
  52.9 1.6 %collective-permute-done.17.refs_2_ = bf16[176,128]{1,0:T(8,128)(2,1)S(1)} collective-permute-done((bf16[176,128]{1,0:T(8,128)(2,1)S(1)}, bf16[176,128]{1,0:T(8,128)(2,1)S(1)}, u32[]{:S(2)}, u32[]{:S(2)}) %collective-permute-start.17) | collective-permute-done | bytes 45088 | tf_op jit(solution)/shard_map/ppermute | solution.py:368
  54.5 1.0 %shard_map.103 = (f32[27,16,16]{2,1,0:T(8,128)}, f32[27,16,32]{2,1,0:T(8,128)}) custom-call(bf16[176,128]{1,0:T(8,128)(2,1)S(1)} %add_convert_fusion.refs_0_, bf16[176,128]{1,0:T(8,128)(2,1)S(1)} %collective-permute-done.16.refs_1_, bf16[176,128]{1,0:T(8,128)(2,1)S(1)} %collective-permute-done.17.refs_2_, bf16[176,128]{1,0:T(8,128)(2,1)S(1)} %collective-permute-done.18.refs_3_), custom_call_target="tpu_custom_call" | custom-call | flops 10000000 | bytes 180224 | tf_op jit(solution)/shard_map/pallas_call | solution.py:343
  (30 shorter events, 0.4 us)
Async XLA Ops:
  0.6 1.0 %copy-start = (bf16[16,4,8,256]{3,2,1,0:T(8,128)(2,1)S(1)}, bf16[16,4,8,256]{3,2,1,0:T(8,128)(2,1)}, u32[]{:S(2)}) copy-start(bf16[16,4,8,256]{3,2,1,0:T(8,128)(2,1)} %vol.1) | copy-start | bytes 786436
  1.8 5.3 %collective-permute-start = (bf16[128,256]{1,0:T(8,128)(2,1)S(1)}, bf16[128,256]{1,0:T(8,128)(2,1)S(1)}, u32[]{:S(2)}, u32[]{:S(2)}) collective-permute-start(bf16[128,256]{1,0:T(8,128)(2,1)S(1)} %get-tuple-element.44), channel_id=1, source_target_pairs={{0,4},{8,12},{16,20},{24,28},{4,0},{12,8},{20,16},{28,24},{1,5},{9... | collective-permute-start | bytes 196616 | tf_op jit(solution)/shard_map/ppermute | solution.py:360
  4.8 2.2 %collective-permute-start.1 = (bf16[128,256]{1,0:T(8,128)(2,1)S(1)}, bf16[128,256]{1,0:T(8,128)(2,1)S(1)}, u32[]{:S(2)}, u32[]{:S(2)}) collective-permute-start(bf16[128,256]{1,0:T(8,128)(2,1)S(1)} %get-tuple-element.45), channel_id=1, source_target_pairs={{4,8},{12,16},{20,24},{8,4},{16,12},{24,20},{5,9},{13,17},{21,25},... | collective-permute-start | bytes 196616 | tf_op jit(solution)/shard_map/ppermute | solution.py:360
  7.1 0.9 %copy-start.2 = (bf16[3,3,3,16,16]{4,3,2,1,0:T(8,128)(2,1)S(1)}, bf16[3,3,3,16,16]{4,3,2,1,0:T(8,128)(2,1)}, u32[]{:S(2)}) copy-start(bf16[3,3,3,16,16]{4,3,2,1,0:T(8,128)(2,1)} %param.6) | copy-start | bytes 41476
  7.1 0.9 %copy-start.3 = (bf16[3,3,3,32,16]{3,4,2,1,0:T(8,128)(2,1)S(1)}, bf16[3,3,3,32,16]{3,4,2,1,0:T(8,128)(2,1)}, u32[]{:S(2)}) copy-start(bf16[3,3,3,32,16]{3,4,2,1,0:T(8,128)(2,1)} %param.7) | copy-start | bytes 82948
  7.1 2.1 %collective-permute-start.2 = (bf16[16,1536]{1,0:T(8,128)(2,1)S(1)}, bf16[16,1536]{1,0:T(8,128)(2,1)S(1)}, u32[]{:S(2)}, u32[]{:S(2)}) collective-permute-start(bf16[16,1536]{1,0:T(8,128)(2,1)S(1)} %get-tuple-element.47), channel_id=1, source_target_pairs={{0,1},{2,3},{1,0},{3,2},{4,5},{6,7},{5,4},{7,6},{8,9},{10,11},{9,8... | collective-permute-start | bytes 147464 | tf_op jit(solution)/shard_map/ppermute | solution.py:360
  7.2 2.1 %collective-permute-start.3 = (bf16[16,1536]{1,0:T(8,128)(2,1)S(1)}, bf16[16,1536]{1,0:T(8,128)(2,1)S(1)}, u32[]{:S(2)}, u32[]{:S(2)}) collective-permute-start(bf16[16,1536]{1,0:T(8,128)(2,1)S(1)} %get-tuple-element.48), channel_id=1, source_target_pairs={{1,2},{2,1},{5,6},{6,5},{9,10},{10,9},{13,14},{14,13},{17,18},{18,... | collective-permute-start | bytes 147464 | tf_op jit(solution)/shard_map/ppermute | solution.py:360
  8.0 0.9 %copy-start.1 = (bf16[16,4,8,256]{3,2,1,0:T(8,128)(2,1)S(1)}, bf16[16,4,8,256]{3,2,1,0:T(8,128)(2,1)}, u32[]{:S(2)}) copy-start(bf16[16,4,8,256]{3,2,1,0:T(8,128)(2,1)} %fc.1) | copy-start | bytes 786436
  8.0 1.0 %copy-start.4 = (bf16[32,2,4,128]{3,2,1,0:T(4,128)(2,1)S(1)}, bf16[32,2,4,128]{3,2,1,0:T(4,128)(2,1)}, u32[]{:S(2)}) copy-start(bf16[32,2,4,128]{3,2,1,0:T(4,128)(2,1)} %param.9) | copy-start | bytes 196612
  10.4 7.2 %collective-permute-start.4 = (bf16[64,512]{1,0:T(8,128)(2,1)S(1)}, bf16[64,512]{1,0:T(8,128)(2,1)S(1)}, u32[]{:S(2)}, u32[]{:S(2)}) collective-permute-start(bf16[64,512]{1,0:T(8,128)(2,1)S(1)} %get-tuple-element.55), channel_id=1, source_target_pairs={{0,4},{8,12},{16,20},{24,28},{4,0},{12,8},{20,16},{28,24},{1,5},{9... | collective-permute-start | bytes 196616 | tf_op jit(solution)/shard_map/ppermute | solution.py:360
  15.3 2.2 %collective-permute-start.5 = (bf16[64,512]{1,0:T(8,128)(2,1)S(1)}, bf16[64,512]{1,0:T(8,128)(2,1)S(1)}, u32[]{:S(2)}, u32[]{:S(2)}) collective-permute-start(bf16[64,512]{1,0:T(8,128)(2,1)S(1)} %get-tuple-element.56), channel_id=1, source_target_pairs={{4,8},{12,16},{20,24},{8,4},{16,12},{24,20},{5,9},{13,17},{21,25},... | collective-permute-start | bytes 196616 | tf_op jit(solution)/shard_map/ppermute | solution.py:360
  17.6 4.8 %collective-permute-start.6 = (bf16[32,1280]{1,0:T(8,128)(2,1)S(1)}, bf16[32,1280]{1,0:T(8,128)(2,1)S(1)}, u32[]{:S(2)}, u32[]{:S(2)}) collective-permute-start(bf16[32,1280]{1,0:T(8,128)(2,1)S(1)} %get-tuple-element.59), channel_id=1, source_target_pairs={{0,1},{2,3},{1,0},{3,2},{4,5},{6,7},{5,4},{7,6},{8,9},{10,11},{9,8... | collective-permute-start | bytes 245768 | tf_op jit(solution)/shard_map/ppermute | solution.py:360
  20.7 1.7 %collective-permute-start.7 = (bf16[32,1280]{1,0:T(8,128)(2,1)S(1)}, bf16[32,1280]{1,0:T(8,128)(2,1)S(1)}, u32[]{:S(2)}, u32[]{:S(2)}) collective-permute-start(bf16[32,1280]{1,0:T(8,128)(2,1)S(1)} %get-tuple-element.60), channel_id=1, source_target_pairs={{1,2},{2,1},{5,6},{6,5},{9,10},{10,9},{13,14},{14,13},{17,18},{18,... | collective-permute-start | bytes 245768 | tf_op jit(solution)/shard_map/ppermute | solution.py:360
  24.7 10.4 %collective-permute-start.12 = (f32[176,128]{1,0:T(8,128)S(1)}, f32[176,128]{1,0:T(8,128)S(1)}, u32[]{:S(2)}, u32[]{:S(2)}) collective-permute-start(f32[176,128]{1,0:T(8,128)S(1)} %shard_map.102), channel_id=1, source_target_pairs={{0,1},{1,0},{2,3},{3,2},{4,5},{5,4},{6,7},{7,6},{8,9},{9,8},{10,11... | collective-permute-start | bytes 270344 | tf_op jit(solution)/shard_map/ppermute | solution.py:368
  29.5 13.1 %collective-permute-start.8 = (bf16[128,256]{1,0:T(8,128)(2,1)S(1)}, bf16[128,256]{1,0:T(8,128)(2,1)S(1)}, u32[]{:S(2)}, u32[]{:S(2)}) collective-permute-start(bf16[128,256]{1,0:T(8,128)(2,1)S(1)} %get-tuple-element.66), channel_id=1, source_target_pairs={{0,4},{8,12},{16,20},{24,28},{4,0},{12,8},{20,16},{28,24},{1,5},{9... | collective-permute-start | bytes 196616 | tf_op jit(solution)/shard_map/ppermute | solution.py:360
  34.5 8.2 %collective-permute-start.9 = (bf16[128,256]{1,0:T(8,128)(2,1)S(1)}, bf16[128,256]{1,0:T(8,128)(2,1)S(1)}, u32[]{:S(2)}, u32[]{:S(2)}) collective-permute-start(bf16[128,256]{1,0:T(8,128)(2,1)S(1)} %get-tuple-element.67), channel_id=1, source_target_pairs={{4,8},{12,16},{20,24},{8,4},{16,12},{24,20},{5,9},{13,17},{21,25},... | collective-permute-start | bytes 196616 | tf_op jit(solution)/shard_map/ppermute | solution.py:360
  35.2 9.3 %collective-permute-start.15 = (bf16[176,128]{1,0:T(8,128)(2,1)S(1)}, bf16[176,128]{1,0:T(8,128)(2,1)S(1)}, u32[]{:S(2)}, u32[]{:S(2)}) collective-permute-start(bf16[176,128]{1,0:T(8,128)(2,1)S(1)} %add_convert_fusion.1), channel_id=1, source_target_pairs={{0,6},{1,7},{2,4},{3,5},{4,2},{5,3},{6,0},{7,1},{8,14},{9,15},{10,... | collective-permute-start | bytes 135176 | tf_op jit(solution)/shard_map/ppermute | solution.py:368
  42.0 4.0 %collective-permute-start.14 = (bf16[176,128]{1,0:T(8,128)(2,1)S(1)}, bf16[176,128]{1,0:T(8,128)(2,1)S(1)}, u32[]{:S(2)}, u32[]{:S(2)}) collective-permute-start(bf16[176,128]{1,0:T(8,128)(2,1)S(1)} %add_convert_fusion.1), channel_id=1, source_target_pairs={{0,4},{1,5},{2,6},{3,7},{4,0},{5,1},{6,2},{7,3},{8,12},{9,13},{10,... | collective-permute-start | bytes 135176 | tf_op jit(solution)/shard_map/ppermute | solution.py:368
  42.0 4.0 %collective-permute-start.13 = (bf16[176,128]{1,0:T(8,128)(2,1)S(1)}, bf16[176,128]{1,0:T(8,128)(2,1)S(1)}, u32[]{:S(2)}, u32[]{:S(2)}) collective-permute-start(bf16[176,128]{1,0:T(8,128)(2,1)S(1)} %add_convert_fusion.1), channel_id=1, source_target_pairs={{0,2},{1,3},{2,0},{3,1},{4,6},{5,7},{6,4},{7,5},{8,10},{9,11},{10,... | collective-permute-start | bytes 135176 | tf_op jit(solution)/shard_map/ppermute | solution.py:368
  42.7 7.8 %collective-permute-start.10 = (bf16[16,1536]{1,0:T(8,128)(2,1)S(1)}, bf16[16,1536]{1,0:T(8,128)(2,1)S(1)}, u32[]{:S(2)}, u32[]{:S(2)}) collective-permute-start(bf16[16,1536]{1,0:T(8,128)(2,1)S(1)} %get-tuple-element.69), channel_id=1, source_target_pairs={{0,1},{2,3},{1,0},{3,2},{4,5},{6,7},{5,4},{7,6},{8,9},{10,11},{9,8... | collective-permute-start | bytes 147464 | tf_op jit(solution)/shard_map/ppermute | solution.py:360
  42.8 7.8 %collective-permute-start.11 = (bf16[16,1536]{1,0:T(8,128)(2,1)S(1)}, bf16[16,1536]{1,0:T(8,128)(2,1)S(1)}, u32[]{:S(2)}, u32[]{:S(2)}) collective-permute-start(bf16[16,1536]{1,0:T(8,128)(2,1)S(1)} %get-tuple-element.70), channel_id=1, source_target_pairs={{1,2},{2,1},{5,6},{6,5},{9,10},{10,9},{13,14},{14,13},{17,18},{18,... | collective-permute-start | bytes 147464 | tf_op jit(solution)/shard_map/ppermute | solution.py:360
  46.1 6.8 %collective-permute-start.18 = (bf16[176,128]{1,0:T(8,128)(2,1)S(1)}, bf16[176,128]{1,0:T(8,128)(2,1)S(1)}, u32[]{:S(2)}, u32[]{:S(2)}) collective-permute-start(bf16[176,128]{1,0:T(8,128)(2,1)S(1)} %add_convert_fusion.refs_0_), channel_id=1, source_target_pairs={{0,24},{1,25},{2,26},{3,27},{4,28},{5,29},{6,30},{7,31},{8,16},{9,... | collective-permute-start | bytes 135176 | tf_op jit(solution)/shard_map/ppermute | solution.py:368
  49.2 5.3 %collective-permute-start.17 = (bf16[176,128]{1,0:T(8,128)(2,1)S(1)}, bf16[176,128]{1,0:T(8,128)(2,1)S(1)}, u32[]{:S(2)}, u32[]{:S(2)}) collective-permute-start(bf16[176,128]{1,0:T(8,128)(2,1)S(1)} %add_convert_fusion.refs_0_), channel_id=1, source_target_pairs={{0,16},{1,17},{2,18},{3,19},{4,20},{5,21},{6,22},{7,23},{8,24},{9,... | collective-permute-start | bytes 135176 | tf_op jit(solution)/shard_map/ppermute | solution.py:368
  49.2 5.3 %collective-permute-start.16 = (bf16[176,128]{1,0:T(8,128)(2,1)S(1)}, bf16[176,128]{1,0:T(8,128)(2,1)S(1)}, u32[]{:S(2)}, u32[]{:S(2)}) collective-permute-start(bf16[176,128]{1,0:T(8,128)(2,1)S(1)} %add_convert_fusion.refs_0_), channel_id=1, source_target_pairs={{0,8},{1,9},{2,10},{3,11},{4,12},{5,13},{6,14},{7,15},{8,0},{9,1},... | collective-permute-start | bytes 135176 | tf_op jit(solution)/shard_map/ppermute | solution.py:368

commit v3 on v2

--- a/solution.py
+++ b/solution.py
@@ -94,6 +94,12 @@
     return [lax.axis_index(axis) % 2 == 0 for axis in ("gx", "gy")]
 
 
+def from_odd(value, axis):
+    at = lax.axis_index(axis)
+    alone = jnp.logical_or(at == 0, at == lax.axis_size(axis) - 1)
+    return jnp.where(alone, jnp.zeros_like(value), value)
+
+
 def volume_rows_kernel(vol, own, even, odd):
     c1, nz, ny, nx = vol.shape
     swap = swap_matrix(ny, c1)
@@ -120,7 +126,7 @@
 def stack_layers(out, own, even, odd):
     first = ends()[0]
     width = even.shape[1]
-    low, high = even[...], odd[...]
+    low, high = even[...], from_odd(odd[...], "gx")
     out[:, :width] = jnp.where(first, high, low)
     out[:, width : width + own.shape[1]] = own[...]
     out[:, width + own.shape[1] :] = jnp.where(first, low, high)
@@ -129,7 +135,7 @@
 def stack_rows(out, own, even, odd):
     first = ends()[1]
     edge = even.shape[0]
-    low, high = even[...], odd[...]
+    low, high = even[...], from_odd(odd[...], "gy")
     out[:edge] = jnp.where(first, high, low)
     out[edge : edge + own.shape[0]] = own[...]
     out[edge + own.shape[0] :] = jnp.where(first, low, high)
@@ -152,7 +158,7 @@
     width = co.shape[1]
     for part in range(2):
         span = slice(lanes + part * half, lanes + (part + 1) * half)
-        low, high = z_even[:, span], z_odd[:, span]
+        low, high = z_even[:, span], from_odd(z_odd[:, span], "gx")
         into = slice(part * rows, (part + 1) * rows)
         c_out[into, :half] = jnp.where(first, high, low)
         c_out[into, half + width :] = jnp.where(first, low, high)
@@ -352,12 +358,19 @@
 
 
 def swap_pairs(even, odd, axis):
-    count = lax.axis_size(axis)
+    nx, ny = lax.axis_size("gx"), lax.axis_size("gy")
     out = []
     for value, first in ((even, 0), (odd, 1)):
-        pairs = [(i, i + 1) for i in range(first, count - 1, 2)]
-        pairs += [(target, source) for source, target in pairs]
-        out.append(lax.ppermute(value, axis, pairs))
+        pairs = []
+        for place in range(nx * ny):
+            at = [place // ny, place % ny]
+            own = 0 if axis == "gx" else 1
+            if first and at[own] in (0, (nx, ny)[own] - 1):
+                at[1 - own] ^= 1
+            else:
+                at[own] = ((at[own] + first) ^ 1) - first
+            pairs.append((place, at[0] * ny + at[1]))
+        out.append(lax.ppermute(value, ("gx", "gy"), pairs))
     return out
 
 

time: 55.8 us -> 46.1 us (0.83)
  starting transfers between devices: 36.8 us -> 24.8 us
  waiting for transfers between devices: 7.38 us -> 10 us
    ppermute x7, starting transfers between devices: 16.8 us -> 10.1 us  [swap_bits(): lax.ppermute(value, ('gx', 'gy'), [(i, i ^ flip) for i in range(count)])]
    ppermute x12, starting transfers between devices: 20 us -> 14.7 us  [swap_pairs(): out.append(lax.ppermute(value, ('gx', 'gy'), pairs))]
    ppermute x12, waiting for transfers between devices: 3.2 us -> 8.53 us  [swap_pairs(): out.append(lax.ppermute(value, ('gx', 'gy'), pairs))]
    ppermute x7, waiting for transfers between devices: 4.18 us -> 1.5 us  [swap_bits(): lax.ppermute(value, ('gx', 'gy'), [(i, i ^ flip) for i in range(count)])]
  transfers between devices with their start and end apart: 19 -> 19, of which waited for: 5 -> 8; matrix products, arithmetic and copies ran while one was open for 0% -> 0% of each run, Pallas kernels for 8% -> 10%
where the time goes in v3:
time: 46.1 us; the launch traced here: 45.9 us
  starting transfers between devices  24.8 us (54%)
  waiting for transfers between devices  10 us (22%)
  Pallas kernels  9.27 us (20%)
  local copies, waits for them, and re-layouts  1.04 us (2%)
  between operations  0.77 us (2%)
    ppermute x12, starting transfers between devices, swap_pairs(): out.append(lax.ppermute(value, ('gx', 'gy'), pairs))  14.7 us
    ppermute x7, starting transfers between devices, swap_bits(): lax.ppermute(value, ('gx', 'gy'), [(i, i ^ flip) for i in range(count)])  10.1 us
    pallas_call x12, Pallas kernels, call(): pl.pallas_call(body, out_shape=outs, in_specs=specs, out_specs=[pl.BlockS...  9.27 us
    ppermute x12, waiting for transfers between devices, swap_pairs(): out.append(lax.ppermute(value, ('gx', 'gy'), pairs))  8.53 us
    ppermute x7, waiting for transfers between devices, swap_bits(): lax.ppermute(value, ('gx', 'gy'), [(i, i ^ flip) for i in range(count)])  1.5 us
    unnamed x10, local copies, waits for them, and re-layouts  1.04 us
  transfers between devices with their start and end apart: 19, of which 8 were waited for; matrix products, arithmetic and copies ran while one was open for 0% of the time, Pallas kernels for 10%

profile of v3, /device:TPU:0, one launch (start us, length us, event | category | flops | bytes accessed | tf_op | source)
XLA Modules:
  0.0 45.9 jit_solution(14012947677784860080)
XLA Ops:
  0.6 0.9 %copy-done = bf16[16,4,8,256]{3,2,1,0:T(8,128)(2,1)S(1)} copy-done((bf16[16,4,8,256]{3,2,1,0:T(8,128)(2,1)S(1)}, bf16[16,4,8,256]{3,2,1,0:T(8,128)(2,1)}, u32[]{:S(2)}) %copy-start) | copy-done | bytes 262168
  1.6 0.2 shard_map.92
  1.8 3.0 %collective-permute-start = (bf16[128,256]{1,0:T(8,128)(2,1)S(1)}, bf16[128,256]{1,0:T(8,128)(2,1)S(1)}, u32[]{:S(2)}, u32[]{:S(2)}) collective-permute-start(bf16[128,256]{1,0:T(8,128)(2,1)S(1)} %get-tuple-element.44), channel_id=1, source_target_pairs={{0,4},{1,5},{2,6},{3,7},{4,0},{5,1},{6,2},{7,3},{8,12},{9,13},{10,... | collective-permute-start | bytes 196616 | tf_op jit(solution)/shard_map/ppermute | solution.py:373
  4.8 3.1 %collective-permute-done.z_even = bf16[128,256]{1,0:T(8,128)(2,1)S(1)} collective-permute-done((bf16[128,256]{1,0:T(8,128)(2,1)S(1)}, bf16[128,256]{1,0:T(8,128)(2,1)S(1)}, u32[]{:S(2)}, u32[]{:S(2)}) %collective-permute-start) | collective-permute-done | bytes 65568 | tf_op jit(solution)/shard_map/ppermute | solution.py:373
  8.1 2.5 %collective-permute-start.3 = (bf16[16,1536]{1,0:T(8,128)(2,1)S(1)}, bf16[16,1536]{1,0:T(8,128)(2,1)S(1)}, u32[]{:S(2)}, u32[]{:S(2)}) collective-permute-start(bf16[16,1536]{1,0:T(8,128)(2,1)S(1)} %get-tuple-element.48), channel_id=1, source_target_pairs={{0,4},{1,2},{2,1},{3,7},{4,0},{5,6},{6,5},{7,3},{8,12},{9,10},{10,... | collective-permute-start | bytes 147464 | tf_op jit(solution)/shard_map/ppermute | solution.py:373
  10.6 0.9 %shard_map.94 = (bf16[384,480]{1,0:T(8,128)(2,1)S(1)}, bf16[384,480]{1,0:T(8,128)(2,1)S(1)}, bf16[576,384]{1,0:T(8,128)(2,1)S(1)}, bf16[192,576]{1,0:T(8,128)(2,1)S(1)}) custom-call(bf16[27,16,16]{2,1,0:T(8,128)(2,1)S(1)} %bitcast.10, bf16[27,16,32]{2,1,0:T(8,128)(2,1)S(1)} %bitcast.11), custom_call_target="tpu_custom_call" | custom-call | flops 1000000000 | bytes 41472 | tf_op jit(solution)/shard_map/pallas_call | solution.py:349
  11.5 0.1 copy-done.1
  11.5 0.3 shard_map.95
  11.8 0.8 %collective-permute-done.3.y_odd = bf16[16,1536]{1,0:T(8,128)(2,1)S(1)} collective-permute-done((bf16[16,1536]{1,0:T(8,128)(2,1)S(1)}, bf16[16,1536]{1,0:T(8,128)(2,1)S(1)}, u32[]{:S(2)}, u32[]{:S(2)}) %collective-permute-start.3) | collective-permute-done | bytes 49184 | tf_op jit(solution)/shard_map/ppermute | solution.py:373
  12.7 1.1 %shard_map.96 = (bf16[160,1536]{1,0:T(8,128)(2,1)S(1)}, f32[128,1024]{1,0:T(8,128)S(1)}, bf16[128,1024]{1,0:T(8,128)(2,1)S(1)}, bf16[64,256]{1,0:T(8,128)(2,1)S(...) custom-call(bf16[128,1536]{1,0:T(8,128)(2,1)S(1)} %get-tuple-element.46.xo, ...), custom_call_target="tpu_custom_call" | custom-call | flops 3000000000 | bytes 925696 | tf_op jit(solution)/shard_map/pallas_call | solution.py:349
  13.7 2.1 %collective-permute-start.4 = (bf16[64,512]{1,0:T(8,128)(2,1)S(1)}, bf16[64,512]{1,0:T(8,128)(2,1)S(1)}, u32[]{:S(2)}, u32[]{:S(2)}) collective-permute-start(bf16[64,512]{1,0:T(8,128)(2,1)S(1)} %get-tuple-element.55), channel_id=1, source_target_pairs={{0,4},{1,5},{2,6},{3,7},{4,0},{5,1},{6,2},{7,3},{8,12},{9,13},{10,... | collective-permute-start | bytes 196616 | tf_op jit(solution)/shard_map/ppermute | solution.py:373
  15.8 3.2 %collective-permute-done.4.z_even = bf16[64,512]{1,0:T(8,128)(2,1)S(1)} collective-permute-done((bf16[64,512]{1,0:T(8,128)(2,1)S(1)}, bf16[64,512]{1,0:T(8,128)(2,1)S(1)}, u32[]{:S(2)}, u32[]{:S(2)}) %collective-permute-start.4) | collective-permute-done | bytes 65568 | tf_op jit(solution)/shard_map/ppermute | solution.py:373
  19.2 2.5 %collective-permute-start.7 = (bf16[32,1280]{1,0:T(8,128)(2,1)S(1)}, bf16[32,1280]{1,0:T(8,128)(2,1)S(1)}, u32[]{:S(2)}, u32[]{:S(2)}) collective-permute-start(bf16[32,1280]{1,0:T(8,128)(2,1)S(1)} %get-tuple-element.60), channel_id=1, source_target_pairs={{0,4},{1,2},{2,1},{3,7},{4,0},{5,6},{6,5},{7,3},{8,12},{9,10},{10,... | collective-permute-start | bytes 245768 | tf_op jit(solution)/shard_map/ppermute | solution.py:373
  21.7 1.1 %shard_map.97 = (bf16[16,4,8,256]{3,2,1,0:T(8,128)(2,1)}, f32[128,1024]{1,0:T(8,128)S(1)}) custom-call(f32[128,1024]{1,0:T(8,128)S(1)} %get-tuple-element.51.pre_ref, bf16[128,1024]{1,0:T(8,128)(2,1)S(1)} %get-tuple-element.52.fo), custom_call_target="tpu_custom_call" | custom-call | flops 2000000000 | bytes 786432 | tf_op jit(solution)/shard_map/pallas_call | solution.py:349
  22.8 1.4 %collective-permute-done.7.y_odd = bf16[32,1280]{1,0:T(8,128)(2,1)S(1)} collective-permute-done((bf16[32,1280]{1,0:T(8,128)(2,1)S(1)}, bf16[32,1280]{1,0:T(8,128)(2,1)S(1)}, u32[]{:S(2)}, u32[]{:S(2)}) %collective-permute-start.7) | collective-permute-done | bytes 81952 | tf_op jit(solution)/shard_map/ppermute | solution.py:373
  24.1 1.2 %shard_map.99 = (bf16[128,768]{1,0:T(8,128)(2,1)S(1)}, bf16[192,512]{1,0:T(8,128)(2,1)S(1)}, bf16[256,128]{1,0:T(8,128)(2,1)S(1)}, bf16[128,1024]{1,0:T(8,128)(2...) custom-call(bf16[64,768]{1,0:T(8,128)(2,1)S(1)} %get-tuple-element.57.po, ...), custom_call_target="tpu_custom_call" | custom-call | flops 4000000000 | bytes 1843200 | tf_op jit(solution)/shard_map/pallas_call | solution.py:349
  25.3 1.1 %shard_map.102 = f32[176,128]{1,0:T(8,128)S(1)} custom-call(bf16[160,1536]{1,0:T(8,128)(2,1)S(1)} %get-tuple-element.76.x_ref, bf16[128,1024]{1,0:T(8,128)(2,1)S(1)} %get-tuple-element.65.own.fs, bf16[128,768]{1,0:T(8,128)(2,1)S(1)} %get-tuple-element.77.p_ref, bf16[192,512]{1,0:T(8,128)(2,1)S(1)} %get-tuple-element.78.cs), custom_call_target="tpu_custom_call" | custom-call | flops 2000000000 | bytes 1146880 | tf_op jit(solution)/shard_map/pallas_call | solution.py:349
  26.5 2.1 %collective-permute-start.8 = (bf16[128,256]{1,0:T(8,128)(2,1)S(1)}, bf16[128,256]{1,0:T(8,128)(2,1)S(1)}, u32[]{:S(2)}, u32[]{:S(2)}) collective-permute-start(bf16[128,256]{1,0:T(8,128)(2,1)S(1)} %get-tuple-element.66), channel_id=1, source_target_pairs={{0,4},{1,5},{2,6},{3,7},{4,0},{5,1},{6,2},{7,3},{8,12},{9,13},{10,... | collective-permute-start | bytes 196616 | tf_op jit(solution)/shard_map/ppermute | solution.py:373
  28.7 0.1 collective-permute-start.9
  28.8 3.9 %collective-permute-start.15 = (bf16[176,128]{1,0:T(8,128)(2,1)S(1)}, bf16[176,128]{1,0:T(8,128)(2,1)S(1)}, u32[]{:S(2)}, u32[]{:S(2)}) collective-permute-start(bf16[176,128]{1,0:T(8,128)(2,1)S(1)} %add_convert_fusion.1), channel_id=1, source_target_pairs={{0,6},{1,7},{2,4},{3,5},{4,2},{5,3},{6,0},{7,1},{8,14},{9,15},{10,... | collective-permute-start | bytes 135176 | tf_op jit(solution)/shard_map/ppermute | solution.py:381
  32.7 0.3 collective-permute-start.14
  33.0 1.4 %collective-permute-start.13 = (bf16[176,128]{1,0:T(8,128)(2,1)S(1)}, bf16[176,128]{1,0:T(8,128)(2,1)S(1)}, u32[]{:S(2)}, u32[]{:S(2)}) collective-permute-start(bf16[176,128]{1,0:T(8,128)(2,1)S(1)} %add_convert_fusion.1), channel_id=1, source_target_pairs={{0,2},{1,3},{2,0},{3,1},{4,6},{5,7},{6,4},{7,5},{8,10},{9,11},{10,... | collective-permute-start | bytes 135176 | tf_op jit(solution)/shard_map/ppermute | solution.py:381
  34.5 2.1 %collective-permute-start.11 = (bf16[16,1536]{1,0:T(8,128)(2,1)S(1)}, bf16[16,1536]{1,0:T(8,128)(2,1)S(1)}, u32[]{:S(2)}, u32[]{:S(2)}) collective-permute-start(bf16[16,1536]{1,0:T(8,128)(2,1)S(1)} %get-tuple-element.70), channel_id=1, source_target_pairs={{0,4},{1,2},{2,1},{3,7},{4,0},{5,6},{6,5},{7,3},{8,12},{9,10},{10,... | collective-permute-start | bytes 147464 | tf_op jit(solution)/shard_map/ppermute | solution.py:373
  36.6 0.2 collective-permute-done.14
  36.8 0.3 collective-permute-done.13
  37.1 2.8 %collective-permute-start.18 = (bf16[176,128]{1,0:T(8,128)(2,1)S(1)}, bf16[176,128]{1,0:T(8,128)(2,1)S(1)}, u32[]{:S(2)}, u32[]{:S(2)}) collective-permute-start(bf16[176,128]{1,0:T(8,128)(2,1)S(1)} %add_convert_fusion.refs_0_), channel_id=1, source_target_pairs={{0,24},{1,25},{2,26},{3,27},{4,28},{5,29},{6,30},{7,31},{8,16},{9,... | collective-permute-start | bytes 135176 | tf_op jit(solution)/shard_map/ppermute | solution.py:381
  39.9 0.3 collective-permute-start.17
  40.2 1.3 %collective-permute-start.16 = (bf16[176,128]{1,0:T(8,128)(2,1)S(1)}, bf16[176,128]{1,0:T(8,128)(2,1)S(1)}, u32[]{:S(2)}, u32[]{:S(2)}) collective-permute-start(bf16[176,128]{1,0:T(8,128)(2,1)S(1)} %add_convert_fusion.refs_0_), channel_id=1, source_target_pairs={{0,8},{1,9},{2,10},{3,11},{4,12},{5,13},{6,14},{7,15},{8,0},{9,1},... | collective-permute-start | bytes 135176 | tf_op jit(solution)/shard_map/ppermute | solution.py:381
  41.5 2.4 %shard_map.101 = (bf16[16,4,8,256]{3,2,1,0:T(8,128)(2,1)}, bf16[256,128]{1,0:T(8,128)(2,1)}) custom-call(bf16[128,1536]{1,0:T(8,128)(2,1)S(1)} %get-tuple-element.68.fs, bf16[16,1536]{1,0:T(8,128)(2,1)S(1)} %collective-permute-done.10.y_even, bf16[16,1536]{1,0:T(8,128)(2,1)S(1)} %collective-permute-done.11.y_odd, f32[128,1024]{1,0:T(8,128)S(1)} %get-tuple-element.71.fg, ...), custom_call_target="tpu_custom_call" | custom-call | flops 2000000000 | bytes 1449984 | tf_op jit(solution)/shard_map/pallas_call | solution.py:349
  43.9 0.9 %collective-permute-done.17.refs_2_ = bf16[176,128]{1,0:T(8,128)(2,1)S(1)} collective-permute-done((bf16[176,128]{1,0:T(8,128)(2,1)S(1)}, bf16[176,128]{1,0:T(8,128)(2,1)S(1)}, u32[]{:S(2)}, u32[]{:S(2)}) %collective-permute-start.17) | collective-permute-done | bytes 45088 | tf_op jit(solution)/shard_map/ppermute | solution.py:381
  44.8 0.1 collective-permute-done.16.refs_1_
  44.9 1.0 %shard_map.103 = (f32[27,16,16]{2,1,0:T(8,128)}, f32[27,16,32]{2,1,0:T(8,128)}) custom-call(bf16[176,128]{1,0:T(8,128)(2,1)S(1)} %add_convert_fusion.refs_0_, bf16[176,128]{1,0:T(8,128)(2,1)S(1)} %collective-permute-done.16.refs_1_, bf16[176,128]{1,0:T(8,128)(2,1)S(1)} %collective-permute-done.17.refs_2_, bf16[176,128]{1,0:T(8,128)(2,1)S(1)} %collective-permute-done.18.refs_3_), custom_call_target="tpu_custom_call" | custom-call | flops 10000000 | bytes 180224 | tf_op jit(solution)/shard_map/pallas_call | solution.py:349
  (30 shorter events, 0.5 us)
Async XLA Ops:
  0.6 1.0 %copy-start = (bf16[16,4,8,256]{3,2,1,0:T(8,128)(2,1)S(1)}, bf16[16,4,8,256]{3,2,1,0:T(8,128)(2,1)}, u32[]{:S(2)}) copy-start(bf16[16,4,8,256]{3,2,1,0:T(8,128)(2,1)} %vol.1) | copy-start | bytes 786436
  1.8 6.1 %collective-permute-start = (bf16[128,256]{1,0:T(8,128)(2,1)S(1)}, bf16[128,256]{1,0:T(8,128)(2,1)S(1)}, u32[]{:S(2)}, u32[]{:S(2)}) collective-permute-start(bf16[128,256]{1,0:T(8,128)(2,1)S(1)} %get-tuple-element.44), channel_id=1, source_target_pairs={{0,4},{1,5},{2,6},{3,7},{4,0},{5,1},{6,2},{7,3},{8,12},{9,13},{10,... | collective-permute-start | bytes 196616 | tf_op jit(solution)/shard_map/ppermute | solution.py:373
  4.8 3.1 %collective-permute-start.1 = (bf16[128,256]{1,0:T(8,128)(2,1)S(1)}, bf16[128,256]{1,0:T(8,128)(2,1)S(1)}, u32[]{:S(2)}, u32[]{:S(2)}) collective-permute-start(bf16[128,256]{1,0:T(8,128)(2,1)S(1)} %get-tuple-element.45), channel_id=1, source_target_pairs={{0,1},{1,0},{2,3},{3,2},{4,8},{5,9},{6,10},{7,11},{8,4},{9,5},{10,... | collective-permute-start | bytes 196616 | tf_op jit(solution)/shard_map/ppermute | solution.py:373
  7.9 2.6 %copy-start.2 = (bf16[3,3,3,16,16]{4,3,2,1,0:T(8,128)(2,1)S(1)}, bf16[3,3,3,16,16]{4,3,2,1,0:T(8,128)(2,1)}, u32[]{:S(2)}) copy-start(bf16[3,3,3,16,16]{4,3,2,1,0:T(8,128)(2,1)} %param.6) | copy-start | bytes 41476
  7.9 2.6 %copy-start.3 = (bf16[3,3,3,32,16]{3,4,2,1,0:T(8,128)(2,1)S(1)}, bf16[3,3,3,32,16]{3,4,2,1,0:T(8,128)(2,1)}, u32[]{:S(2)}) copy-start(bf16[3,3,3,32,16]{3,4,2,1,0:T(8,128)(2,1)} %param.7) | copy-start | bytes 82948
  8.0 3.8 %collective-permute-start.2 = (bf16[16,1536]{1,0:T(8,128)(2,1)S(1)}, bf16[16,1536]{1,0:T(8,128)(2,1)S(1)}, u32[]{:S(2)}, u32[]{:S(2)}) collective-permute-start(bf16[16,1536]{1,0:T(8,128)(2,1)S(1)} %get-tuple-element.47), channel_id=1, source_target_pairs={{0,1},{1,0},{2,3},{3,2},{4,5},{5,4},{6,7},{7,6},{8,9},{9,8},{10,11... | collective-permute-start | bytes 147464 | tf_op jit(solution)/shard_map/ppermute | solution.py:373
  8.1 4.6 %collective-permute-start.3 = (bf16[16,1536]{1,0:T(8,128)(2,1)S(1)}, bf16[16,1536]{1,0:T(8,128)(2,1)S(1)}, u32[]{:S(2)}, u32[]{:S(2)}) collective-permute-start(bf16[16,1536]{1,0:T(8,128)(2,1)S(1)} %get-tuple-element.48), channel_id=1, source_target_pairs={{0,4},{1,2},{2,1},{3,7},{4,0},{5,6},{6,5},{7,3},{8,12},{9,10},{10,... | collective-permute-start | bytes 147464 | tf_op jit(solution)/shard_map/ppermute | solution.py:373
  10.6 1.0 %copy-start.1 = (bf16[16,4,8,256]{3,2,1,0:T(8,128)(2,1)S(1)}, bf16[16,4,8,256]{3,2,1,0:T(8,128)(2,1)}, u32[]{:S(2)}) copy-start(bf16[16,4,8,256]{3,2,1,0:T(8,128)(2,1)} %fc.1) | copy-start | bytes 786436
  10.6 1.0 %copy-start.4 = (bf16[32,2,4,128]{3,2,1,0:T(4,128)(2,1)S(1)}, bf16[32,2,4,128]{3,2,1,0:T(4,128)(2,1)}, u32[]{:S(2)}) copy-start(bf16[32,2,4,128]{3,2,1,0:T(4,128)(2,1)} %param.9) | copy-start | bytes 196612
  13.7 5.3 %collective-permute-start.4 = (bf16[64,512]{1,0:T(8,128)(2,1)S(1)}, bf16[64,512]{1,0:T(8,128)(2,1)S(1)}, u32[]{:S(2)}, u32[]{:S(2)}) collective-permute-start(bf16[64,512]{1,0:T(8,128)(2,1)S(1)} %get-tuple-element.55), channel_id=1, source_target_pairs={{0,4},{1,5},{2,6},{3,7},{4,0},{5,1},{6,2},{7,3},{8,12},{9,13},{10,... | collective-permute-start | bytes 196616 | tf_op jit(solution)/shard_map/ppermute | solution.py:373
  15.8 3.2 %collective-permute-start.5 = (bf16[64,512]{1,0:T(8,128)(2,1)S(1)}, bf16[64,512]{1,0:T(8,128)(2,1)S(1)}, u32[]{:S(2)}, u32[]{:S(2)}) collective-permute-start(bf16[64,512]{1,0:T(8,128)(2,1)S(1)} %get-tuple-element.56), channel_id=1, source_target_pairs={{0,1},{1,0},{2,3},{3,2},{4,8},{5,9},{6,10},{7,11},{8,4},{9,5},{10,... | collective-permute-start | bytes 196616 | tf_op jit(solution)/shard_map/ppermute | solution.py:373
  19.1 3.7 %collective-permute-start.6 = (bf16[32,1280]{1,0:T(8,128)(2,1)S(1)}, bf16[32,1280]{1,0:T(8,128)(2,1)S(1)}, u32[]{:S(2)}, u32[]{:S(2)}) collective-permute-start(bf16[32,1280]{1,0:T(8,128)(2,1)S(1)} %get-tuple-element.59), channel_id=1, source_target_pairs={{0,1},{1,0},{2,3},{3,2},{4,5},{5,4},{6,7},{7,6},{8,9},{9,8},{10,11... | collective-permute-start | bytes 245768 | tf_op jit(solution)/shard_map/ppermute | solution.py:373
  19.2 4.9 %collective-permute-start.7 = (bf16[32,1280]{1,0:T(8,128)(2,1)S(1)}, bf16[32,1280]{1,0:T(8,128)(2,1)S(1)}, u32[]{:S(2)}, u32[]{:S(2)}) collective-permute-start(bf16[32,1280]{1,0:T(8,128)(2,1)S(1)} %get-tuple-element.60), channel_id=1, source_target_pairs={{0,4},{1,2},{2,1},{3,7},{4,0},{5,6},{6,5},{7,3},{8,12},{9,10},{10,... | collective-permute-start | bytes 245768 | tf_op jit(solution)/shard_map/ppermute | solution.py:373
  26.5 2.3 %collective-permute-start.12 = (f32[176,128]{1,0:T(8,128)S(1)}, f32[176,128]{1,0:T(8,128)S(1)}, u32[]{:S(2)}, u32[]{:S(2)}) collective-permute-start(f32[176,128]{1,0:T(8,128)S(1)} %shard_map.102), channel_id=1, source_target_pairs={{0,1},{1,0},{2,3},{3,2},{4,5},{5,4},{6,7},{7,6},{8,9},{9,8},{10,11... | collective-permute-start | bytes 270344 | tf_op jit(solution)/shard_map/ppermute | solution.py:381
  26.5 7.8 %collective-permute-start.8 = (bf16[128,256]{1,0:T(8,128)(2,1)S(1)}, bf16[128,256]{1,0:T(8,128)(2,1)S(1)}, u32[]{:S(2)}, u32[]{:S(2)}) collective-permute-start(bf16[128,256]{1,0:T(8,128)(2,1)S(1)} %get-tuple-element.66), channel_id=1, source_target_pairs={{0,4},{1,5},{2,6},{3,7},{4,0},{5,1},{6,2},{7,3},{8,12},{9,13},{10,... | collective-permute-start | bytes 196616 | tf_op jit(solution)/shard_map/ppermute | solution.py:373
  28.7 5.7 %collective-permute-start.9 = (bf16[128,256]{1,0:T(8,128)(2,1)S(1)}, bf16[128,256]{1,0:T(8,128)(2,1)S(1)}, u32[]{:S(2)}, u32[]{:S(2)}) collective-permute-start(bf16[128,256]{1,0:T(8,128)(2,1)S(1)} %get-tuple-element.67), channel_id=1, source_target_pairs={{0,1},{1,0},{2,3},{3,2},{4,8},{5,9},{6,10},{7,11},{8,4},{9,5},{10,... | collective-permute-start | bytes 196616 | tf_op jit(solution)/shard_map/ppermute | solution.py:373
  28.8 7.8 %collective-permute-start.15 = (bf16[176,128]{1,0:T(8,128)(2,1)S(1)}, bf16[176,128]{1,0:T(8,128)(2,1)S(1)}, u32[]{:S(2)}, u32[]{:S(2)}) collective-permute-start(bf16[176,128]{1,0:T(8,128)(2,1)S(1)} %add_convert_fusion.1), channel_id=1, source_target_pairs={{0,6},{1,7},{2,4},{3,5},{4,2},{5,3},{6,0},{7,1},{8,14},{9,15},{10,... | collective-permute-start | bytes 135176 | tf_op jit(solution)/shard_map/ppermute | solution.py:381
  32.7 4.0 %collective-permute-start.14 = (bf16[176,128]{1,0:T(8,128)(2,1)S(1)}, bf16[176,128]{1,0:T(8,128)(2,1)S(1)}, u32[]{:S(2)}, u32[]{:S(2)}) collective-permute-start(bf16[176,128]{1,0:T(8,128)(2,1)S(1)} %add_convert_fusion.1), channel_id=1, source_target_pairs={{0,4},{1,5},{2,6},{3,7},{4,0},{5,1},{6,2},{7,3},{8,12},{9,13},{10,... | collective-permute-start | bytes 135176 | tf_op jit(solution)/shard_map/ppermute | solution.py:381
  33.0 4.0 %collective-permute-start.13 = (bf16[176,128]{1,0:T(8,128)(2,1)S(1)}, bf16[176,128]{1,0:T(8,128)(2,1)S(1)}, u32[]{:S(2)}, u32[]{:S(2)}) collective-permute-start(bf16[176,128]{1,0:T(8,128)(2,1)S(1)} %add_convert_fusion.1), channel_id=1, source_target_pairs={{0,2},{1,3},{2,0},{3,1},{4,6},{5,7},{6,4},{7,5},{8,10},{9,11},{10,... | collective-permute-start | bytes 135176 | tf_op jit(solution)/shard_map/ppermute | solution.py:381
  34.4 7.1 %collective-permute-start.10 = (bf16[16,1536]{1,0:T(8,128)(2,1)S(1)}, bf16[16,1536]{1,0:T(8,128)(2,1)S(1)}, u32[]{:S(2)}, u32[]{:S(2)}) collective-permute-start(bf16[16,1536]{1,0:T(8,128)(2,1)S(1)} %get-tuple-element.69), channel_id=1, source_target_pairs={{0,1},{1,0},{2,3},{3,2},{4,5},{5,4},{6,7},{7,6},{8,9},{9,8},{10,11... | collective-permute-start | bytes 147464 | tf_op jit(solution)/shard_map/ppermute | solution.py:373
  34.5 7.0 %collective-permute-start.11 = (bf16[16,1536]{1,0:T(8,128)(2,1)S(1)}, bf16[16,1536]{1,0:T(8,128)(2,1)S(1)}, u32[]{:S(2)}, u32[]{:S(2)}) collective-permute-start(bf16[16,1536]{1,0:T(8,128)(2,1)S(1)} %get-tuple-element.70), channel_id=1, source_target_pairs={{0,4},{1,2},{2,1},{3,7},{4,0},{5,6},{6,5},{7,3},{8,12},{9,10},{10,... | collective-permute-start | bytes 147464 | tf_op jit(solution)/shard_map/ppermute | solution.py:373
  37.1 6.8 %collective-permute-start.18 = (bf16[176,128]{1,0:T(8,128)(2,1)S(1)}, bf16[176,128]{1,0:T(8,128)(2,1)S(1)}, u32[]{:S(2)}, u32[]{:S(2)}) collective-permute-start(bf16[176,128]{1,0:T(8,128)(2,1)S(1)} %add_convert_fusion.refs_0_), channel_id=1, source_target_pairs={{0,24},{1,25},{2,26},{3,27},{4,28},{5,29},{6,30},{7,31},{8,16},{9,... | collective-permute-start | bytes 135176 | tf_op jit(solution)/shard_map/ppermute | solution.py:381
  39.9 4.9 %collective-permute-start.17 = (bf16[176,128]{1,0:T(8,128)(2,1)S(1)}, bf16[176,128]{1,0:T(8,128)(2,1)S(1)}, u32[]{:S(2)}, u32[]{:S(2)}) collective-permute-start(bf16[176,128]{1,0:T(8,128)(2,1)S(1)} %add_convert_fusion.refs_0_), channel_id=1, source_target_pairs={{0,16},{1,17},{2,18},{3,19},{4,20},{5,21},{6,22},{7,23},{8,24},{9,... | collective-permute-start | bytes 135176 | tf_op jit(solution)/shard_map/ppermute | solution.py:381
  40.2 4.8 %collective-permute-start.16 = (bf16[176,128]{1,0:T(8,128)(2,1)S(1)}, bf16[176,128]{1,0:T(8,128)(2,1)S(1)}, u32[]{:S(2)}, u32[]{:S(2)}) collective-permute-start(bf16[176,128]{1,0:T(8,128)(2,1)S(1)} %add_convert_fusion.refs_0_), channel_id=1, source_target_pairs={{0,8},{1,9},{2,10},{3,11},{4,12},{5,13},{6,14},{7,15},{8,0},{9,1},... | collective-permute-start | bytes 135176 | tf_op jit(solution)/shard_map/ppermute | solution.py:381

commit v4 on v3

--- a/solution.py
+++ b/solution.py
@@ -53,9 +53,9 @@
     return values.astype(F32).reshape(chans * rows, width).astype(BF16)
 
 
-def band(taps_ref, out_ref, out_rows, turned, flipped):
+def band(taps_ref, out_ref, out_rows, in_rows, shift, turned, flipped):
     m, n = taps_ref.shape[1:][::-1] if turned else taps_ref.shape[1:]
-    wide = (out_rows + 2) * n
+    wide = in_rows * n
     spread = one_hot((n, wide), lambda r, c: c % n == r)
     block = lax.broadcasted_iota(jnp.int32, (m, wide), 1) // n
     if turned:
@@ -74,20 +74,24 @@
         for c in range(3):
             taps = [tiled[(a * 3 + b) * 3 + c] for b in range(3)]
             for y in range(out_rows):
-                value = jnp.where(
-                    block == y,
-                    taps[0],
-                    jnp.where(block == y + 1, taps[1], jnp.where(block == y + 2, taps[2], 0.0)),
-                )
+                value = jnp.zeros((m, wide), F32)
+                for b in range(3):
+                    if 0 <= y + b - shift < in_rows:
+                        value = jnp.where(block == y + b - shift, taps[b], value)
                 start = (c * out_rows + y) * m
                 out_ref[start : start + m, a * wide : (a + 1) * wide] = value.astype(BF16)
 
 
-def weights_kernel(kf, kc, wa, wt, wc, wct, *, ny):
-    band(kf, wa, ny, False, False)
-    band(kf, wt, ny, True, True)
-    band(kc, wc, ny // 2 + 2, True, False)
-    band(kc, wct, ny // 2, False, True)
+def weights_kernel(kf, kc, wa, wl, wh, wt, wc, wcl, wch, wct, *, ny):
+    hy = ny // 2
+    band(kf, wa, ny, ny, 1, False, False)
+    band(kf, wl, 1, 1, 0, False, False)
+    band(kf, wh, 1, 1, 2, False, False)
+    band(kc, wc, hy + 2, hy, 2, True, False)
+    band(kc, wcl, 2, 2, 0, True, False)
+    band(kc, wch, 2, 2, 2, True, False)
+    band(kf, wt, ny, ny + 2, 0, True, True)
+    band(kc, wct, hy, hy + 2, 0, False, True)
 
 
 def ends():
@@ -178,31 +182,63 @@
     )
 
 
-def fine_kernel_fn(xo, y_even, y_odd, wa, co, x_ref, pre_out, fo_out, po, z_even, z_odd, *, nz, nx):
+def neighbours(even, odd, axis):
+    first = ends()[0 if axis == "gx" else 1]
+    odd = from_odd(odd, axis)
+    return jnp.where(first, odd, even), jnp.where(first, even, odd)
+
+
+def all_layers(values, count, step):
+    return jnp.concatenate([values[:, dz * step : (dz + count) * step] for dz in range(3)], axis=0)
+
+
+def fine_inner_kernel(xo, wa, pre_out, fo_out, sums_out, *, c1, nz, nx):
+    half = nx // 2
+    pool = one_hot((nx, half), lambda r, c: r // 2 == c)
+    inner = slice(c1, xo.shape[0] - c1)
+    for layer in range(nz):
+        pre = combine(mm(wa[...], three_layers(xo, slice(None), layer * nx, nx, nx)), nx)
+        span = slice(layer * nx, (layer + 1) * nx)
+        pre_out[:, span] = pre
+        pre = pre[inner]
+        value = xo[inner, (layer + 1) * nx : (layer + 2) * nx].astype(F32)
+        fo = (value + pre * jax.nn.sigmoid(pre)).astype(BF16)
+        fo_out[:, span] = fo
+        pooled = mm(fo, pool)
+        sums = pooled if layer % 2 == 0 else sums + pooled
+        if layer % 2:
+            sums_out[:, layer // 2 * half : (layer // 2 + 1) * half] = sums
+
+
+def fine_edge_kernel(
+    xo, y_even, y_odd, wl, wh, pre_ref, sums, co, pre_out, fo_out, po, z_even, z_odd, *, nz, nx
+):
     c1 = y_even.shape[0]
     half = nx // 2
-    stack_rows(x_ref, xo, y_even, y_odd)
+    rows = xo.shape[0]
+    low, high = neighbours(y_even[...], y_odd[...], "gy")
+    last = slice(rows - c1, rows)
+    pre = jnp.concatenate(
+        [
+            pre_ref[:c1] + combine(mm(wl[...], all_layers(low, nz, nx)), nx),
+            pre_ref[last] + combine(mm(wh[...], all_layers(high, nz, nx)), nx),
+        ],
+        axis=0,
+    )
+    pre_out[...] = pre
+    own = slice(nx, (nz + 1) * nx)
+    value = jnp.concatenate([xo[:c1, own], xo[last, own]], axis=0).astype(F32)
+    fo = (value + pre * jax.nn.sigmoid(pre)).astype(BF16)
+    fo_out[...] = fo
     pool = one_hot((nx, half), lambda r, c: r // 2 == c)
-    rows = xo.shape[0]
-    for layer in range(nz):
-        parts = mm(wa[...], three_layers(x_ref, slice(None), layer * nx, nx, nx))
-        pre = combine(parts, nx)
-        pre_out[:, layer * nx : (layer + 1) * nx] = pre
-        value = xo[:, (layer + 1) * nx : (layer + 2) * nx].astype(F32)
-        fo = (value + pre * jax.nn.sigmoid(pre)).astype(BF16)
-        fo_out[:, layer * nx : (layer + 1) * nx] = fo
-        pooled = mm(fo, pool)
-        if layer % 2 == 0:
-            sums = pooled
-            continue
-        sums = sums + pooled
-        cells = [
-            sums[2 * r * c1 : (2 * r + 1) * c1] + sums[(2 * r + 1) * c1 : (2 * r + 2) * c1]
-            for r in range(rows // c1 // 2)
-        ]
-        place = layer // 2
-        value = jnp.concatenate(cells, axis=0) * 0.125
-        po[:, place * half : (place + 1) * half] = value.astype(BF16)
+    for place in range(nz // 2):
+        first = 2 * place * nx
+        pooled = mm(fo[:, first : first + nx], pool) + mm(fo[:, first + nx : first + 2 * nx], pool)
+        span = slice(place * half, (place + 1) * half)
+        cells = [pooled[:c1]] + [sums[r * c1 : (r + 1) * c1, span] for r in range(rows // c1 - 2)]
+        cells.append(pooled[c1:])
+        cells = [cells[r] + cells[r + 1] for r in range(0, len(cells), 2)]
+        po[:, span] = (jnp.concatenate(cells, axis=0) * 0.125).astype(BF16)
     lanes = po.shape[1]
     low, high = co[:, :half], co[:, co.shape[1] - half :]
     first = ends()[0]
@@ -215,36 +251,55 @@
         ref[:, lanes + half :] = value[rows // 2 :]
 
 
-def slope_kernel_fn(pre_ref, fo, fo_out, sl_out, *, c1, nz, ny, nx):
+def slope_kernel_fn(
+    xo, y_even, y_odd, pre_ref, pre_edge, fo, fo_edge, fo_out, sl_out, x_ref, *, c1, nz, ny, nx
+):
+    stack_rows(x_ref, xo, y_even, y_odd)
     swap_back = swap_matrix(c1, ny)
     for layer in range(nz):
         span = slice(layer * nx, (layer + 1) * nx)
-        pre = pre_ref[:, span]
+        pre = jnp.concatenate(
+            [pre_edge[:c1, span], pre_ref[c1 : c1 * (ny - 1), span], pre_edge[c1:, span]], axis=0
+        )
         sig = jax.nn.sigmoid(pre)
         sl_out[:, span] = sig * (1.0 + pre * (1.0 - sig))
-        rows = mm(swap_back, fo[:, span])
-        fo_out[:, layer] = rows.reshape(c1, ny, nx).astype(BF16)
+        rows = jnp.concatenate([fo_edge[:c1, span], fo[:, span], fo_edge[c1:, span]], axis=0)
+        fo_out[:, layer] = mm(swap_back, rows).reshape(c1, ny, nx).astype(BF16)
+
+
+def coarse_inner_kernel(po, wc, pre_out, *, count, half):
+    for pair in range(count // 2):
+        parts = mm(wc[...], three_layers(po, slice(None), pair * 2 * half, half, 2 * half))
+        pre_out[:, pair * 2 * half : (pair + 1) * 2 * half] = combine(parts, half)
 
 
 def coarse_kernel_fn(
-    po, cc, y_even, y_odd, fc, sl, wc, wct,
-    p_ref, cs_ref, co_out, fs_out, fg_out, z_even, z_odd, c_ref, *, c1, c2, nz, ny, nx,
+    po, cc, y_even, y_odd, fc, sl, pre_ref, wcl, wch, wct,
+    p_ref, cs_ref, co_out, fs_out, fg_out, z_even, z_odd, *, c1, c2, nz, ny, nx,
 ):
     half, hz, hy = nx // 2, nz // 2, ny // 2
     pooled = po.shape[1]
-    stack_rows(p_ref, po, y_even.at[:, :pooled], y_odd.at[:, :pooled])
-    stack_rows(c_ref, cc, y_even.at[:, pooled:], y_odd.at[:, pooled:])
+    low, high = neighbours(y_even[...], y_odd[...], "gy")
+    edge = low.shape[0]
+    p_ref[:edge] = low[:, :pooled]
+    p_ref[edge : edge + po.shape[0]] = po[...]
+    p_ref[edge + po.shape[0] :] = high[:, :pooled]
+    count = hz + 2
+    pre = jnp.concatenate(
+        [
+            combine(mm(wcl[...], all_layers(low[:, :pooled], count, half)), half),
+            jnp.zeros(((hy - 2) * c2, count * half), F32),
+            combine(mm(wch[...], all_layers(high[:, :pooled], count, half)), half),
+        ],
+        axis=0,
+    )
+    pre = pre + pre_ref[...]
+    sig = jax.nn.sigmoid(pre)
+    cot = jnp.concatenate([low[:, pooled:], cc[...], high[:, pooled:]], axis=0).astype(F32)
+    cs_ref[...] = (cot * (sig * (1.0 + pre * (1.0 - sig)))).astype(BF16)
     inner = slice(c2, c2 + hy * c2)
-    own = []
-    for pair in range((hz + 2) // 2):
-        pre = combine(mm(wc[...], three_layers(p_ref, slice(None), pair * nx, half, nx)), half)
-        sig = jax.nn.sigmoid(pre)
-        span = slice(pair * nx, (pair + 1) * nx)
-        cot = c_ref[:, span].astype(F32)
-        cs_ref[:, span] = (cot * (sig * (1.0 + pre * (1.0 - sig)))).astype(BF16)
-        out = (pre[inner] * sig[inner]).astype(BF16)
-        own += [out[:, :half], out[:, half:]]
-    stacked = jnp.concatenate(own[1:-1], axis=0)
+    out = (pre[inner, half:-half] * sig[inner, half:-half]).astype(BF16)
+    stacked = jnp.concatenate([out[:, z * half : (z + 1) * half] for z in range(hz)], axis=0)
     co_out[...] = mm(swap_matrix(c2, hz * hy), stacked).astype(BF16)
     widen = one_hot((half, nx), lambda r, c: c // 2 == r)
     for pair in range(hz // 2):
@@ -397,12 +452,16 @@
         flops=10**8,
     )
     z_even, z_odd = swap_pairs(z_even, z_odd, "gx")
-    wa, wt, wc, wct = call(
+    wa, wl, wh, wt, wc, wcl, wch, wct = call(
         functools.partial(weights_kernel, ny=ny),
         shapes(
+            ((3 * ny * c1, 3 * ny * c1), BF16),
+            ((3 * c1, 3 * c1), BF16),
+            ((3 * c1, 3 * c1), BF16),
             ((3 * ny * c1, 3 * (ny + 2) * c1), BF16),
-            ((3 * ny * c1, 3 * (ny + 2) * c1), BF16),
-            ((3 * (hy + 2) * c2, 3 * (hy + 4) * c1), BF16),
+            ((3 * (hy + 2) * c2, 3 * hy * c1), BF16),
+            ((6 * c2, 6 * c1), BF16),
+            ((6 * c2, 6 * c1), BF16),
             ((3 * hy * c1, 3 * (hy + 2) * c2), BF16),
         ),
         [
@@ -423,25 +482,35 @@
     own, y_even, y_odd = call(layers_kernel, stacked, [own, z_even, z_odd], flops=10**8)
     y_even, y_odd = swap_pairs(y_even, y_odd, "gy")
 
+    pre, fine_rows, sums = call(
+        functools.partial(fine_inner_kernel, c1=c1, nz=nz, nx=nx),
+        shapes(
+            ((rows, nz * nx), F32),
+            ((rows - 2 * c1, nz * nx), BF16),
+            ((rows - 2 * c1, hz * half), F32),
+        ),
+        [own, wa],
+        flops=3 * 10**9,
+    )
     sent = (half_rows, hz * half + 2 * half)
-    volume_rows, pre, fine_rows, pooled, z_even, z_odd = call(
-        functools.partial(fine_kernel_fn, nz=nz, nx=nx),
+    pre_edge, fine_edge, pooled, z_even, z_odd = call(
+        functools.partial(fine_edge_kernel, nz=nz, nx=nx),
         shapes(
-            ((rows + 2 * c1, layers), BF16),
-            ((rows, nz * nx), F32),
-            ((rows, nz * nx), BF16),
+            ((2 * c1, nz * nx), F32),
+            ((2 * c1, nz * nx), BF16),
             ((half_rows, hz * half), BF16),
             (sent, BF16),
             (sent, BF16),
         ),
-        [own, y_even, y_odd, wa, coarse_cot],
-        flops=3 * 10**9,
+        [own, y_even, y_odd, wl, wh, pre, sums, coarse_cot],
+        flops=10**9,
     )
     z_even, z_odd = swap_pairs(z_even, z_odd, "gx")
-    fine_out, slopes = call(
+    fine_out, slopes, volume_rows = call(
         functools.partial(slope_kernel_fn, **sizes),
-        [result((c1, nz, ny, nx), BF16)] + shapes(((rows, nz * nx), F32)),
-        [pre, fine_rows],
+        [result((c1, nz, ny, nx), BF16)]
+        + shapes(((rows, nz * nx), F32), ((rows + 2 * c1, layers), BF16)),
+        [own, y_even, y_odd, pre, pre_edge, fine_rows, fine_edge],
         flops=2 * 10**9,
     )
     pooled_lanes = 3 * hz * half
@@ -459,6 +528,12 @@
         flops=10**8,
     )
     y_even, y_odd = swap_pairs(y_even, y_odd, "gy")
+    (pre,) = call(
+        functools.partial(coarse_inner_kernel, count=hz + 2, half=half),
+        shapes((((hy + 2) * c2, cot_lanes), F32)),
+        [pooled, wc],
+        flops=2 * 10**9,
+    )
 
     pooled, coarse_slope, coarse_out, fslope, fgrad, z_even, z_odd = call(
         functools.partial(coarse_kernel_fn, c2=c2, **sizes),
@@ -471,9 +546,8 @@
             ((rows, nx), BF16),
             ((rows, nx), BF16),
         ),
-        [pooled, coarse_cot, y_even, y_odd, fine_cot, slopes, wc, wct],
+        [pooled, coarse_cot, y_even, y_odd, fine_cot, slopes, pre, wcl, wch, wct],
         flops=4 * 10**9,
-        scratch=[pltpu.VMEM(((hy + 2) * c2, cot_lanes), BF16)],
     )
     z_even, z_odd = swap_pairs(z_even, z_odd, "gx")
     (terms,) = call(

time: 46.1 us -> 45.2 us (0.980)
  waiting for transfers between devices: 10 us -> 7.97 us
  local copies, waits for them, and re-layouts: 1.04 us -> 1.63 us
  Pallas kernels: 9.27 us -> 9.79 us
    ppermute x12, waiting for transfers between devices: 8.53 us -> 6.47 us  [swap_pairs(): out.append(lax.ppermute(value, ('gx', 'gy'), pairs))]
    unnamed x10, local copies, waits for them, and re-layouts: 1.04 us -> 1.63 us
    pallas_call x12 -> x14, Pallas kernels: 9.27 us -> 9.79 us  [call(): pl.pallas_call(body, out_shape=outs, in_specs=specs, out_specs=[pl.BlockS...]
  transfers between devices with their start and end apart: 19 -> 19, of which waited for: 8 -> 8; matrix products, arithmetic and copies ran while one was open for 0% -> 0% of each run, Pallas kernels for 10% -> 13%
where the time goes in v4:
time: 45.2 us; the launch traced here: 45 us
  starting transfers between devices  24.8 us (55%)
  Pallas kernels  9.79 us (22%)
  waiting for transfers between devices  7.97 us (18%)
  local copies, waits for them, and re-layouts  1.63 us (4%)
  between operations  0.8 us (2%)
    ppermute x12, starting transfers between devices, swap_pairs(): out.append(lax.ppermute(value, ('gx', 'gy'), pairs))  14.7 us
    ppermute x7, starting transfers between devices, swap_bits(): lax.ppermute(value, ('gx', 'gy'), [(i, i ^ flip) for i in range(count)])  10.1 us
    pallas_call x14, Pallas kernels, call(): pl.pallas_call(body, out_shape=outs, in_specs=specs, out_specs=[pl.BlockS...  9.79 us
    ppermute x12, waiting for transfers between devices, swap_pairs(): out.append(lax.ppermute(value, ('gx', 'gy'), pairs))  6.47 us
    unnamed x10, local copies, waits for them, and re-layouts  1.63 us
    ppermute x7, waiting for transfers between devices, swap_bits(): lax.ppermute(value, ('gx', 'gy'), [(i, i ^ flip) for i in range(count)])  1.5 us
  transfers between devices with their start and end apart: 19, of which 8 were waited for; matrix products, arithmetic and copies ran while one was open for 0% of the time, Pallas kernels for 13%

profile of v4, /device:TPU:0, one launch (start us, length us, event | category | flops | bytes accessed | tf_op | source)
XLA Modules:
  0.0 45.0 jit_solution(11210286664581441557)
XLA Ops:
  0.6 0.9 %copy-done = bf16[16,4,8,256]{3,2,1,0:T(8,128)(2,1)S(1)} copy-done((bf16[16,4,8,256]{3,2,1,0:T(8,128)(2,1)S(1)}, bf16[16,4,8,256]{3,2,1,0:T(8,128)(2,1)}, u32[]{:S(2)}) %copy-start) | copy-done | bytes 262168
  1.6 0.2 shard_map.92
  1.8 3.0 %collective-permute-start = (bf16[128,256]{1,0:T(8,128)(2,1)S(1)}, bf16[128,256]{1,0:T(8,128)(2,1)S(1)}, u32[]{:S(2)}, u32[]{:S(2)}) collective-permute-start(bf16[128,256]{1,0:T(8,128)(2,1)S(1)} %get-tuple-element.51), channel_id=1, source_target_pairs={{0,4},{1,5},{2,6},{3,7},{4,0},{5,1},{6,2},{7,3},{8,12},{9,13},{10,... | collective-permute-start | bytes 196616 | tf_op jit(solution)/shard_map/ppermute | solution.py:428
  4.9 0.3 shard_map.96
  5.1 0.6 %copy-done.2 = bf16[3,3,3,16,16]{4,3,2,1,0:T(8,128)(2,1)S(1)} copy-done((bf16[3,3,3,16,16]{4,3,2,1,0:T(8,128)(2,1)S(1)}, bf16[3,3,3,16,16]{4,3,2,1,0:T(8,128)(2,1)}, u32[]{:S(2)}) %copy-start.2) | copy-done | bytes 13848
  5.8 0.9 %shard_map.94 = (bf16[384,384]{1,0:T(8,128)(2,1)S(1)}, bf16[48,48]{1,0:T(8,128)(2,1)S(1)}, bf16[48,48]{1,0:T(8,128)(2,1)S(1)}, bf16[384,480]{1,0:T(8,128)(2,1)S(...) custom-call(bf16[27,16,16]{2,1,0:T(8,128)(2,1)S(1)} %bitcast.10, ...), custom_call_target="tpu_custom_call" | custom-call | flops 1000000000 | bytes 41472 | tf_op jit(solution)/shard_map/pallas_call | solution.py:404
  6.7 1.3 %collective-permute-done.z_even = bf16[128,256]{1,0:T(8,128)(2,1)S(1)} collective-permute-done((bf16[128,256]{1,0:T(8,128)(2,1)S(1)}, bf16[128,256]{1,0:T(8,128)(2,1)S(1)}, u32[]{:S(2)}, u32[]{:S(2)}) %collective-permute-start) | collective-permute-done | bytes 65568 | tf_op jit(solution)/shard_map/ppermute | solution.py:428
  8.1 2.5 %collective-permute-start.3 = (bf16[16,1536]{1,0:T(8,128)(2,1)S(1)}, bf16[16,1536]{1,0:T(8,128)(2,1)S(1)}, u32[]{:S(2)}, u32[]{:S(2)}) collective-permute-start(bf16[16,1536]{1,0:T(8,128)(2,1)S(1)} %get-tuple-element.55), channel_id=1, source_target_pairs={{0,4},{1,2},{2,1},{3,7},{4,0},{5,6},{6,5},{7,3},{8,12},{9,10},{10,... | collective-permute-start | bytes 147464 | tf_op jit(solution)/shard_map/ppermute | solution.py:428
  10.6 1.0 %shard_map.95 = (f32[128,1024]{1,0:T(8,128)S(1)}, bf16[96,1024]{1,0:T(8,128)(2,1)S(1)}, f32[96,256]{1,0:T(8,128)S(1)}) custom-call(bf16[128,1536]{1,0:T(8,128)(2,1)S(1)} %get-tuple-element.53.xo, bf16[384,384]{1,0:T(8,128)(2,1)S(1)} %get-tuple-element.56.wa), custom_call_target="tpu_custom_call" | custom-call | flops 3000000000 | bytes 688128 | tf_op jit(solution)/shard_map/pallas_call | solution.py:404
  11.6 1.0 %collective-permute-done.3.y_odd = bf16[16,1536]{1,0:T(8,128)(2,1)S(1)} collective-permute-done((bf16[16,1536]{1,0:T(8,128)(2,1)S(1)}, bf16[16,1536]{1,0:T(8,128)(2,1)S(1)}, u32[]{:S(2)}, u32[]{:S(2)}) %collective-permute-start.3) | collective-permute-done | bytes 49184 | tf_op jit(solution)/shard_map/ppermute | solution.py:428
  12.7 0.4 shard_map.97
  13.1 2.1 %collective-permute-start.4 = (bf16[64,512]{1,0:T(8,128)(2,1)S(1)}, bf16[64,512]{1,0:T(8,128)(2,1)S(1)}, u32[]{:S(2)}, u32[]{:S(2)}) collective-permute-start(bf16[64,512]{1,0:T(8,128)(2,1)S(1)} %get-tuple-element.67), channel_id=1, source_target_pairs={{0,4},{1,5},{2,6},{3,7},{4,0},{5,1},{6,2},{7,3},{8,12},{9,13},{10,... | collective-permute-start | bytes 196616 | tf_op jit(solution)/shard_map/ppermute | solution.py:428
  15.2 1.0 %shard_map.98 = (bf16[16,4,8,256]{3,2,1,0:T(8,128)(2,1)}, f32[128,1024]{1,0:T(8,128)S(1)}, bf16[160,1536]{1,0:T(8,128)(2,1)S(1)}) custom-call(bf16[128,1536]{1,0:T(8,128)(2,1)S(1)} %get-tuple-element.53.xo, bf16[16,1536]{1,0:T(8,128)(2,1)S(1)} %collective-permute-done.2.y_even, bf16[16,1536]{1,0:T(8,128)(2,1)S(1)} %collective-permute-done.3.y_odd, ...), custom_call_target="tpu_custom_call" | custom-call | flops 2000000000 | bytes 1409024 | tf_op jit(solution)/shard_map/pallas_call | solution.py:404
  16.2 2.2 %collective-permute-done.4.z_even = bf16[64,512]{1,0:T(8,128)(2,1)S(1)} collective-permute-done((bf16[64,512]{1,0:T(8,128)(2,1)S(1)}, bf16[64,512]{1,0:T(8,128)(2,1)S(1)}, u32[]{:S(2)}, u32[]{:S(2)}) %collective-permute-start.4) | collective-permute-done | bytes 65568 | tf_op jit(solution)/shard_map/ppermute | solution.py:428
  18.5 2.5 %collective-permute-start.7 = (bf16[32,1280]{1,0:T(8,128)(2,1)S(1)}, bf16[32,1280]{1,0:T(8,128)(2,1)S(1)}, u32[]{:S(2)}, u32[]{:S(2)}) collective-permute-start(bf16[32,1280]{1,0:T(8,128)(2,1)S(1)} %get-tuple-element.72), channel_id=1, source_target_pairs={{0,4},{1,2},{2,1},{3,7},{4,0},{5,6},{6,5},{7,3},{8,12},{9,10},{10,... | collective-permute-start | bytes 245768 | tf_op jit(solution)/shard_map/ppermute | solution.py:428
  21.0 0.4 shard_map.100.pre_ref
  21.5 2.0 %collective-permute-done.7.y_odd = bf16[32,1280]{1,0:T(8,128)(2,1)S(1)} collective-permute-done((bf16[32,1280]{1,0:T(8,128)(2,1)S(1)}, bf16[32,1280]{1,0:T(8,128)(2,1)S(1)}, u32[]{:S(2)}, u32[]{:S(2)}) %collective-permute-start.7) | collective-permute-done | bytes 81952 | tf_op jit(solution)/shard_map/ppermute | solution.py:428
  23.4 1.0 %shard_map.101 = (bf16[128,768]{1,0:T(8,128)(2,1)S(1)}, bf16[192,512]{1,0:T(8,128)(2,1)S(1)}, bf16[256,128]{1,0:T(8,128)(2,1)S(1)}, bf16[128,1024]{1,0:T(8,128)(...) custom-call(bf16[64,768]{1,0:T(8,128)(2,1)S(1)} %get-tuple-element.69.po, ...), custom_call_target="tpu_custom_call" | custom-call | flops 4000000000 | bytes 1867776 | tf_op jit(solution)/shard_map/pallas_call | solution.py:404
  24.4 1.1 %shard_map.104 = f32[176,128]{1,0:T(8,128)S(1)} custom-call(bf16[160,1536]{1,0:T(8,128)(2,1)S(1)} %get-tuple-element.90.x_ref, bf16[128,1024]{1,0:T(8,128)(2,1)S(1)} %get-tuple-element.79.own.fs, bf16[128,768]{1,0:T(8,128)(2,1)S(1)} %get-tuple-element.91.p_ref, bf16[192,512]{1,0:T(8,128)(2,1)S(1)} %get-tuple-element.92.cs), custom_call_target="tpu_custom_call" | custom-call | flops 2000000000 | bytes 1146880 | tf_op jit(solution)/shard_map/pallas_call | solution.py:404
  25.6 2.1 %collective-permute-start.8 = (bf16[128,256]{1,0:T(8,128)(2,1)S(1)}, bf16[128,256]{1,0:T(8,128)(2,1)S(1)}, u32[]{:S(2)}, u32[]{:S(2)}) collective-permute-start(bf16[128,256]{1,0:T(8,128)(2,1)S(1)} %get-tuple-element.80), channel_id=1, source_target_pairs={{0,4},{1,5},{2,6},{3,7},{4,0},{5,1},{6,2},{7,3},{8,12},{9,13},{10,... | collective-permute-start | bytes 196616 | tf_op jit(solution)/shard_map/ppermute | solution.py:428
  27.9 3.9 %collective-permute-start.15 = (bf16[176,128]{1,0:T(8,128)(2,1)S(1)}, bf16[176,128]{1,0:T(8,128)(2,1)S(1)}, u32[]{:S(2)}, u32[]{:S(2)}) collective-permute-start(bf16[176,128]{1,0:T(8,128)(2,1)S(1)} %add_convert_fusion.1), channel_id=1, source_target_pairs={{0,6},{1,7},{2,4},{3,5},{4,2},{5,3},{6,0},{7,1},{8,14},{9,15},{10,... | collective-permute-start | bytes 135176 | tf_op jit(solution)/shard_map/ppermute | solution.py:436
  31.8 0.3 collective-permute-start.14
  32.1 1.4 %collective-permute-start.13 = (bf16[176,128]{1,0:T(8,128)(2,1)S(1)}, bf16[176,128]{1,0:T(8,128)(2,1)S(1)}, u32[]{:S(2)}, u32[]{:S(2)}) collective-permute-start(bf16[176,128]{1,0:T(8,128)(2,1)S(1)} %add_convert_fusion.1), channel_id=1, source_target_pairs={{0,2},{1,3},{2,0},{3,1},{4,6},{5,7},{6,4},{7,5},{8,10},{9,11},{10,... | collective-permute-start | bytes 135176 | tf_op jit(solution)/shard_map/ppermute | solution.py:436
  33.6 2.1 %collective-permute-start.11 = (bf16[16,1536]{1,0:T(8,128)(2,1)S(1)}, bf16[16,1536]{1,0:T(8,128)(2,1)S(1)}, u32[]{:S(2)}, u32[]{:S(2)}) collective-permute-start(bf16[16,1536]{1,0:T(8,128)(2,1)S(1)} %get-tuple-element.84), channel_id=1, source_target_pairs={{0,4},{1,2},{2,1},{3,7},{4,0},{5,6},{6,5},{7,3},{8,12},{9,10},{10,... | collective-permute-start | bytes 147464 | tf_op jit(solution)/shard_map/ppermute | solution.py:428
  35.7 0.2 collective-permute-done.14
  35.9 0.3 collective-permute-done.13
  36.2 2.8 %collective-permute-start.18 = (bf16[176,128]{1,0:T(8,128)(2,1)S(1)}, bf16[176,128]{1,0:T(8,128)(2,1)S(1)}, u32[]{:S(2)}, u32[]{:S(2)}) collective-permute-start(bf16[176,128]{1,0:T(8,128)(2,1)S(1)} %add_convert_fusion.refs_0_), channel_id=1, source_target_pairs={{0,24},{1,25},{2,26},{3,27},{4,28},{5,29},{6,30},{7,31},{8,16},{9,... | collective-permute-start | bytes 135176 | tf_op jit(solution)/shard_map/ppermute | solution.py:436
  39.0 0.3 collective-permute-start.17
  39.3 1.3 %collective-permute-start.16 = (bf16[176,128]{1,0:T(8,128)(2,1)S(1)}, bf16[176,128]{1,0:T(8,128)(2,1)S(1)}, u32[]{:S(2)}, u32[]{:S(2)}) collective-permute-start(bf16[176,128]{1,0:T(8,128)(2,1)S(1)} %add_convert_fusion.refs_0_), channel_id=1, source_target_pairs={{0,8},{1,9},{2,10},{3,11},{4,12},{5,13},{6,14},{7,15},{8,0},{9,1},... | collective-permute-start | bytes 135176 | tf_op jit(solution)/shard_map/ppermute | solution.py:436
  40.6 2.3 %shard_map.103 = (bf16[16,4,8,256]{3,2,1,0:T(8,128)(2,1)}, bf16[256,128]{1,0:T(8,128)(2,1)}) custom-call(bf16[128,1536]{1,0:T(8,128)(2,1)S(1)} %get-tuple-element.82.fs, bf16[16,1536]{1,0:T(8,128)(2,1)S(1)} %collective-permute-done.10.y_even, bf16[16,1536]{1,0:T(8,128)(2,1)S(1)} %collective-permute-done.11.y_odd, f32[128,1024]{1,0:T(8,128)S(1)} %get-tuple-element.85.fg, ...), custom_call_target="tpu_custom_call" | custom-call | flops 2000000000 | bytes 1449984 | tf_op jit(solution)/shard_map/pallas_call | solution.py:404
  43.0 0.9 %collective-permute-done.17.refs_2_ = bf16[176,128]{1,0:T(8,128)(2,1)S(1)} collective-permute-done((bf16[176,128]{1,0:T(8,128)(2,1)S(1)}, bf16[176,128]{1,0:T(8,128)(2,1)S(1)}, u32[]{:S(2)}, u32[]{:S(2)}) %collective-permute-start.17) | collective-permute-done | bytes 45088 | tf_op jit(solution)/shard_map/ppermute | solution.py:436
  44.0 1.0 %shard_map.105 = (f32[27,16,16]{2,1,0:T(8,128)}, f32[27,16,32]{2,1,0:T(8,128)}) custom-call(bf16[176,128]{1,0:T(8,128)(2,1)S(1)} %add_convert_fusion.refs_0_, bf16[176,128]{1,0:T(8,128)(2,1)S(1)} %collective-permute-done.16.refs_1_, bf16[176,128]{1,0:T(8,128)(2,1)S(1)} %collective-permute-done.17.refs_2_, bf16[176,128]{1,0:T(8,128)(2,1)S(1)} %collective-permute-done.18.refs_3_), custom_call_target="tpu_custom_call" | custom-call | flops 10000000 | bytes 180224 | tf_op jit(solution)/shard_map/pallas_call | solution.py:404
  (32 shorter events, 0.8 us)
Async XLA Ops:
  0.6 1.0 %copy-start = (bf16[16,4,8,256]{3,2,1,0:T(8,128)(2,1)S(1)}, bf16[16,4,8,256]{3,2,1,0:T(8,128)(2,1)}, u32[]{:S(2)}) copy-start(bf16[16,4,8,256]{3,2,1,0:T(8,128)(2,1)} %vol.1) | copy-start | bytes 786436
  1.6 3.3 %copy-start.1 = (bf16[16,4,8,256]{3,2,1,0:T(8,128)(2,1)S(1)}, bf16[16,4,8,256]{3,2,1,0:T(8,128)(2,1)}, u32[]{:S(2)}) copy-start(bf16[16,4,8,256]{3,2,1,0:T(8,128)(2,1)} %fc.1) | copy-start | bytes 786436
  1.6 3.3 %copy-start.4 = (bf16[32,2,4,128]{3,2,1,0:T(4,128)(2,1)S(1)}, bf16[32,2,4,128]{3,2,1,0:T(4,128)(2,1)}, u32[]{:S(2)}) copy-start(bf16[32,2,4,128]{3,2,1,0:T(4,128)(2,1)} %param.9) | copy-start | bytes 196612
  1.8 6.1 %collective-permute-start = (bf16[128,256]{1,0:T(8,128)(2,1)S(1)}, bf16[128,256]{1,0:T(8,128)(2,1)S(1)}, u32[]{:S(2)}, u32[]{:S(2)}) collective-permute-start(bf16[128,256]{1,0:T(8,128)(2,1)S(1)} %get-tuple-element.51), channel_id=1, source_target_pairs={{0,4},{1,5},{2,6},{3,7},{4,0},{5,1},{6,2},{7,3},{8,12},{9,13},{10,... | collective-permute-start | bytes 196616 | tf_op jit(solution)/shard_map/ppermute | solution.py:428
  4.8 3.1 %collective-permute-start.1 = (bf16[128,256]{1,0:T(8,128)(2,1)S(1)}, bf16[128,256]{1,0:T(8,128)(2,1)S(1)}, u32[]{:S(2)}, u32[]{:S(2)}) collective-permute-start(bf16[128,256]{1,0:T(8,128)(2,1)S(1)} %get-tuple-element.52), channel_id=1, source_target_pairs={{0,1},{1,0},{2,3},{3,2},{4,8},{5,9},{6,10},{7,11},{8,4},{9,5},{10,... | collective-permute-start | bytes 196616 | tf_op jit(solution)/shard_map/ppermute | solution.py:428
  4.9 0.9 %copy-start.2 = (bf16[3,3,3,16,16]{4,3,2,1,0:T(8,128)(2,1)S(1)}, bf16[3,3,3,16,16]{4,3,2,1,0:T(8,128)(2,1)}, u32[]{:S(2)}) copy-start(bf16[3,3,3,16,16]{4,3,2,1,0:T(8,128)(2,1)} %param.6) | copy-start | bytes 41476
  4.9 0.9 %copy-start.3 = (bf16[3,3,3,32,16]{3,4,2,1,0:T(8,128)(2,1)S(1)}, bf16[3,3,3,32,16]{3,4,2,1,0:T(8,128)(2,1)}, u32[]{:S(2)}) copy-start(bf16[3,3,3,32,16]{3,4,2,1,0:T(8,128)(2,1)} %param.7) | copy-start | bytes 82948
  8.0 3.6 %collective-permute-start.2 = (bf16[16,1536]{1,0:T(8,128)(2,1)S(1)}, bf16[16,1536]{1,0:T(8,128)(2,1)S(1)}, u32[]{:S(2)}, u32[]{:S(2)}) collective-permute-start(bf16[16,1536]{1,0:T(8,128)(2,1)S(1)} %get-tuple-element.54), channel_id=1, source_target_pairs={{0,1},{1,0},{2,3},{3,2},{4,5},{5,4},{6,7},{7,6},{8,9},{9,8},{10,11... | collective-permute-start | bytes 147464 | tf_op jit(solution)/shard_map/ppermute | solution.py:428
  8.1 4.6 %collective-permute-start.3 = (bf16[16,1536]{1,0:T(8,128)(2,1)S(1)}, bf16[16,1536]{1,0:T(8,128)(2,1)S(1)}, u32[]{:S(2)}, u32[]{:S(2)}) collective-permute-start(bf16[16,1536]{1,0:T(8,128)(2,1)S(1)} %get-tuple-element.55), channel_id=1, source_target_pairs={{0,4},{1,2},{2,1},{3,7},{4,0},{5,6},{6,5},{7,3},{8,12},{9,10},{10,... | collective-permute-start | bytes 147464 | tf_op jit(solution)/shard_map/ppermute | solution.py:428
  13.1 5.3 %collective-permute-start.4 = (bf16[64,512]{1,0:T(8,128)(2,1)S(1)}, bf16[64,512]{1,0:T(8,128)(2,1)S(1)}, u32[]{:S(2)}, u32[]{:S(2)}) collective-permute-start(bf16[64,512]{1,0:T(8,128)(2,1)S(1)} %get-tuple-element.67), channel_id=1, source_target_pairs={{0,4},{1,5},{2,6},{3,7},{4,0},{5,1},{6,2},{7,3},{8,12},{9,13},{10,... | collective-permute-start | bytes 196616 | tf_op jit(solution)/shard_map/ppermute | solution.py:428
  15.2 3.2 %collective-permute-start.5 = (bf16[64,512]{1,0:T(8,128)(2,1)S(1)}, bf16[64,512]{1,0:T(8,128)(2,1)S(1)}, u32[]{:S(2)}, u32[]{:S(2)}) collective-permute-start(bf16[64,512]{1,0:T(8,128)(2,1)S(1)} %get-tuple-element.68), channel_id=1, source_target_pairs={{0,1},{1,0},{2,3},{3,2},{4,8},{5,9},{6,10},{7,11},{8,4},{9,5},{10,... | collective-permute-start | bytes 196616 | tf_op jit(solution)/shard_map/ppermute | solution.py:428
  18.4 3.0 %collective-permute-start.6 = (bf16[32,1280]{1,0:T(8,128)(2,1)S(1)}, bf16[32,1280]{1,0:T(8,128)(2,1)S(1)}, u32[]{:S(2)}, u32[]{:S(2)}) collective-permute-start(bf16[32,1280]{1,0:T(8,128)(2,1)S(1)} %get-tuple-element.71), channel_id=1, source_target_pairs={{0,1},{1,0},{2,3},{3,2},{4,5},{5,4},{6,7},{7,6},{8,9},{9,8},{10,11... | collective-permute-start | bytes 245768 | tf_op jit(solution)/shard_map/ppermute | solution.py:428
  18.5 4.9 %collective-permute-start.7 = (bf16[32,1280]{1,0:T(8,128)(2,1)S(1)}, bf16[32,1280]{1,0:T(8,128)(2,1)S(1)}, u32[]{:S(2)}, u32[]{:S(2)}) collective-permute-start(bf16[32,1280]{1,0:T(8,128)(2,1)S(1)} %get-tuple-element.72), channel_id=1, source_target_pairs={{0,4},{1,2},{2,1},{3,7},{4,0},{5,6},{6,5},{7,3},{8,12},{9,10},{10,... | collective-permute-start | bytes 245768 | tf_op jit(solution)/shard_map/ppermute | solution.py:428
  25.5 2.3 %collective-permute-start.12 = (f32[176,128]{1,0:T(8,128)S(1)}, f32[176,128]{1,0:T(8,128)S(1)}, u32[]{:S(2)}, u32[]{:S(2)}) collective-permute-start(f32[176,128]{1,0:T(8,128)S(1)} %shard_map.104), channel_id=1, source_target_pairs={{0,1},{1,0},{2,3},{3,2},{4,5},{5,4},{6,7},{7,6},{8,9},{9,8},{10,11... | collective-permute-start | bytes 270344 | tf_op jit(solution)/shard_map/ppermute | solution.py:436
  25.6 7.8 %collective-permute-start.8 = (bf16[128,256]{1,0:T(8,128)(2,1)S(1)}, bf16[128,256]{1,0:T(8,128)(2,1)S(1)}, u32[]{:S(2)}, u32[]{:S(2)}) collective-permute-start(bf16[128,256]{1,0:T(8,128)(2,1)S(1)} %get-tuple-element.80), channel_id=1, source_target_pairs={{0,4},{1,5},{2,6},{3,7},{4,0},{5,1},{6,2},{7,3},{8,12},{9,13},{10,... | collective-permute-start | bytes 196616 | tf_op jit(solution)/shard_map/ppermute | solution.py:428
  27.7 5.7 %collective-permute-start.9 = (bf16[128,256]{1,0:T(8,128)(2,1)S(1)}, bf16[128,256]{1,0:T(8,128)(2,1)S(1)}, u32[]{:S(2)}, u32[]{:S(2)}) collective-permute-start(bf16[128,256]{1,0:T(8,128)(2,1)S(1)} %get-tuple-element.81), channel_id=1, source_target_pairs={{0,1},{1,0},{2,3},{3,2},{4,8},{5,9},{6,10},{7,11},{8,4},{9,5},{10,... | collective-permute-start | bytes 196616 | tf_op jit(solution)/shard_map/ppermute | solution.py:428
  27.9 7.8 %collective-permute-start.15 = (bf16[176,128]{1,0:T(8,128)(2,1)S(1)}, bf16[176,128]{1,0:T(8,128)(2,1)S(1)}, u32[]{:S(2)}, u32[]{:S(2)}) collective-permute-start(bf16[176,128]{1,0:T(8,128)(2,1)S(1)} %add_convert_fusion.1), channel_id=1, source_target_pairs={{0,6},{1,7},{2,4},{3,5},{4,2},{5,3},{6,0},{7,1},{8,14},{9,15},{10,... | collective-permute-start | bytes 135176 | tf_op jit(solution)/shard_map/ppermute | solution.py:436
  31.8 4.0 %collective-permute-start.14 = (bf16[176,128]{1,0:T(8,128)(2,1)S(1)}, bf16[176,128]{1,0:T(8,128)(2,1)S(1)}, u32[]{:S(2)}, u32[]{:S(2)}) collective-permute-start(bf16[176,128]{1,0:T(8,128)(2,1)S(1)} %add_convert_fusion.1), channel_id=1, source_target_pairs={{0,4},{1,5},{2,6},{3,7},{4,0},{5,1},{6,2},{7,3},{8,12},{9,13},{10,... | collective-permute-start | bytes 135176 | tf_op jit(solution)/shard_map/ppermute | solution.py:436
  32.1 4.0 %collective-permute-start.13 = (bf16[176,128]{1,0:T(8,128)(2,1)S(1)}, bf16[176,128]{1,0:T(8,128)(2,1)S(1)}, u32[]{:S(2)}, u32[]{:S(2)}) collective-permute-start(bf16[176,128]{1,0:T(8,128)(2,1)S(1)} %add_convert_fusion.1), channel_id=1, source_target_pairs={{0,2},{1,3},{2,0},{3,1},{4,6},{5,7},{6,4},{7,5},{8,10},{9,11},{10,... | collective-permute-start | bytes 135176 | tf_op jit(solution)/shard_map/ppermute | solution.py:436
  33.5 7.1 %collective-permute-start.10 = (bf16[16,1536]{1,0:T(8,128)(2,1)S(1)}, bf16[16,1536]{1,0:T(8,128)(2,1)S(1)}, u32[]{:S(2)}, u32[]{:S(2)}) collective-permute-start(bf16[16,1536]{1,0:T(8,128)(2,1)S(1)} %get-tuple-element.83), channel_id=1, source_target_pairs={{0,1},{1,0},{2,3},{3,2},{4,5},{5,4},{6,7},{7,6},{8,9},{9,8},{10,11... | collective-permute-start | bytes 147464 | tf_op jit(solution)/shard_map/ppermute | solution.py:428
  33.6 7.0 %collective-permute-start.11 = (bf16[16,1536]{1,0:T(8,128)(2,1)S(1)}, bf16[16,1536]{1,0:T(8,128)(2,1)S(1)}, u32[]{:S(2)}, u32[]{:S(2)}) collective-permute-start(bf16[16,1536]{1,0:T(8,128)(2,1)S(1)} %get-tuple-element.84), channel_id=1, source_target_pairs={{0,4},{1,2},{2,1},{3,7},{4,0},{5,6},{6,5},{7,3},{8,12},{9,10},{10,... | collective-permute-start | bytes 147464 | tf_op jit(solution)/shard_map/ppermute | solution.py:428
  36.2 6.8 %collective-permute-start.18 = (bf16[176,128]{1,0:T(8,128)(2,1)S(1)}, bf16[176,128]{1,0:T(8,128)(2,1)S(1)}, u32[]{:S(2)}, u32[]{:S(2)}) collective-permute-start(bf16[176,128]{1,0:T(8,128)(2,1)S(1)} %add_convert_fusion.refs_0_), channel_id=1, source_target_pairs={{0,24},{1,25},{2,26},{3,27},{4,28},{5,29},{6,30},{7,31},{8,16},{9,... | collective-permute-start | bytes 135176 | tf_op jit(solution)/shard_map/ppermute | solution.py:436
  39.0 5.0 %collective-permute-start.17 = (bf16[176,128]{1,0:T(8,128)(2,1)S(1)}, bf16[176,128]{1,0:T(8,128)(2,1)S(1)}, u32[]{:S(2)}, u32[]{:S(2)}) collective-permute-start(bf16[176,128]{1,0:T(8,128)(2,1)S(1)} %add_convert_fusion.refs_0_), channel_id=1, source_target_pairs={{0,16},{1,17},{2,18},{3,19},{4,20},{5,21},{6,22},{7,23},{8,24},{9,... | collective-permute-start | bytes 135176 | tf_op jit(solution)/shard_map/ppermute | solution.py:436
  39.3 4.8 %collective-permute-start.16 = (bf16[176,128]{1,0:T(8,128)(2,1)S(1)}, bf16[176,128]{1,0:T(8,128)(2,1)S(1)}, u32[]{:S(2)}, u32[]{:S(2)}) collective-permute-start(bf16[176,128]{1,0:T(8,128)(2,1)S(1)} %add_convert_fusion.refs_0_), channel_id=1, source_target_pairs={{0,8},{1,9},{2,10},{3,11},{4,12},{5,13},{6,14},{7,15},{8,0},{9,1},... | collective-permute-start | bytes 135176 | tf_op jit(solution)/shard_map/ppermute | solution.py:436

commit v5 on v4

--- a/solution.py
+++ b/solution.py
@@ -429,11 +429,15 @@
     return out
 
 
-def swap_bits(value, bits):
+def swap_bits(value, bits, odd_bits=()):
     ny = lax.axis_size("gy")
     count = lax.axis_size("gx") * ny
-    flip = sum((bit if axis == "gy" else bit * ny) for axis, bit in bits)
-    return lax.ppermute(value, ("gx", "gy"), [(i, i ^ flip) for i in range(count)])
+    flip, more = (
+        sum((bit if axis == "gy" else bit * ny) for axis, bit in some) for some in (bits, odd_bits)
+    )
+    return lax.ppermute(
+        value, ("gx", "gy"), [(i, i ^ flip ^ (more if i % 2 else 0)) for i in range(count)]
+    )
 
 
 def program(volume, fine_kernel, coarse_kernel, fine_cotangent, coarse_cotangent):
@@ -568,9 +572,10 @@
     for index, group in enumerate(rounds):
         if index:
             value = value.astype(BF16)
-        parts = [value]
-        for some in [[bit] for bit in group] + [group] * (len(group) == 2):
-            parts.append(swap_bits(value, some))
+        parts = [value, swap_bits(value, group[:1])]
+        if len(group) == 2:
+            fetched = swap_bits(value, group[1:], group[:1])
+            parts += [fetched, swap_bits(fetched, bits[:1])]
         if index + 1 < len(rounds):
             value = tree_sum([part.astype(F32) for part in parts])
     volume_grad, coarse_out = call(

time: 45.2 us -> 46 us (1.018)
  waiting for transfers between devices: 7.97 us -> 12.5 us
  starting transfers between devices: 24.8 us -> 21 us
    ppermute x7, waiting for transfers between devices: 1.5 us -> 4.04 us  [swap_bits(): lax.ppermute(value, ('gx', 'gy'), [(i, i ^ flip ^ (more if i % 2 else 0))...]
    ppermute x7, starting transfers between devices: 10.1 us -> 7.61 us  [swap_bits(): lax.ppermute(value, ('gx', 'gy'), [(i, i ^ flip ^ (more if i % 2 else 0))...]
    ppermute x12, waiting for transfers between devices: 6.47 us -> 8.45 us  [swap_pairs(): out.append(lax.ppermute(value, ('gx', 'gy'), pairs))]
    ppermute x12, starting transfers between devices: 14.7 us -> 13.4 us  [swap_pairs(): out.append(lax.ppermute(value, ('gx', 'gy'), pairs))]
where the time goes in v5:
time: 46 us; the launch traced here: 45.8 us
  starting transfers between devices  21 us (46%)
  waiting for transfers between devices  12.5 us (27%)
  Pallas kernels  9.8 us (21%)
  local copies, waits for them, and re-layouts  1.63 us (4%)
  between operations  0.81 us (2%)
    ppermute x12, starting transfers between devices, swap_pairs(): out.append(lax.ppermute(value, ('gx', 'gy'), pairs))  13.4 us
    pallas_call x14, Pallas kernels, call(): pl.pallas_call(body, out_shape=outs, in_specs=specs, out_specs=[pl.BlockS...  9.8 us
    ppermute x12, waiting for transfers between devices, swap_pairs(): out.append(lax.ppermute(value, ('gx', 'gy'), pairs))  8.45 us
    ppermute x7, starting transfers between devices, swap_bits(): lax.ppermute(value, ('gx', 'gy'), [(i, i ^ flip ^ (more if i % 2 else 0))...  7.61 us
    ppermute x7, waiting for transfers between devices, swap_bits(): lax.ppermute(value, ('gx', 'gy'), [(i, i ^ flip ^ (more if i % 2 else 0))...  4.04 us
    unnamed x10, local copies, waits for them, and re-layouts  1.63 us
  transfers between devices with their start and end apart: 19, of which 8 were waited for; matrix products, arithmetic and copies ran while one was open for 0% of the time, Pallas kernels for 13%

profile of v5, /device:TPU:0, one launch (start us, length us, event | category | flops | bytes accessed | tf_op | source)
XLA Modules:
  0.0 45.8 jit_solution(11652057791691175368)
XLA Ops:
  0.6 0.9 %copy-done = bf16[16,4,8,256]{3,2,1,0:T(8,128)(2,1)S(1)} copy-done((bf16[16,4,8,256]{3,2,1,0:T(8,128)(2,1)S(1)}, bf16[16,4,8,256]{3,2,1,0:T(8,128)(2,1)}, u32[]{:S(2)}) %copy-start) | copy-done | bytes 262168
  1.6 0.2 shard_map.92
  1.8 3.0 %collective-permute-start = (bf16[128,256]{1,0:T(8,128)(2,1)S(1)}, bf16[128,256]{1,0:T(8,128)(2,1)S(1)}, u32[]{:S(2)}, u32[]{:S(2)}) collective-permute-start(bf16[128,256]{1,0:T(8,128)(2,1)S(1)} %get-tuple-element.51), channel_id=1, source_target_pairs={{0,4},{1,5},{2,6},{3,7},{4,0},{5,1},{6,2},{7,3},{8,12},{9,13},{10,... | collective-permute-start | bytes 196616 | tf_op jit(solution)/shard_map/ppermute | solution.py:428
  4.9 0.3 shard_map.96
  5.1 0.6 %copy-done.2 = bf16[3,3,3,16,16]{4,3,2,1,0:T(8,128)(2,1)S(1)} copy-done((bf16[3,3,3,16,16]{4,3,2,1,0:T(8,128)(2,1)S(1)}, bf16[3,3,3,16,16]{4,3,2,1,0:T(8,128)(2,1)}, u32[]{:S(2)}) %copy-start.2) | copy-done | bytes 13848
  5.8 0.9 %shard_map.94 = (bf16[384,384]{1,0:T(8,128)(2,1)S(1)}, bf16[48,48]{1,0:T(8,128)(2,1)S(1)}, bf16[48,48]{1,0:T(8,128)(2,1)S(1)}, bf16[384,480]{1,0:T(8,128)(2,1)S(...) custom-call(bf16[27,16,16]{2,1,0:T(8,128)(2,1)S(1)} %bitcast.10, ...), custom_call_target="tpu_custom_call" | custom-call | flops 1000000000 | bytes 41472 | tf_op jit(solution)/shard_map/pallas_call | solution.py:404
  6.7 1.3 %collective-permute-done.z_even = bf16[128,256]{1,0:T(8,128)(2,1)S(1)} collective-permute-done((bf16[128,256]{1,0:T(8,128)(2,1)S(1)}, bf16[128,256]{1,0:T(8,128)(2,1)S(1)}, u32[]{:S(2)}, u32[]{:S(2)}) %collective-permute-start) | collective-permute-done | bytes 65568 | tf_op jit(solution)/shard_map/ppermute | solution.py:428
  8.1 2.5 %collective-permute-start.3 = (bf16[16,1536]{1,0:T(8,128)(2,1)S(1)}, bf16[16,1536]{1,0:T(8,128)(2,1)S(1)}, u32[]{:S(2)}, u32[]{:S(2)}) collective-permute-start(bf16[16,1536]{1,0:T(8,128)(2,1)S(1)} %get-tuple-element.55), channel_id=1, source_target_pairs={{0,4},{1,2},{2,1},{3,7},{4,0},{5,6},{6,5},{7,3},{8,12},{9,10},{10,... | collective-permute-start | bytes 147464 | tf_op jit(solution)/shard_map/ppermute | solution.py:428
  10.6 1.0 %shard_map.95 = (f32[128,1024]{1,0:T(8,128)S(1)}, bf16[96,1024]{1,0:T(8,128)(2,1)S(1)}, f32[96,256]{1,0:T(8,128)S(1)}) custom-call(bf16[128,1536]{1,0:T(8,128)(2,1)S(1)} %get-tuple-element.53.xo, bf16[384,384]{1,0:T(8,128)(2,1)S(1)} %get-tuple-element.56.wa), custom_call_target="tpu_custom_call" | custom-call | flops 3000000000 | bytes 688128 | tf_op jit(solution)/shard_map/pallas_call | solution.py:404
  11.6 1.0 %collective-permute-done.3.y_odd = bf16[16,1536]{1,0:T(8,128)(2,1)S(1)} collective-permute-done((bf16[16,1536]{1,0:T(8,128)(2,1)S(1)}, bf16[16,1536]{1,0:T(8,128)(2,1)S(1)}, u32[]{:S(2)}, u32[]{:S(2)}) %collective-permute-start.3) | collective-permute-done | bytes 49184 | tf_op jit(solution)/shard_map/ppermute | solution.py:428
  12.7 0.4 shard_map.97
  13.1 2.1 %collective-permute-start.4 = (bf16[64,512]{1,0:T(8,128)(2,1)S(1)}, bf16[64,512]{1,0:T(8,128)(2,1)S(1)}, u32[]{:S(2)}, u32[]{:S(2)}) collective-permute-start(bf16[64,512]{1,0:T(8,128)(2,1)S(1)} %get-tuple-element.67), channel_id=1, source_target_pairs={{0,4},{1,5},{2,6},{3,7},{4,0},{5,1},{6,2},{7,3},{8,12},{9,13},{10,... | collective-permute-start | bytes 196616 | tf_op jit(solution)/shard_map/ppermute | solution.py:428
  15.2 1.0 %shard_map.98 = (bf16[16,4,8,256]{3,2,1,0:T(8,128)(2,1)}, f32[128,1024]{1,0:T(8,128)S(1)}, bf16[160,1536]{1,0:T(8,128)(2,1)S(1)}) custom-call(bf16[128,1536]{1,0:T(8,128)(2,1)S(1)} %get-tuple-element.53.xo, bf16[16,1536]{1,0:T(8,128)(2,1)S(1)} %collective-permute-done.2.y_even, bf16[16,1536]{1,0:T(8,128)(2,1)S(1)} %collective-permute-done.3.y_odd, ...), custom_call_target="tpu_custom_call" | custom-call | flops 2000000000 | bytes 1409024 | tf_op jit(solution)/shard_map/pallas_call | solution.py:404
  16.2 2.2 %collective-permute-done.4.z_even = bf16[64,512]{1,0:T(8,128)(2,1)S(1)} collective-permute-done((bf16[64,512]{1,0:T(8,128)(2,1)S(1)}, bf16[64,512]{1,0:T(8,128)(2,1)S(1)}, u32[]{:S(2)}, u32[]{:S(2)}) %collective-permute-start.4) | collective-permute-done | bytes 65568 | tf_op jit(solution)/shard_map/ppermute | solution.py:428
  18.5 2.5 %collective-permute-start.7 = (bf16[32,1280]{1,0:T(8,128)(2,1)S(1)}, bf16[32,1280]{1,0:T(8,128)(2,1)S(1)}, u32[]{:S(2)}, u32[]{:S(2)}) collective-permute-start(bf16[32,1280]{1,0:T(8,128)(2,1)S(1)} %get-tuple-element.72), channel_id=1, source_target_pairs={{0,4},{1,2},{2,1},{3,7},{4,0},{5,6},{6,5},{7,3},{8,12},{9,10},{10,... | collective-permute-start | bytes 245768 | tf_op jit(solution)/shard_map/ppermute | solution.py:428
  21.0 0.4 shard_map.100.pre_ref
  21.5 2.0 %collective-permute-done.7.y_odd = bf16[32,1280]{1,0:T(8,128)(2,1)S(1)} collective-permute-done((bf16[32,1280]{1,0:T(8,128)(2,1)S(1)}, bf16[32,1280]{1,0:T(8,128)(2,1)S(1)}, u32[]{:S(2)}, u32[]{:S(2)}) %collective-permute-start.7) | collective-permute-done | bytes 81952 | tf_op jit(solution)/shard_map/ppermute | solution.py:428
  23.4 1.0 %shard_map.101 = (bf16[128,768]{1,0:T(8,128)(2,1)S(1)}, bf16[192,512]{1,0:T(8,128)(2,1)S(1)}, bf16[256,128]{1,0:T(8,128)(2,1)S(1)}, bf16[128,1024]{1,0:T(8,128)(...) custom-call(bf16[64,768]{1,0:T(8,128)(2,1)S(1)} %get-tuple-element.69.po, ...), custom_call_target="tpu_custom_call" | custom-call | flops 4000000000 | bytes 1867776 | tf_op jit(solution)/shard_map/pallas_call | solution.py:404
  24.4 1.1 %shard_map.104 = f32[176,128]{1,0:T(8,128)S(1)} custom-call(bf16[160,1536]{1,0:T(8,128)(2,1)S(1)} %get-tuple-element.90.x_ref, bf16[128,1024]{1,0:T(8,128)(2,1)S(1)} %get-tuple-element.79.own.fs, bf16[128,768]{1,0:T(8,128)(2,1)S(1)} %get-tuple-element.91.p_ref, bf16[192,512]{1,0:T(8,128)(2,1)S(1)} %get-tuple-element.92.cs), custom_call_target="tpu_custom_call" | custom-call | flops 2000000000 | bytes 1146880 | tf_op jit(solution)/shard_map/pallas_call | solution.py:404
  25.6 1.3 %collective-permute-done.12 = f32[176,128]{1,0:T(8,128)S(1)} collective-permute-done((f32[176,128]{1,0:T(8,128)S(1)}, f32[176,128]{1,0:T(8,128)S(1)}, u32[]{:S(2)}, u32[]{:S(2)}) %collective-permute-start.12) | collective-permute-done | bytes 90144 | tf_op jit(solution)/shard_map/ppermute | solution.py:438
  26.9 2.1 %collective-permute-start.14 = (bf16[176,128]{1,0:T(8,128)(2,1)S(1)}, bf16[176,128]{1,0:T(8,128)(2,1)S(1)}, u32[]{:S(2)}, u32[]{:S(2)}) collective-permute-start(bf16[176,128]{1,0:T(8,128)(2,1)S(1)} %add_convert_fusion.1), channel_id=1, source_target_pairs={{0,4},{1,7},{2,6},{3,5},{4,0},{5,3},{6,2},{7,1},{8,12},{9,15},{10,... | collective-permute-start | bytes 135176 | tf_op jit(solution)/shard_map/ppermute | solution.py:438
  29.0 0.1 collective-permute-start.8
  29.1 1.3 %collective-permute-start.13 = (bf16[176,128]{1,0:T(8,128)(2,1)S(1)}, bf16[176,128]{1,0:T(8,128)(2,1)S(1)}, u32[]{:S(2)}, u32[]{:S(2)}) collective-permute-start(bf16[176,128]{1,0:T(8,128)(2,1)S(1)} %add_convert_fusion.1), channel_id=1, source_target_pairs={{0,2},{1,3},{2,0},{3,1},{4,6},{5,7},{6,4},{7,5},{8,10},{9,11},{10,... | collective-permute-start | bytes 135176 | tf_op jit(solution)/shard_map/ppermute | solution.py:438
  30.3 0.7 %collective-permute-done.14 = bf16[176,128]{1,0:T(8,128)(2,1)S(1)} collective-permute-done((bf16[176,128]{1,0:T(8,128)(2,1)S(1)}, bf16[176,128]{1,0:T(8,128)(2,1)S(1)}, u32[]{:S(2)}, u32[]{:S(2)}) %collective-permute-start.14) | collective-permute-done | bytes 45088 | tf_op jit(solution)/shard_map/ppermute | solution.py:438
  31.0 0.3 collective-permute-start.15
  31.3 2.0 %collective-permute-done.8.z_even = bf16[128,256]{1,0:T(8,128)(2,1)S(1)} collective-permute-done((bf16[128,256]{1,0:T(8,128)(2,1)S(1)}, bf16[128,256]{1,0:T(8,128)(2,1)S(1)}, u32[]{:S(2)}, u32[]{:S(2)}) %collective-permute-start.8) | collective-permute-done | bytes 65568 | tf_op jit(solution)/shard_map/ppermute | solution.py:428
  33.4 3.0 %collective-permute-start.11 = (bf16[16,1536]{1,0:T(8,128)(2,1)S(1)}, bf16[16,1536]{1,0:T(8,128)(2,1)S(1)}, u32[]{:S(2)}, u32[]{:S(2)}) collective-permute-start(bf16[16,1536]{1,0:T(8,128)(2,1)S(1)} %get-tuple-element.84), channel_id=1, source_target_pairs={{0,4},{1,2},{2,1},{3,7},{4,0},{5,6},{6,5},{7,3},{8,12},{9,10},{10,... | collective-permute-start | bytes 147464 | tf_op jit(solution)/shard_map/ppermute | solution.py:428
  36.4 3.8 %collective-permute-start.17 = (bf16[176,128]{1,0:T(8,128)(2,1)S(1)}, bf16[176,128]{1,0:T(8,128)(2,1)S(1)}, u32[]{:S(2)}, u32[]{:S(2)}) collective-permute-start(bf16[176,128]{1,0:T(8,128)(2,1)S(1)} %add_convert_fusion.refs_0_), channel_id=1, source_target_pairs={{0,16},{1,25},{2,18},{3,27},{4,20},{5,29},{6,22},{7,31},{8,24},{9,... | collective-permute-start | bytes 135176 | tf_op jit(solution)/shard_map/ppermute | solution.py:438
  40.2 0.2 collective-permute-start.16
  40.4 2.1 %collective-permute-done.17.refs_2_ = bf16[176,128]{1,0:T(8,128)(2,1)S(1)} collective-permute-done((bf16[176,128]{1,0:T(8,128)(2,1)S(1)}, bf16[176,128]{1,0:T(8,128)(2,1)S(1)}, u32[]{:S(2)}, u32[]{:S(2)}) %collective-permute-start.17) | collective-permute-done | bytes 45088 | tf_op jit(solution)/shard_map/ppermute | solution.py:438
  42.4 2.4 %shard_map.103 = (bf16[16,4,8,256]{3,2,1,0:T(8,128)(2,1)}, bf16[256,128]{1,0:T(8,128)(2,1)}) custom-call(bf16[128,1536]{1,0:T(8,128)(2,1)S(1)} %get-tuple-element.82.fs, bf16[16,1536]{1,0:T(8,128)(2,1)S(1)} %collective-permute-done.10.y_even, bf16[16,1536]{1,0:T(8,128)(2,1)S(1)} %collective-permute-done.11.y_odd, f32[128,1024]{1,0:T(8,128)S(1)} %get-tuple-element.85.fg, ...), custom_call_target="tpu_custom_call" | custom-call | flops 2000000000 | bytes 1449984 | tf_op jit(solution)/shard_map/pallas_call | solution.py:404
  44.8 1.0 %shard_map.105 = (f32[27,16,16]{2,1,0:T(8,128)}, f32[27,16,32]{2,1,0:T(8,128)}) custom-call(bf16[176,128]{1,0:T(8,128)(2,1)S(1)} %add_convert_fusion.refs_0_, bf16[176,128]{1,0:T(8,128)(2,1)S(1)} %collective-permute-done.16.refs_1_, bf16[176,128]{1,0:T(8,128)(2,1)S(1)} %collective-permute-done.17.refs_2_, bf16[176,128]{1,0:T(8,128)(2,1)S(1)} %collective-permute-done.18.refs_3_), custom_call_target="tpu_custom_call" | custom-call | flops 10000000 | bytes 180224 | tf_op jit(solution)/shard_map/pallas_call | solution.py:404
  (32 shorter events, 0.6 us)
Async XLA Ops:
  0.6 1.0 %copy-start = (bf16[16,4,8,256]{3,2,1,0:T(8,128)(2,1)S(1)}, bf16[16,4,8,256]{3,2,1,0:T(8,128)(2,1)}, u32[]{:S(2)}) copy-start(bf16[16,4,8,256]{3,2,1,0:T(8,128)(2,1)} %vol.1) | copy-start | bytes 786436
  1.6 3.3 %copy-start.1 = (bf16[16,4,8,256]{3,2,1,0:T(8,128)(2,1)S(1)}, bf16[16,4,8,256]{3,2,1,0:T(8,128)(2,1)}, u32[]{:S(2)}) copy-start(bf16[16,4,8,256]{3,2,1,0:T(8,128)(2,1)} %fc.1) | copy-start | bytes 786436
  1.6 3.3 %copy-start.4 = (bf16[32,2,4,128]{3,2,1,0:T(4,128)(2,1)S(1)}, bf16[32,2,4,128]{3,2,1,0:T(4,128)(2,1)}, u32[]{:S(2)}) copy-start(bf16[32,2,4,128]{3,2,1,0:T(4,128)(2,1)} %param.9) | copy-start | bytes 196612
  1.8 6.1 %collective-permute-start = (bf16[128,256]{1,0:T(8,128)(2,1)S(1)}, bf16[128,256]{1,0:T(8,128)(2,1)S(1)}, u32[]{:S(2)}, u32[]{:S(2)}) collective-permute-start(bf16[128,256]{1,0:T(8,128)(2,1)S(1)} %get-tuple-element.51), channel_id=1, source_target_pairs={{0,4},{1,5},{2,6},{3,7},{4,0},{5,1},{6,2},{7,3},{8,12},{9,13},{10,... | collective-permute-start | bytes 196616 | tf_op jit(solution)/shard_map/ppermute | solution.py:428
  4.8 3.1 %collective-permute-start.1 = (bf16[128,256]{1,0:T(8,128)(2,1)S(1)}, bf16[128,256]{1,0:T(8,128)(2,1)S(1)}, u32[]{:S(2)}, u32[]{:S(2)}) collective-permute-start(bf16[128,256]{1,0:T(8,128)(2,1)S(1)} %get-tuple-element.52), channel_id=1, source_target_pairs={{0,1},{1,0},{2,3},{3,2},{4,8},{5,9},{6,10},{7,11},{8,4},{9,5},{10,... | collective-permute-start | bytes 196616 | tf_op jit(solution)/shard_map/ppermute | solution.py:428
  4.9 0.9 %copy-start.2 = (bf16[3,3,3,16,16]{4,3,2,1,0:T(8,128)(2,1)S(1)}, bf16[3,3,3,16,16]{4,3,2,1,0:T(8,128)(2,1)}, u32[]{:S(2)}) copy-start(bf16[3,3,3,16,16]{4,3,2,1,0:T(8,128)(2,1)} %param.6) | copy-start | bytes 41476
  4.9 0.9 %copy-start.3 = (bf16[3,3,3,32,16]{3,4,2,1,0:T(8,128)(2,1)S(1)}, bf16[3,3,3,32,16]{3,4,2,1,0:T(8,128)(2,1)}, u32[]{:S(2)}) copy-start(bf16[3,3,3,32,16]{3,4,2,1,0:T(8,128)(2,1)} %param.7) | copy-start | bytes 82948
  8.0 3.6 %collective-permute-start.2 = (bf16[16,1536]{1,0:T(8,128)(2,1)S(1)}, bf16[16,1536]{1,0:T(8,128)(2,1)S(1)}, u32[]{:S(2)}, u32[]{:S(2)}) collective-permute-start(bf16[16,1536]{1,0:T(8,128)(2,1)S(1)} %get-tuple-element.54), channel_id=1, source_target_pairs={{0,1},{1,0},{2,3},{3,2},{4,5},{5,4},{6,7},{7,6},{8,9},{9,8},{10,11... | collective-permute-start | bytes 147464 | tf_op jit(solution)/shard_map/ppermute | solution.py:428
  8.1 4.6 %collective-permute-start.3 = (bf16[16,1536]{1,0:T(8,128)(2,1)S(1)}, bf16[16,1536]{1,0:T(8,128)(2,1)S(1)}, u32[]{:S(2)}, u32[]{:S(2)}) collective-permute-start(bf16[16,1536]{1,0:T(8,128)(2,1)S(1)} %get-tuple-element.55), channel_id=1, source_target_pairs={{0,4},{1,2},{2,1},{3,7},{4,0},{5,6},{6,5},{7,3},{8,12},{9,10},{10,... | collective-permute-start | bytes 147464 | tf_op jit(solution)/shard_map/ppermute | solution.py:428
  13.1 5.3 %collective-permute-start.4 = (bf16[64,512]{1,0:T(8,128)(2,1)S(1)}, bf16[64,512]{1,0:T(8,128)(2,1)S(1)}, u32[]{:S(2)}, u32[]{:S(2)}) collective-permute-start(bf16[64,512]{1,0:T(8,128)(2,1)S(1)} %get-tuple-element.67), channel_id=1, source_target_pairs={{0,4},{1,5},{2,6},{3,7},{4,0},{5,1},{6,2},{7,3},{8,12},{9,13},{10,... | collective-permute-start | bytes 196616 | tf_op jit(solution)/shard_map/ppermute | solution.py:428
  15.2 3.2 %collective-permute-start.5 = (bf16[64,512]{1,0:T(8,128)(2,1)S(1)}, bf16[64,512]{1,0:T(8,128)(2,1)S(1)}, u32[]{:S(2)}, u32[]{:S(2)}) collective-permute-start(bf16[64,512]{1,0:T(8,128)(2,1)S(1)} %get-tuple-element.68), channel_id=1, source_target_pairs={{0,1},{1,0},{2,3},{3,2},{4,8},{5,9},{6,10},{7,11},{8,4},{9,5},{10,... | collective-permute-start | bytes 196616 | tf_op jit(solution)/shard_map/ppermute | solution.py:428
  18.4 3.0 %collective-permute-start.6 = (bf16[32,1280]{1,0:T(8,128)(2,1)S(1)}, bf16[32,1280]{1,0:T(8,128)(2,1)S(1)}, u32[]{:S(2)}, u32[]{:S(2)}) collective-permute-start(bf16[32,1280]{1,0:T(8,128)(2,1)S(1)} %get-tuple-element.71), channel_id=1, source_target_pairs={{0,1},{1,0},{2,3},{3,2},{4,5},{5,4},{6,7},{7,6},{8,9},{9,8},{10,11... | collective-permute-start | bytes 245768 | tf_op jit(solution)/shard_map/ppermute | solution.py:428
  18.5 4.9 %collective-permute-start.7 = (bf16[32,1280]{1,0:T(8,128)(2,1)S(1)}, bf16[32,1280]{1,0:T(8,128)(2,1)S(1)}, u32[]{:S(2)}, u32[]{:S(2)}) collective-permute-start(bf16[32,1280]{1,0:T(8,128)(2,1)S(1)} %get-tuple-element.72), channel_id=1, source_target_pairs={{0,4},{1,2},{2,1},{3,7},{4,0},{5,6},{6,5},{7,3},{8,12},{9,10},{10,... | collective-permute-start | bytes 245768 | tf_op jit(solution)/shard_map/ppermute | solution.py:428
  25.5 1.4 %collective-permute-start.12 = (f32[176,128]{1,0:T(8,128)S(1)}, f32[176,128]{1,0:T(8,128)S(1)}, u32[]{:S(2)}, u32[]{:S(2)}) collective-permute-start(f32[176,128]{1,0:T(8,128)S(1)} %shard_map.104), channel_id=1, source_target_pairs={{0,1},{1,0},{2,3},{3,2},{4,5},{5,4},{6,7},{7,6},{8,9},{9,8},{10,11... | collective-permute-start | bytes 270344 | tf_op jit(solution)/shard_map/ppermute | solution.py:438
  26.9 4.1 %collective-permute-start.14 = (bf16[176,128]{1,0:T(8,128)(2,1)S(1)}, bf16[176,128]{1,0:T(8,128)(2,1)S(1)}, u32[]{:S(2)}, u32[]{:S(2)}) collective-permute-start(bf16[176,128]{1,0:T(8,128)(2,1)S(1)} %add_convert_fusion.1), channel_id=1, source_target_pairs={{0,4},{1,7},{2,6},{3,5},{4,0},{5,3},{6,2},{7,1},{8,12},{9,15},{10,... | collective-permute-start | bytes 135176 | tf_op jit(solution)/shard_map/ppermute | solution.py:438
  29.0 4.3 %collective-permute-start.8 = (bf16[128,256]{1,0:T(8,128)(2,1)S(1)}, bf16[128,256]{1,0:T(8,128)(2,1)S(1)}, u32[]{:S(2)}, u32[]{:S(2)}) collective-permute-start(bf16[128,256]{1,0:T(8,128)(2,1)S(1)} %get-tuple-element.80), channel_id=1, source_target_pairs={{0,4},{1,5},{2,6},{3,7},{4,0},{5,1},{6,2},{7,3},{8,12},{9,13},{10,... | collective-permute-start | bytes 196616 | tf_op jit(solution)/shard_map/ppermute | solution.py:428
  29.1 4.2 %collective-permute-start.9 = (bf16[128,256]{1,0:T(8,128)(2,1)S(1)}, bf16[128,256]{1,0:T(8,128)(2,1)S(1)}, u32[]{:S(2)}, u32[]{:S(2)}) collective-permute-start(bf16[128,256]{1,0:T(8,128)(2,1)S(1)} %get-tuple-element.81), channel_id=1, source_target_pairs={{0,1},{1,0},{2,3},{3,2},{4,8},{5,9},{6,10},{7,11},{8,4},{9,5},{10,... | collective-permute-start | bytes 196616 | tf_op jit(solution)/shard_map/ppermute | solution.py:428
  29.1 7.3 %collective-permute-start.13 = (bf16[176,128]{1,0:T(8,128)(2,1)S(1)}, bf16[176,128]{1,0:T(8,128)(2,1)S(1)}, u32[]{:S(2)}, u32[]{:S(2)}) collective-permute-start(bf16[176,128]{1,0:T(8,128)(2,1)S(1)} %add_convert_fusion.1), channel_id=1, source_target_pairs={{0,2},{1,3},{2,0},{3,1},{4,6},{5,7},{6,4},{7,5},{8,10},{9,11},{10,... | collective-permute-start | bytes 135176 | tf_op jit(solution)/shard_map/ppermute | solution.py:438
  31.0 5.4 %collective-permute-start.15 = (bf16[176,128]{1,0:T(8,128)(2,1)S(1)}, bf16[176,128]{1,0:T(8,128)(2,1)S(1)}, u32[]{:S(2)}, u32[]{:S(2)}) collective-permute-start(bf16[176,128]{1,0:T(8,128)(2,1)S(1)} %collective-permute-done.14), channel_id=1, source_target_pairs={{0,1},{1,0},{2,3},{3,2},{4,5},{5,4},{6,7},{7,6},{8,9},{9,8},{10,11... | collective-permute-start | bytes 135176 | tf_op jit(solution)/shard_map/ppermute | solution.py:438
  33.3 9.1 %collective-permute-start.10 = (bf16[16,1536]{1,0:T(8,128)(2,1)S(1)}, bf16[16,1536]{1,0:T(8,128)(2,1)S(1)}, u32[]{:S(2)}, u32[]{:S(2)}) collective-permute-start(bf16[16,1536]{1,0:T(8,128)(2,1)S(1)} %get-tuple-element.83), channel_id=1, source_target_pairs={{0,1},{1,0},{2,3},{3,2},{4,5},{5,4},{6,7},{7,6},{8,9},{9,8},{10,11... | collective-permute-start | bytes 147464 | tf_op jit(solution)/shard_map/ppermute | solution.py:428
  33.4 9.0 %collective-permute-start.11 = (bf16[16,1536]{1,0:T(8,128)(2,1)S(1)}, bf16[16,1536]{1,0:T(8,128)(2,1)S(1)}, u32[]{:S(2)}, u32[]{:S(2)}) collective-permute-start(bf16[16,1536]{1,0:T(8,128)(2,1)S(1)} %get-tuple-element.84), channel_id=1, source_target_pairs={{0,4},{1,2},{2,1},{3,7},{4,0},{5,6},{6,5},{7,3},{8,12},{9,10},{10,... | collective-permute-start | bytes 147464 | tf_op jit(solution)/shard_map/ppermute | solution.py:428
  36.4 6.0 %collective-permute-start.17 = (bf16[176,128]{1,0:T(8,128)(2,1)S(1)}, bf16[176,128]{1,0:T(8,128)(2,1)S(1)}, u32[]{:S(2)}, u32[]{:S(2)}) collective-permute-start(bf16[176,128]{1,0:T(8,128)(2,1)S(1)} %add_convert_fusion.refs_0_), channel_id=1, source_target_pairs={{0,16},{1,25},{2,18},{3,27},{4,20},{5,29},{6,22},{7,31},{8,24},{9,... | collective-permute-start | bytes 135176 | tf_op jit(solution)/shard_map/ppermute | solution.py:438
  40.2 4.6 %collective-permute-start.16 = (bf16[176,128]{1,0:T(8,128)(2,1)S(1)}, bf16[176,128]{1,0:T(8,128)(2,1)S(1)}, u32[]{:S(2)}, u32[]{:S(2)}) collective-permute-start(bf16[176,128]{1,0:T(8,128)(2,1)S(1)} %add_convert_fusion.refs_0_), channel_id=1, source_target_pairs={{0,8},{1,9},{2,10},{3,11},{4,12},{5,13},{6,14},{7,15},{8,0},{9,1},... | collective-permute-start | bytes 135176 | tf_op jit(solution)/shard_map/ppermute | solution.py:438
  42.4 2.4 %collective-permute-start.18 = (bf16[176,128]{1,0:T(8,128)(2,1)S(1)}, bf16[176,128]{1,0:T(8,128)(2,1)S(1)}, u32[]{:S(2)}, u32[]{:S(2)}) collective-permute-start(bf16[176,128]{1,0:T(8,128)(2,1)S(1)} %collective-permute-done.17.refs_2_), channel_id=1, source_target_pairs={{0,1},{1,0},{2,3},{3,2},{4,5},{5,4},{6,7},{7,6},{8,9},{9,8},{10,11... | collective-permute-start | bytes 135176 | tf_op jit(solution)/shard_map/ppermute | solution.py:438
